TPU v7x, 128 devices: a whole 4x4x4 slice. The times are simulated.
128 devices in a mesh: lang: 16 (over y_lo, z, core), shard: 8 (over y_hi, x).
Axes of the slice: x: 4, y: 4 (y_hi: 2, y_lo: 2; y = y_hi * 2 + y_lo), z: 4, core: 2. Of those that a mesh axis runs over, the one named last changes fastest.
Arguments:
- queries: bfloat16 [16384, 768], P(('lang', 'shard')), may hold values from -6 to 6
- routes: int32 [16384, 1], P(('lang', 'shard')), may hold values from 0 to 15; in each aligned block of 128 rows (0 to 127, 128 to 255, ...) at most 20 rows name the same one
- corpus: bfloat16 [131072, 768], P(('lang', 'shard')), may hold values from -0.21875 to 0.21875
Outputs:
- top_scores: float32 [16384, 128], P(('lang', 'shard'))
Inputs may be any that keep to these rules, and one draw needn't show every extreme that they name: `routes`: among the 128 queries of one device, each language is named at most 20 times; some language is named exactly 20 times.
All inputs are finite; a program needn't handle non-finite values.
Results may differ from a plain program's by a relative error of at most 0.0012.
Values may be sent and summed in bfloat16 or wider, within the bound.
No kernel may reach another device: no remote copies, remote signals or barrier semaphores. Data moves between devices by JAX's collectives and lax.ppermute only.
A program may use at most 64 MiB of HBM per device.

v0:
```python
import jax
import jax.numpy as jnp
from jax import lax
from jax.sharding import PartitionSpec as P

CAP = 20
TOPK = 128


epsilon = 1e-06


def in_order(parts, dim):
    parts = jnp.moveaxis(parts, 0, dim)
    lengths = parts.shape
    return parts.reshape(*lengths[:dim], lengths[dim] * lengths[dim + 1], *lengths[dim + 2 :])


def sent_to_all(x, axis):
    count = lax.axis_size(axis)
    return lax.all_to_all(jnp.broadcast_to(x[None], (count, *x.shape)), axis, 0, 0, tiled=True)


def gathered_copies(x, axis, dim):
    return in_order(sent_to_all(x, axis), dim)


def score_block(query_rows, corpus, keep_count):
    leaders = None
    scores = lax.dot_general(
        query_rows, corpus, (((1,), (1,)), ((), ())), preferred_element_type=jnp.float32
    )
    leaders = lax.top_k(scores, keep_count)[0]
    return leaders


def shards(queries, routes, corpus):
    lang_count = lax.axis_size("lang")
    feature_count = queries.shape[1]
    capacity = CAP
    keep_count = TOPK
    widened = queries.astype(jnp.float32)
    unit_query = (
        widened * lax.rsqrt(jnp.mean(widened * widened, axis=1, keepdims=True) + epsilon)
    ).astype(jnp.bfloat16)
    language = routes[:, 0]
    onehot = (language[:, None] == jnp.arange(lang_count, dtype=jnp.int32)[None, :]).astype(
        jnp.int32
    )
    slot_index = jnp.sum(jnp.cumsum(onehot, axis=0) * onehot, axis=1) - 1
    position = language * capacity + slot_index
    outbox = (
        jnp.zeros((lang_count * capacity, feature_count), jnp.bfloat16).at[position].set(unit_query)
    )
    arrived = lax.all_to_all(outbox, "lang", split_axis=0, concat_axis=0, tiled=True)
    candidates = score_block(gathered_copies(arrived, "shard", 0), corpus, keep_count)
    pooled = lax.all_to_all(candidates, "shard", split_axis=0, concat_axis=1, tiled=True)
    owned = lax.top_k(pooled, keep_count)[0]
    returned = lax.all_to_all(owned, "lang", split_axis=0, concat_axis=0, tiled=True)
    return returned[position]


def solution(mesh):
    placed = (P(("lang", "shard"), None), P(("lang", "shard"), None), P(("lang", "shard"), None))
    return jax.shard_map(
        shards, mesh=mesh, in_specs=placed, out_specs=P(("lang", "shard"), None), check_vma=False
    )
```

profile of v0, /device:TPU:1, one launch (start us, length us, event | category | flops | bytes accessed | tf_op | source)
XLA Modules:
  0.0 526.3 jit_solution(10240677926728779488)
XLA Ops:
  0.0 0.0 copy-start
  0.0 0.9 fusion.6
  0.9 0.2 reduce_window_sum.11
  1.0 0.8 select_reduce_fusion
  1.9 0.7 fusion.7
  2.5 1.0 fusion
  3.6 1.7 scatter_custom_fusion
  5.3 0.1 all_to_all.31
  5.5 18.8 %all_to_all.45 = bf16[16,20,768]{2,1,0:T(8,128)(2,1)S(1)} all-to-all(bf16[16,20,768]{2,1,0:T(8,128)(2,1)S(1)} %all_to_all.31), channel_id=1, replica_groups=mesh['lang'=16,'shard'=8] {'lang'}, dimensions={0} | all-to-all | bytes 983040 | tf_op jit(solution)/shard_map/all_to_all | solution.py:55
  24.3 0.1 broadcast_in_dim.7
  24.4 0.3 broadcast_in_dim.8
  24.7 53.5 %all_to_all.46 = bf16[8,320,768]{2,1,0:T(8,128)(2,1)S(1)} all-to-all(bf16[8,320,768]{2,1,0:T(8,128)(2,1)S(1)} %broadcast_in_dim.8), channel_id=1, replica_groups=mesh['lang'=16,'shard'=8] {'shard'}, dimensions={0} | all-to-all | bytes 7864320 | tf_op jit(solution)/shard_map/all_to_all | solution.py:21
  78.2 0.0 copy-done
  78.2 6.9 %fusion.8 = f32[2560,1024]{0,1:T(8,128)} fusion(bf16[2560,768]{1,0:T(8,128)(2,1)S(1)} %bitcast.18, bf16[1024,768]{1,0:T(8,128)(2,1)S(1)} %copy-done), kind=kOutput, calls=%fused_computation.18 | convolution fusion | flops 4026531840 | bytes 15990784
  85.0 4.5 iota.10.clone
  89.5 356.4 %top_k.14 = (f32[2560,1024]{0,1:T(8,128)}, s32[2560,1024]{0,1:T(8,128)}) sort(f32[2560,1024]{0,1:T(8,128)} %fusion.8, s32[2560,1024]{0,1:T(8,128)} %iota.10.clone), dimensions={1}, to_apply=%region_4.5 | sort | flops 57671680 | bytes 41943040 | tf_op jit(solution)/shard_map/top_k | solution.py:33
  445.9 11.4 %copy.7 = f32[2560,1024]{1,0:T(8,128)} copy(f32[2560,1024]{0,1:T(8,128)} %get-tuple-element.11) | data formatting | bytes 20971520 | tf_op jit(solution)/shard_map/top_k | solution.py:33
  457.3 0.0 slice-start
  457.3 1.3 slice-done
  458.7 21.3 %all_to_all.47 = f32[8,320,128]{2,1,0:T(8,128)S(1)} all-to-all(f32[8,320,128]{2,1,0:T(8,128)S(1)} %bitcast.17), channel_id=1, replica_groups=mesh['lang'=16,'shard'=8] {'shard'}, dimensions={0} | all-to-all | bytes 2621440 | tf_op jit(solution)/shard_map/all_to_all | solution.py:57
  480.0 0.0 copy-start.1
  480.0 0.2 copy_bitcast_fusion
  480.1 32.1 %sort_prefixfusion = f32[320,128]{1,0:T(8,128)S(1)} fusion(f32[320,1024]{1,0:T(8,128)S(1)} %copy_bitcast_fusion), kind=kCustom, calls=%top_k.20.sort_prefix | custom fusion | flops 6225920 | bytes 1474560 | tf_op jit(solution)/shard_map/top_k | solution.py:58
  512.2 0.7 all_to_all.38
  512.9 5.4 %all-to-all-start.3 = ((f32[16,20,128]{2,1,0:T(8,128)}), f32[16,20,128]{2,1,0:T(8,128)S(1)}, u32[]{:S(2)}, u32[]{:S(2)}) async-start(f32[16,20,128]{2,1,0:T(8,128)} %all_to_all.38), calls=%async_computation.3 | async-start | bytes 393216 | tf_op jit(solution)/shard_map/all_to_all | solution.py:59
  518.3 6.7 %all-to-all-done.3 = f32[16,20,128]{2,1,0:T(8,128)S(1)} async-done(((f32[16,20,128]{2,1,0:T(8,128)}), f32[16,20,128]{2,1,0:T(8,128)S(1)}, u32[]{:S(2)}, u32[]{:S(2)}) %all-to-all-start.3) | async-done | bytes 163872 | tf_op jit(solution)/shard_map/all_to_all | solution.py:59
  525.0 1.2 gather_fusion
  526.3 0.0 copy-done.1
  (3 shorter events, 0.0 us)
Async XLA Ops:
  0.0 78.2 %copy-start = (bf16[1024,768]{1,0:T(8,128)(2,1)S(1)}, bf16[1024,768]{1,0:T(8,128)(2,1)}, u32[]{:S(2)}) copy-start(bf16[1024,768]{1,0:T(8,128)(2,1)} %param.5) | copy-start | bytes 4718596
  457.3 1.3 slice-start
  480.0 46.3 %copy-start.1 = (bf16[1024,768]{1,0:T(8,128)(2,1)S(1)}, bf16[1024,768]{1,0:T(8,128)(2,1)}, u32[]{:S(2)}) copy-start(bf16[1024,768]{1,0:T(8,128)(2,1)} %param.5) | copy-start | bytes 4718596
  512.9 12.1 %all-to-all-start.3 = ((f32[16,20,128]{2,1,0:T(8,128)}), f32[16,20,128]{2,1,0:T(8,128)S(1)}, u32[]{:S(2)}, u32[]{:S(2)}) async-start(f32[16,20,128]{2,1,0:T(8,128)} %all_to_all.38), calls=%async_computation.3 | async-start | bytes 393216 | tf_op jit(solution)/shard_map/all_to_all | solution.py:59
where the time goes:
time: 529 us; the launch traced here: 526 us
  other arithmetic  394 us (74%)
  blocking collectives  93.6 us (18%)
  local copies, waits for them, and re-layouts  19.8 us (4%)
  matrix products  6.86 us (1%)
  waiting for transfers between devices  6.71 us (1%)
  starting transfers between devices  5.4 us (1%)
    top_k x1, other arithmetic, score_block(): leaders = lax.top_k(scores, keep_count)[0]  356 us
    all_to_all x1, blocking collectives, sent_to_all(): lax.all_to_all(jnp.broadcast_to(x[None], (count, *x.shape)), axis, 0, 0,...  53.5 us
    top_k x1, other arithmetic, shards(): owned = lax.top_k(pooled, keep_count)[0]  32.1 us
    all_to_all x1, blocking collectives, shards(): lax.all_to_all(candidates, 'shard', split_axis=0, concat_axis=1, tiled=True)  21.3 us
    all_to_all x1, blocking collectives, shards(): lax.all_to_all(outbox, 'lang', split_axis=0, concat_axis=0, tiled=True)  18.8 us
    top_k x3, local copies, waits for them, and re-layouts, score_block(): leaders = lax.top_k(scores, keep_count)[0]  12.7 us
  transfers between devices with their start and end apart: 1, of which 1 were waited for; matrix products, arithmetic and copies ran while one was open for 0% of the time, Pallas kernels for 0%

commit v1 on v0

v1 whole, which is shorter than its diff:
```python
import functools

import jax
import jax.numpy as jnp
from jax import lax
from jax.experimental import pallas as pl
from jax.experimental.pallas import tpu as pltpu
from jax.sharding import PartitionSpec as P

CAP = 20
TOPK = 128
SLOTS = 320
MAIN = 256
TAIL = SLOTS - MAIN

epsilon = 1e-06


def batcher(n):
    pairs = []
    p = 1
    while p < n:
        k = p
        while k >= 1:
            for j in range(k % p, n - k, 2 * k):
                for i in range(min(k, n - j - k)):
                    if (i + j) // (2 * p) == (i + j + k) // (2 * p):
                        pairs.append((i + j, i + j + k))
            k //= 2
        p *= 2
    return pairs


SORT32 = batcher(32)


def wire(ref, base, i):
    return ref[pl.ds(pl.multiple_of((base + i) * 8, 8), 8), :]


def put(ref, base, i, value):
    ref[pl.ds(pl.multiple_of((base + i) * 8, 8), 8), :] = value


def sort32(ref, base):
    v = [wire(ref, base, i) for i in range(32)]
    for i, j in SORT32:
        v[i], v[j] = jnp.maximum(v[i], v[j]), jnp.minimum(v[i], v[j])
    for i in range(32):
        put(ref, base, i, v[i])


def clean(v):
    n = len(v)
    step = n // 2
    while step:
        for i in range(n):
            if not i & step:
                v[i], v[i + step] = jnp.maximum(v[i], v[i + step]), jnp.minimum(v[i], v[i + step])
        step //= 2
    return v


def clean_at(ref, base):
    v = clean([wire(ref, base, i) for i in range(32)])
    for i in range(32):
        put(ref, base, i, v[i])


def merge64(src, base, dst):
    for op, at in ((jnp.maximum, 0), (jnp.minimum, 32)):
        v = clean([op(wire(src, base, i), wire(src, base, 63 - i)) for i in range(32)])
        for i in range(32):
            put(dst, base + at, i, v[i])


def merge128(src, base, dst):
    for op, at in ((jnp.maximum, 0), (jnp.minimum, 64)):
        v = []
        for i in range(32):
            a = op(wire(src, base, i), wire(src, base, 127 - i))
            b = op(wire(src, base, i + 32), wire(src, base, 95 - i))
            v.append(jnp.maximum(a, b))
            put(dst, base + at + 32, i, jnp.minimum(a, b))
        v = clean(v)
        for i in range(32):
            put(dst, base + at, i, v[i])
        clean_at(dst, base + at + 32)


def merge_top(a, a_base, b, b_base, dst, dst_base, turn=0):
    def other(i):
        value = wire(b, b_base, 127 - i)
        return pltpu.roll(value, turn, 0) if turn else value

    v = []
    for i in range(32):
        c = [jnp.maximum(wire(a, a_base, i + 32 * k), other(i + 32 * k)) for k in range(4)]
        f0, g0 = jnp.maximum(c[0], c[2]), jnp.minimum(c[0], c[2])
        f1, g1 = jnp.maximum(c[1], c[3]), jnp.minimum(c[1], c[3])
        v.append(jnp.maximum(f0, f1))
        put(dst, dst_base + 32, i, jnp.minimum(f0, f1))
        put(dst, dst_base + 64, i, jnp.maximum(g0, g1))
        put(dst, dst_base + 96, i, jnp.minimum(g0, g1))
    v = clean(v)
    for i in range(32):
        put(dst, dst_base, i, v[i])

    def rest(k, carry):
        clean_at(dst, dst_base + 32 + 32 * k)
        return carry

    lax.fori_loop(0, 3, rest, 0)


def loop(n, body):
    def step(i, carry):
        body(i)
        return carry

    lax.fori_loop(0, n, step, 0)


def leaders_kernel(q0, q1, q2, q3, own, far, main_ref, tail_ref, q_all, s, u, w):
    for k, q in enumerate((q0, q1, q2, q3)):
        q_all[k * MAIN : (k + 1) * MAIN, :] = q[0:MAIN, :]
        q_all[4 * MAIN + k * TAIL : 4 * MAIN + (k + 1) * TAIL, :] = q[MAIN:SLOTS, :]

    def scored(corpus, g, dst):
        rows = q_all[pl.ds(pl.multiple_of(g * MAIN, MAIN), MAIN), :]
        for quarter in range(4):
            part = lax.dot_general(
                corpus[quarter * 256 : (quarter + 1) * 256, :],
                rows,
                (((1,), (1,)), ((), ())),
                preferred_element_type=jnp.float32,
            )
            for half in range(2):
                s[pl.ds(quarter * 2 + half, 256, stride=8), :] = part[:, half * 128 : (half + 1) * 128]
        loop(8, lambda i: sort32(s, i * 32))
        loop(4, lambda i: merge64(s, i * 64, u))
        loop(2, lambda i: merge128(u, i * 128, s))
        merge_top(s, 0, s, 128, dst, 0)

    def group(g):
        scored(own, g, w)
        scored(far, g, u)
        merge_top(w, 0, u, 0, s, 0)
        merge_top(s, 0, s, 0, u, 0, turn=4)
        merge_top(u, 0, u, 0, s, 0, turn=2)

        @pl.when(g < 4)
        def _():
            for half in range(2):
                main_ref[g, half] = s[pl.ds(half, 128, stride=8), :]

        @pl.when(g == 4)
        def _():
            for half in range(2):
                tail_ref[half] = s[pl.ds(half, 128, stride=8), :]

    loop(5, group)


def leaders(chunks, own, far):
    return pl.pallas_call(
        leaders_kernel,
        out_shape=(
            jax.ShapeDtypeStruct((4, 2, TOPK, 128), jnp.float32),
            jax.ShapeDtypeStruct((2, TOPK, 128), jnp.float32),
        ),
        in_specs=[pl.BlockSpec(memory_space=pltpu.VMEM)] * 6,
        out_specs=[pl.BlockSpec(memory_space=pltpu.VMEM)] * 2,
        scratch_shapes=[
            pltpu.VMEM((4 * SLOTS, 768), jnp.bfloat16),
            pltpu.VMEM((256 * 8, 128), jnp.float32),
            pltpu.VMEM((256 * 8, 128), jnp.float32),
            pltpu.VMEM((128 * 8, 128), jnp.float32),
        ],
        compiler_params=pltpu.CompilerParams(vmem_limit_bytes=40 << 20),
        name="leaders",
    )(*chunks, own, far)


def join_kernel(m0, m1, m2, m3, t0, t1, t2, t3, out, a, b, c):
    for ref, at, main, tail, shift in (
        (a, 0, m0, t0, 0),
        (b, 0, m1, t1, 64),
        (a, 4, m2, t2, 0),
        (b, 4, m3, t3, 64),
    ):
        for half in range(2):
            ref[pl.ds(at + half, TOPK, stride=8), :] = main[half]
        last = tail[...]
        ref[pl.ds(at + 2, TOPK, stride=8), :] = pltpu.roll(last, 64, 1) if shift else last
        ref[pl.ds(at + 3, TOPK, stride=8), :] = last
    merge_top(a, 0, b, 0, c, 0)
    merge_top(c, 0, c, 0, a, 0, turn=4)
    for half in range(2):
        out[half * 128 : (half + 1) * 128, :] = a[pl.ds(half, TOPK, stride=8), :].T
    out[MAIN:SLOTS, :] = a[pl.ds(2, TOPK, stride=8), :].T[0:TAIL, :]


def join(mains, tails):
    return pl.pallas_call(
        join_kernel,
        out_shape=jax.ShapeDtypeStruct((SLOTS, TOPK), jnp.float32),
        in_specs=[pl.BlockSpec(memory_space=pltpu.VMEM)] * 8,
        out_specs=pl.BlockSpec(memory_space=pltpu.VMEM),
        scratch_shapes=[pltpu.VMEM((128 * 8, 128), jnp.float32)] * 3,
        name="join",
    )(*mains, *tails)


def x_ring(step):
    return [(y * 4 + x, y * 4 + (x + step) % 4) for y in range(2) for x in range(4)]


def across(value):
    return lax.ppermute(value, "shard", [(i, (i + 4) % 8) for i in range(8)])


def shards(queries, routes, corpus):
    lang_count = lax.axis_size("lang")
    feature_count = queries.shape[1]
    capacity = CAP
    far = across(corpus)
    widened = queries.astype(jnp.float32)
    unit_query = (
        widened * lax.rsqrt(jnp.mean(widened * widened, axis=1, keepdims=True) + epsilon)
    ).astype(jnp.bfloat16)
    language = routes[:, 0]
    onehot = (language[:, None] == jnp.arange(lang_count, dtype=jnp.int32)[None, :]).astype(jnp.int32)
    slot_index = jnp.sum(jnp.cumsum(onehot, axis=0) * onehot, axis=1) - 1
    position = language * capacity + slot_index
    outbox = jnp.zeros((lang_count * capacity, feature_count), jnp.bfloat16).at[position].set(unit_query)
    mine = lax.all_to_all(outbox, "lang", split_axis=0, concat_axis=0, tiled=True)
    chunks = (mine,) + tuple(lax.ppermute(mine, "shard", x_ring(s)) for s in (1, -1, 2))
    main, tail = leaders(chunks, corpus, far)
    mains, tails = [main[0]], [tail[0]]
    for k, s in ((1, -1), (2, 1), (3, 2)):
        back = lax.ppermute(
            jnp.concatenate([main[k], tail[k // 2][None]], axis=0), "shard", x_ring(s)
        )
        mains.append(back[:2])
        tails.append(back[2])
    owned = join(mains, tails)
    returned = lax.all_to_all(owned, "lang", split_axis=0, concat_axis=0, tiled=True)
    return returned[position]


def solution(mesh):
    placed = (P(("lang", "shard"), None), P(("lang", "shard"), None), P(("lang", "shard"), None))
    return jax.shard_map(
        shards, mesh=mesh, in_specs=placed, out_specs=P(("lang", "shard"), None), check_vma=False
    )
```

time: 529 us -> 129 us (0.24)
  other arithmetic: 394 us -> 5.25 us
  blocking collectives: 93.6 us -> 39.7 us
  waiting for transfers between devices: 6.71 us -> 35.1 us
  Pallas kernels: 0 us -> 24.9 us
  local copies, waits for them, and re-layouts: 19.8 us -> 8.21 us
  starting transfers between devices: 5.4 us -> 15.9 us
  matrix products: 6.86 us -> 0 us
    top_k x2 -> x0, other arithmetic: 388 us -> none  [the longest x1 356 us: score_block(): leaders = lax.top_k(scores, keep_count)[0]]
    all_to_all x2 -> x0, blocking collectives: 74.8 us -> none  [the longest x1 53.5 us: sent_to_all(): lax.all_to_all(jnp.broadcast_to(x[None], (count, *x.shape)), axis, 0, 0,...]
    ppermute x0 -> x7, waiting for transfers between devices: none -> 28.4 us  [the longest x3 20.6 us: shards(): lax.ppermute(mine, 'shard', x_ring(s))]
    pallas_call x0 -> x2, Pallas kernels: none -> 24.9 us  [the longest x1 22.4 us: leaders(): pl.pallas_call(leaders_kernel, out_shape=(jax.ShapeDtypeStruct((4, 2, TOP...]
    all_to_all x1, blocking collectives: 18.8 us -> 39.7 us  [shards(): lax.all_to_all(outbox, 'lang', split_axis=0, concat_axis=0, tiled=True)]
    top_k x3 -> x0, local copies, waits for them, and re-layouts: 12.7 us -> none  [score_block(): leaders = lax.top_k(scores, keep_count)[0]]
    ppermute x0 -> x7, starting transfers between devices: none -> 11.4 us  [the longest x3 4.28 us: shards(): lax.ppermute(mine, 'shard', x_ring(s))]
    unnamed x1 -> x0, matrix products: 6.86 us -> none
  transfers between devices with their start and end apart: 1 -> 8, of which waited for: 1 -> 5; matrix products, arithmetic and copies ran while one was open for 0% -> 6% of each run, Pallas kernels for 0% -> 0%
where the time goes in v1:
time: 129 us
  blocking collectives  39.7 us (31%)
  waiting for transfers between devices  35.1 us (27%)
  Pallas kernels  24.9 us (19%)
  starting transfers between devices  15.9 us (12%)
  local copies, waits for them, and re-layouts  8.21 us (6%)
  other arithmetic  5.25 us (4%)
    all_to_all x1, blocking collectives, shards(): lax.all_to_all(outbox, 'lang', split_axis=0, concat_axis=0, tiled=True)  39.7 us
    pallas_call x1, Pallas kernels, leaders(): pl.pallas_call(leaders_kernel, out_shape=(jax.ShapeDtypeStruct((4, 2, TOP...  22.4 us
    ppermute x3, waiting for transfers between devices, shards(): lax.ppermute(mine, 'shard', x_ring(s))  20.6 us
    ppermute x3, waiting for transfers between devices, shards(): lax.ppermute(jnp.concatenate([main[k], tail[k // 2][None]], axis=0), 'sha...  7.86 us
    all_to_all x1, waiting for transfers between devices, shards(): lax.all_to_all(owned, 'lang', split_axis=0, concat_axis=0, tiled=True)  6.64 us
    all_to_all x1, starting transfers between devices, shards(): lax.all_to_all(owned, 'lang', split_axis=0, concat_axis=0, tiled=True)  4.59 us
    ppermute x3, starting transfers between devices, shards(): lax.ppermute(mine, 'shard', x_ring(s))  4.28 us
    ppermute x1, starting transfers between devices, across(): return lax.ppermute(value, 'shard', [(i, (i + 4) % 8) for i in range(8)])  3.73 us
  transfers between devices with their start and end apart: 8, of which 5 were waited for; matrix products, arithmetic and copies ran while one was open for 6% of the time, Pallas kernels for 0%

profile of v1, /device:TPU:1, one launch (start us, length us, event | category | flops | bytes accessed | tf_op | source)
XLA Modules:
  0.0 129.1 jit_solution(9559071753516893118)
XLA Ops:
  0.0 3.7 %collective-permute-start.3 = (bf16[1024,768]{1,0:T(8,128)(2,1)}, bf16[1024,768]{1,0:T(8,128)(2,1)}, u32[]{:S(2)}, u32[]{:S(2)}) collective-permute-start(bf16[1024,768]{1,0:T(8,128)(2,1)} %own.1), channel_id=1, source_target_pairs={{0,4},{1,5},{2,6},{3,7},{4,0},{5,1},{6,2},{7,3},{8,12},{9,13},{10,... | collective-permute-start | bytes 4718600 | tf_op jit(solution)/shard_map/ppermute | solution.py:220
  3.7 0.7 fusion.6
  4.5 0.2 reduce_window_sum.11
  4.6 0.8 select_reduce_fusion
  5.5 1.1 fusion
  6.5 0.7 fusion.7
  7.2 1.7 %scatter_custom_fusion = bf16[320,768]{1,0:T(8,128)(2,1)S(1)} fusion(s32[128]{0:T(128)S(1)} %fusion.7, bf16[]{:T(256)} %constant.8.clone.1, bf16[128,768]{1,0:T(8,128)(2,1)} %param.3, f32[128]{0:T(128)S(1)} %add_rsqrt_fusion), kind=kCustom, calls=%fused_computation.8 | custom fusion | flops 294912 | bytes 688642 | tf_op jit(solution)/shard_map/scatter | solution.py:236
  9.0 0.0 copy-start
  9.0 0.1 all_to_all.15
  9.1 39.7 %all_to_all.23 = bf16[16,20,768]{2,1,0:T(8,128)(2,1)S(1)} all-to-all(bf16[16,20,768]{2,1,0:T(8,128)(2,1)S(1)} %all_to_all.15), channel_id=1, replica_groups=mesh['lang'=16,'shard'=8] {'lang'}, dimensions={0} | all-to-all | bytes 983040 | tf_op jit(solution)/shard_map/all_to_all | solution.py:237
  48.7 0.1 all_to_all.17.q0
  48.8 1.3 collective-permute-start
  50.1 1.5 %collective-permute-start.1 = (bf16[320,768]{1,0:T(8,128)(2,1)S(1)}, bf16[320,768]{1,0:T(8,128)(2,1)S(1)}, u32[]{:S(2)}, u32[]{:S(2)}) collective-permute-start(bf16[320,768]{1,0:T(8,128)(2,1)S(1)} %all_to_all.17.q0), channel_id=1, source_target_pairs={{0,3},{1,0},{2,1},{3,2},{4,7},{5,4},{6,5},{7,6},{8,11},{9,8},{10,9... | collective-permute-start | bytes 1474568 | tf_op jit(solution)/shard_map/ppermute | solution.py:238
  51.6 1.5 %collective-permute-start.2 = (bf16[320,768]{1,0:T(8,128)(2,1)S(1)}, bf16[320,768]{1,0:T(8,128)(2,1)S(1)}, u32[]{:S(2)}, u32[]{:S(2)}) collective-permute-start(bf16[320,768]{1,0:T(8,128)(2,1)S(1)} %all_to_all.17.q0), channel_id=1, source_target_pairs={{0,2},{1,3},{2,0},{3,1},{4,6},{5,7},{6,4},{7,5},{8,10},{9,11},{10,... | collective-permute-start | bytes 1474568 | tf_op jit(solution)/shard_map/ppermute | solution.py:238
  53.1 9.0 %collective-permute-done.q1 = bf16[320,768]{1,0:T(8,128)(2,1)S(1)} collective-permute-done((bf16[320,768]{1,0:T(8,128)(2,1)S(1)}, bf16[320,768]{1,0:T(8,128)(2,1)S(1)}, u32[]{:S(2)}, u32[]{:S(2)}) %collective-permute-start) | collective-permute-done | bytes 491552 | tf_op jit(solution)/shard_map/ppermute | solution.py:238
  62.2 0.0 collective-permute-done.1.q2
  62.2 11.5 %collective-permute-done.2.q3 = bf16[320,768]{1,0:T(8,128)(2,1)S(1)} collective-permute-done((bf16[320,768]{1,0:T(8,128)(2,1)S(1)}, bf16[320,768]{1,0:T(8,128)(2,1)S(1)}, u32[]{:S(2)}, u32[]{:S(2)}) %collective-permute-start.2) | collective-permute-done | bytes 491552 | tf_op jit(solution)/shard_map/ppermute | solution.py:238
  73.7 0.0 collective-permute-done.3.far
  73.7 0.0 copy-done
  73.7 22.4 %leaders.1 = (f32[4,2,128,128]{3,2,1,0:T(8,128)S(1)}, f32[2,128,128]{2,1,0:T(8,128)S(1)}) custom-call(bf16[320,768]{1,0:T(8,128)(2,1)S(1)} %all_to_all.17.q0, bf16[320,768]{1,0:T(8,128)(2,1)S(1)} %collective-permute-done.q1, bf16[320,768]{1,0:T(8,128)(2,1)S(1)} %collective-permute-done.1.q2, bf16[320,768]{1,0:T(8,128)(2,1)S(1)} %collective-permute-done.2.q3, ...), custom_call_target="tpu_custom_call" | custom-call | tf_op jit(solution)/shard_map/leaders/pallas_call | solution.py:166
  96.1 0.7 slice_bitcast_fusion
  96.8 0.6 slice_bitcast_fusion.7
  97.5 0.6 collective-permute-start.6
  98.0 1.2 collective-permute-start.5
  99.3 1.5 %collective-permute-start.4 = (f32[3,128,128]{2,1,0:T(8,128)S(1)}, f32[3,128,128]{2,1,0:T(8,128)S(1)}, u32[]{:S(2)}, u32[]{:S(2)}) collective-permute-start(f32[3,128,128]{2,1,0:T(8,128)S(1)} %pad_maximum_fusion.2), channel_id=1, source_target_pairs={{0,3},{1,0},{2,1},{3,2},{4,7},{5,4},{6,5},{7,6},{8,11},{9,8},{10,9... | collective-permute-start | bytes 589832 | tf_op jit(solution)/shard_map/ppermute | solution.py:242
  100.8 3.2 %collective-permute-done.6 = f32[3,128,128]{2,1,0:T(8,128)S(1)} collective-permute-done((f32[3,128,128]{2,1,0:T(8,128)S(1)}, f32[3,128,128]{2,1,0:T(8,128)S(1)}, u32[]{:S(2)}, u32[]{:S(2)}) %collective-permute-start.6) | collective-permute-done | bytes 196640 | tf_op jit(solution)/shard_map/ppermute | solution.py:242
  104.0 0.7 slice.54.m3
  104.6 0.6 slice_bitcast_fusion.4.t3
  105.3 4.7 %collective-permute-done.5 = f32[3,128,128]{2,1,0:T(8,128)S(1)} collective-permute-done((f32[3,128,128]{2,1,0:T(8,128)S(1)}, f32[3,128,128]{2,1,0:T(8,128)S(1)}, u32[]{:S(2)}, u32[]{:S(2)}) %collective-permute-start.5) | collective-permute-done | bytes 196640 | tf_op jit(solution)/shard_map/ppermute | solution.py:242
  109.9 0.7 slice.53.m2
  110.6 0.6 slice_bitcast_fusion.5.t2
  111.2 0.0 collective-permute-done.4
  111.2 0.6 slice.52.m1
  111.9 0.6 slice_bitcast_fusion.6.t1
  112.5 2.5 %join.1 = f32[320,128]{1,0:T(8,128)} custom-call(f32[2,128,128]{2,1,0:T(8,128)} %get-tuple-element.12.m0, f32[2,128,128]{2,1,0:T(8,128)} %slice.52.m1, f32[2,128,128]{2,1,0:T(8,128)} %slice.53.m2, f32[2,128,128]{2,1,0:T(8,128)} %slice.54.m3, f32[128,128]{1,0:T(8,128)} %get-tuple-element.13.t0, f32[128,128]{1,0:T(8,128)} %slice_bitcast_fusion.6.t1, ...), custom_call_target="tpu_custom_call" | custom-call | tf_op jit(solution)/shard_map/join/pallas_call | solution.py:205
  115.0 1.6 %all_to_all.18 = f32[16,20,128]{2,1,0:T(8,128)} reshape(f32[320,128]{1,0:T(8,128)} %join.1) | data formatting | bytes 327680 | tf_op jit(solution)/shard_map/all_to_all | solution.py:248
  116.6 4.6 %all-to-all-start.1 = ((f32[16,20,128]{2,1,0:T(8,128)}), f32[16,20,128]{2,1,0:T(8,128)S(1)}, u32[]{:S(2)}, u32[]{:S(2)}) async-start(f32[16,20,128]{2,1,0:T(8,128)} %all_to_all.18), calls=%async_computation.1 | async-start | bytes 393216 | tf_op jit(solution)/shard_map/all_to_all | solution.py:248
  121.2 6.6 %all-to-all-done.1 = f32[16,20,128]{2,1,0:T(8,128)S(1)} async-done(((f32[16,20,128]{2,1,0:T(8,128)}), f32[16,20,128]{2,1,0:T(8,128)S(1)}, u32[]{:S(2)}, u32[]{:S(2)}) %all-to-all-start.1) | async-done | bytes 163872 | tf_op jit(solution)/shard_map/all_to_all | solution.py:248
  127.9 1.2 gather_fusion
  (5 shorter events, 0.1 us)
Async XLA Ops:
  0.0 73.7 %collective-permute-start.3 = (bf16[1024,768]{1,0:T(8,128)(2,1)}, bf16[1024,768]{1,0:T(8,128)(2,1)}, u32[]{:S(2)}, u32[]{:S(2)}) collective-permute-start(bf16[1024,768]{1,0:T(8,128)(2,1)} %own.1), channel_id=1, source_target_pairs={{0,4},{1,5},{2,6},{3,7},{4,0},{5,1},{6,2},{7,3},{8,12},{9,13},{10,... | collective-permute-start | bytes 4718600 | tf_op jit(solution)/shard_map/ppermute | solution.py:220
  9.0 64.7 %copy-start = (bf16[1024,768]{1,0:T(8,128)(2,1)S(1)}, bf16[1024,768]{1,0:T(8,128)(2,1)}, u32[]{:S(2)}) copy-start(bf16[1024,768]{1,0:T(8,128)(2,1)} %own.1) | copy-start | bytes 4718596
  48.8 13.3 %collective-permute-start = (bf16[320,768]{1,0:T(8,128)(2,1)S(1)}, bf16[320,768]{1,0:T(8,128)(2,1)S(1)}, u32[]{:S(2)}, u32[]{:S(2)}) collective-permute-start(bf16[320,768]{1,0:T(8,128)(2,1)S(1)} %all_to_all.17.q0), channel_id=1, source_target_pairs={{0,1},{1,2},{2,3},{3,0},{4,5},{5,6},{6,7},{7,4},{8,9},{9,10},{10,1... | collective-permute-start | bytes 1474568 | tf_op jit(solution)/shard_map/ppermute | solution.py:238
  50.1 12.0 %collective-permute-start.1 = (bf16[320,768]{1,0:T(8,128)(2,1)S(1)}, bf16[320,768]{1,0:T(8,128)(2,1)S(1)}, u32[]{:S(2)}, u32[]{:S(2)}) collective-permute-start(bf16[320,768]{1,0:T(8,128)(2,1)S(1)} %all_to_all.17.q0), channel_id=1, source_target_pairs={{0,3},{1,0},{2,1},{3,2},{4,7},{5,4},{6,5},{7,6},{8,11},{9,8},{10,9... | collective-permute-start | bytes 1474568 | tf_op jit(solution)/shard_map/ppermute | solution.py:238
  51.6 22.1 %collective-permute-start.2 = (bf16[320,768]{1,0:T(8,128)(2,1)S(1)}, bf16[320,768]{1,0:T(8,128)(2,1)S(1)}, u32[]{:S(2)}, u32[]{:S(2)}) collective-permute-start(bf16[320,768]{1,0:T(8,128)(2,1)S(1)} %all_to_all.17.q0), channel_id=1, source_target_pairs={{0,2},{1,3},{2,0},{3,1},{4,6},{5,7},{6,4},{7,5},{8,10},{9,11},{10,... | collective-permute-start | bytes 1474568 | tf_op jit(solution)/shard_map/ppermute | solution.py:238
  97.5 6.5 %collective-permute-start.6 = (f32[3,128,128]{2,1,0:T(8,128)S(1)}, f32[3,128,128]{2,1,0:T(8,128)S(1)}, u32[]{:S(2)}, u32[]{:S(2)}) collective-permute-start(f32[3,128,128]{2,1,0:T(8,128)S(1)} %get-tuple-element.16), channel_id=1, source_target_pairs={{0,2},{1,3},{2,0},{3,1},{4,6},{5,7},{6,4},{7,5},{8,10},{9,11},{10,... | collective-permute-start | bytes 589832 | tf_op jit(solution)/shard_map/ppermute | solution.py:242
  98.0 11.9 %collective-permute-start.5 = (f32[3,128,128]{2,1,0:T(8,128)S(1)}, f32[3,128,128]{2,1,0:T(8,128)S(1)}, u32[]{:S(2)}, u32[]{:S(2)}) collective-permute-start(f32[3,128,128]{2,1,0:T(8,128)S(1)} %get-tuple-element.17), channel_id=1, source_target_pairs={{0,1},{1,2},{2,3},{3,0},{4,5},{5,6},{6,7},{7,4},{8,9},{9,10},{10,1... | collective-permute-start | bytes 589832 | tf_op jit(solution)/shard_map/ppermute | solution.py:242
  99.3 11.9 %collective-permute-start.4 = (f32[3,128,128]{2,1,0:T(8,128)S(1)}, f32[3,128,128]{2,1,0:T(8,128)S(1)}, u32[]{:S(2)}, u32[]{:S(2)}) collective-permute-start(f32[3,128,128]{2,1,0:T(8,128)S(1)} %pad_maximum_fusion.2), channel_id=1, source_target_pairs={{0,3},{1,0},{2,1},{3,2},{4,7},{5,4},{6,5},{7,6},{8,11},{9,8},{10,9... | collective-permute-start | bytes 589832 | tf_op jit(solution)/shard_map/ppermute | solution.py:242
  116.6 11.2 %all-to-all-start.1 = ((f32[16,20,128]{2,1,0:T(8,128)}), f32[16,20,128]{2,1,0:T(8,128)S(1)}, u32[]{:S(2)}, u32[]{:S(2)}) async-start(f32[16,20,128]{2,1,0:T(8,128)} %all_to_all.18), calls=%async_computation.1 | async-start | bytes 393216 | tf_op jit(solution)/shard_map/all_to_all | solution.py:248

commit v2 on v1

v2 whole, which is shorter than its diff:
```python
import functools

import jax
import jax.numpy as jnp
from jax import lax
from jax.experimental import pallas as pl
from jax.experimental.pallas import tpu as pltpu
from jax.sharding import PartitionSpec as P

TOPK = 128
LANGS = 16
CAP = 20
ROWS = 24
MAIN = 16
TAIL = CAP - MAIN
Q = 128
WIDTH = 768

epsilon = 1e-06


def batcher(n):
    pairs = []
    p = 1
    while p < n:
        k = p
        while k >= 1:
            for j in range(k % p, n - k, 2 * k):
                for i in range(min(k, n - j - k)):
                    if (i + j) // (2 * p) == (i + j + k) // (2 * p):
                        pairs.append((i + j, i + j + k))
            k //= 2
        p *= 2
    return pairs


SORT32 = batcher(32)


def wire(ref, base, i):
    return ref[pl.ds(pl.multiple_of((base + i) * 8, 8), 8), :]


def put(ref, base, i, value):
    ref[pl.ds(pl.multiple_of((base + i) * 8, 8), 8), :] = value


def sort32(ref, base):
    v = [wire(ref, base, i) for i in range(32)]
    for i, j in SORT32:
        v[i], v[j] = jnp.maximum(v[i], v[j]), jnp.minimum(v[i], v[j])
    for i in range(32):
        put(ref, base, i, v[i])


def clean(v):
    n = len(v)
    step = n // 2
    while step:
        for i in range(n):
            if not i & step:
                v[i], v[i + step] = jnp.maximum(v[i], v[i + step]), jnp.minimum(v[i], v[i + step])
        step //= 2
    return v


def clean_at(ref, base):
    v = clean([wire(ref, base, i) for i in range(32)])
    for i in range(32):
        put(ref, base, i, v[i])


def merge64(src, base, dst):
    for op, at in ((jnp.maximum, 0), (jnp.minimum, 32)):
        v = clean([op(wire(src, base, i), wire(src, base, 63 - i)) for i in range(32)])
        for i in range(32):
            put(dst, base + at, i, v[i])


def merge128(src, base, dst):
    for op, at in ((jnp.maximum, 0), (jnp.minimum, 64)):
        v = []
        for i in range(32):
            a = op(wire(src, base, i), wire(src, base, 127 - i))
            b = op(wire(src, base, i + 32), wire(src, base, 95 - i))
            v.append(jnp.maximum(a, b))
            put(dst, base + at + 32, i, jnp.minimum(a, b))
        v = clean(v)
        for i in range(32):
            put(dst, base + at, i, v[i])
        clean_at(dst, base + at + 32)


def merge_top(a, a_base, b, b_base, dst, dst_base, turn=0):
    def other(i):
        value = wire(b, b_base, 127 - i)
        return pltpu.roll(value, turn, 0) if turn else value

    v = []
    for i in range(32):
        c = [jnp.maximum(wire(a, a_base, i + 32 * k), other(i + 32 * k)) for k in range(4)]
        f0, g0 = jnp.maximum(c[0], c[2]), jnp.minimum(c[0], c[2])
        f1, g1 = jnp.maximum(c[1], c[3]), jnp.minimum(c[1], c[3])
        v.append(jnp.maximum(f0, f1))
        put(dst, dst_base + 32, i, jnp.minimum(f0, f1))
        put(dst, dst_base + 64, i, jnp.maximum(g0, g1))
        put(dst, dst_base + 96, i, jnp.minimum(g0, g1))
    v = clean(v)
    for i in range(32):
        put(dst, dst_base, i, v[i])

    def rest(k, carry):
        clean_at(dst, dst_base + 32 + 32 * k)
        return carry

    lax.fori_loop(0, 3, rest, 0)


def loop(n, body):
    def step(i, carry):
        body(i)
        return carry

    lax.fori_loop(0, n, step, 0)


def score(corpus, rows, s):
    for quarter in range(4):
        part = lax.dot_general(
            corpus[quarter * 256 : (quarter + 1) * 256, :],
            rows,
            (((1,), (1,)), ((), ())),
            preferred_element_type=jnp.float32,
        )
        for half in range(2):
            s[pl.ds(quarter * 2 + half, 256, stride=8), :] = part[:, half * 128 : (half + 1) * 128]


def order(s, u, dst):
    loop(8, lambda i: sort32(s, i * 32))
    loop(4, lambda i: merge64(s, i * 64, u))
    loop(2, lambda i: merge128(u, i * 128, s))
    merge_top(s, 0, s, 128, dst, 0)


def leaders(rows_of, groups, own, far, s, u, w, emit):
    def group(g):
        rows = rows_of(g)
        score(own, rows, s)
        order(s, u, w)
        score(far, rows, s)
        order(s, u, u)
        merge_top(w, 0, u, 0, s, 0)
        merge_top(s, 0, s, 0, u, 0, turn=4)
        merge_top(u, 0, u, 0, s, 0, turn=2)
        for half in range(2):
            emit(g, half, s[pl.ds(half, TOPK, stride=8), :].T)

    loop(groups, group)


def main_rows(chunk):
    return chunk[:, 0:MAIN, :].reshape(-1, WIDTH)


def early_kernel(count, *refs):
    chunks, (own, far, out, rows, s, u, w) = refs[:count], refs[count:]
    for k, chunk in enumerate(chunks):
        rows[k * 256 : (k + 1) * 256, :] = main_rows(chunk)

    def emit(g, half, value):
        out[g, half * Q : (half + 1) * Q, :] = value

    leaders(
        lambda g: rows[pl.ds(pl.multiple_of(g * 256, 256), 256), :], count, own, far, s, u, w, emit
    )


def late_kernel(at, mine, cx, cy, cd0, cd1, own, far, first, second, out, rows, tails, s, u, w):
    rows[0:128, :] = main_rows(cd0)
    rows[128:256, :] = main_rows(cd1)
    slot = lax.broadcasted_iota(jnp.int32, (64, LANGS * ROWS), 1)
    row = lax.broadcasted_iota(jnp.int32, (64, LANGS * ROWS), 0)
    picks = (slot == row // TAIL * ROWS + MAIN + row % TAIL).astype(jnp.float32).astype(jnp.bfloat16)
    half_picks = picks[0:32, 0 : 8 * ROWS]

    def tail_of(chunk, sel):
        flat = chunk[...].reshape(-1, WIDTH)
        return jnp.dot(sel, flat, preferred_element_type=jnp.float32).astype(jnp.bfloat16)

    for k, chunk in enumerate((mine, cx, cy)):
        rows[256 + k * 64 : 256 + (k + 1) * 64, :] = tail_of(chunk, picks)
    rows[448:480, :] = tail_of(cd0, half_picks)
    rows[480:512, :] = tail_of(cd1, half_picks)

    me = at[0]
    owner = (me, me ^ 1, me ^ 2, me ^ 3)

    def emit(g, half, value):
        tails[g, half] = value

    leaders(
        lambda g: rows[pl.ds(pl.multiple_of(g * 256, 256), 256), :], 2, own, far, s, u, w, emit
    )
    none = jnp.zeros((ROWS - CAP, TOPK), jnp.float32)
    for k in range(4):
        for lang in range(LANGS):
            if k == 3:
                main = tails[0, lang // 8, lang % 8 * MAIN : (lang % 8 + 1) * MAIN, :]
            else:
                main = (first.at[0] if k == 0 else second.at[k - 1])[lang * MAIN : (lang + 1) * MAIN, :]
            out[lang, owner[k], 0:MAIN, :] = main
            start = k % 2 * 64 + lang * TAIL
            out[lang, owner[k], MAIN:CAP, :] = tails[1, k // 2, start : start + TAIL, :]
            out[lang, owner[k], CAP:ROWS, :] = none


COST = 2 * 256 * 2048 * 768 * 8
VMEM = pl.BlockSpec(memory_space=pltpu.VMEM)
LIMIT = pltpu.CompilerParams(vmem_limit_bytes=40 << 20)


def work(groups):
    return [
        pltpu.VMEM((256 * 8, 128), jnp.float32),
        pltpu.VMEM((256 * 8, 128), jnp.float32),
        pltpu.VMEM((128 * 8, 128), jnp.float32),
    ]


def early(chunks, own, far):
    count = len(chunks)
    return pl.pallas_call(
        functools.partial(early_kernel, count),
        out_shape=jax.ShapeDtypeStruct((count, 256, TOPK), jnp.float32),
        in_specs=[VMEM] * (count + 2),
        out_specs=VMEM,
        scratch_shapes=[pltpu.VMEM((256 * count, WIDTH), jnp.bfloat16)] + work(count),
        compiler_params=LIMIT,
        cost_estimate=pl.CostEstimate(flops=COST * count, bytes_accessed=1 << 20, transcendentals=0),
        name="early",
    )(*chunks, own, far)


def late(at, mine, cx, cy, cd0, cd1, own, far, first, second):
    return pl.pallas_call(
        late_kernel,
        out_shape=jax.ShapeDtypeStruct((LANGS, 4, ROWS, TOPK), jnp.float32),
        in_specs=[pl.BlockSpec(memory_space=pltpu.SMEM)] + [VMEM] * 9,
        out_specs=VMEM,
        scratch_shapes=[
            pltpu.VMEM((512, WIDTH), jnp.bfloat16),
            pltpu.VMEM((2, 2, Q, TOPK), jnp.float32),
        ]
        + work(2),
        compiler_params=LIMIT,
        cost_estimate=pl.CostEstimate(flops=COST * 2, bytes_accessed=1 << 20, transcendentals=0),
        name="late",
    )(at, mine, cx, cy, cd0, cd1, own, far, first, second)


def outbox_kernel(queries, routes, out, slots):
    x = queries[...].astype(jnp.float32)
    unit = (x * lax.rsqrt(jnp.mean(x * x, axis=1, keepdims=True) + epsilon)).astype(jnp.bfloat16)
    along = jnp.broadcast_to(routes[...].astype(jnp.float32), (Q, Q))
    down = along.T
    before = lax.broadcasted_iota(jnp.int32, (Q, Q), 0) < lax.broadcasted_iota(jnp.int32, (Q, Q), 1)
    earlier = jnp.where(before & (along == down), 1.0, 0.0)
    rank = jnp.sum(earlier, axis=0, keepdims=True)
    place = routes[...] * ROWS + rank.astype(jnp.int32)
    slots[...] = place
    total = LANGS * ROWS
    hits = lax.broadcasted_iota(jnp.int32, (total, Q), 0) == jnp.broadcast_to(place, (total, Q))
    picks = jnp.where(hits, 1.0, 0.0).astype(jnp.bfloat16)
    box = jnp.dot(picks, unit, preferred_element_type=jnp.float32).astype(jnp.bfloat16)
    out[...] = box.reshape(LANGS, ROWS, WIDTH)


def outbox_of(queries, routes):
    return pl.pallas_call(
        outbox_kernel,
        out_shape=(
            jax.ShapeDtypeStruct((LANGS, ROWS, WIDTH), jnp.bfloat16),
            jax.ShapeDtypeStruct((1, Q), jnp.int32),
        ),
        in_specs=[VMEM] * 2,
        out_specs=(VMEM, VMEM),
        compiler_params=LIMIT,
        name="outbox",
    )(queries, routes)


def join_kernel(back, slots, out, a, b):
    total = LANGS * ROWS
    hits = lax.broadcasted_iota(jnp.int32, (total, Q), 0) == jnp.broadcast_to(slots[...], (total, Q))
    picks = jnp.where(hits, 1.0, 0.0)
    picks = jnp.concatenate([picks[i * Q : (i + 1) * Q, :].T for i in range(total // Q)], axis=1)
    picks = picks.astype(jnp.bfloat16)
    for k in range(4):
        left = back[:, k].reshape(total, TOPK)
        rows = jnp.zeros((Q, TOPK), jnp.float32)
        for _ in range(3):
            part = left.astype(jnp.bfloat16)
            left = left - part.astype(jnp.float32)
            rows = rows + jnp.dot(picks, part, preferred_element_type=jnp.float32)
        ranks = rows.T
        a[pl.ds(k, TOPK, stride=8), :] = ranks
        a[pl.ds(k + 4, TOPK, stride=8), :] = ranks
    merge_top(a, 0, a, 0, b, 0, turn=2)
    merge_top(b, 0, b, 0, a, 0, turn=1)
    out[...] = a[pl.ds(0, TOPK, stride=8), :].T


def join(back, slots):
    return pl.pallas_call(
        join_kernel,
        out_shape=jax.ShapeDtypeStruct((Q, TOPK), jnp.float32),
        in_specs=[VMEM] * 2,
        out_specs=VMEM,
        scratch_shapes=[pltpu.VMEM((128 * 8, 128), jnp.float32)] * 2,
        compiler_params=LIMIT,
        name="join",
    )(back, slots)


AXES = ("lang", "shard")


def moves(target):
    return [
        (lang * 8 + y * 4 + x, lang * 8 + ty * 4 + tx % 4)
        for lang in range(16)
        for y in range(2)
        for x in range(4)
        for ty, tx in (target(lang % 2, y, x),)
    ]


def pair(core, y, x):
    return y, x + (1 if (x + core) % 2 == 0 else -1)


def over_x(core, y, x):
    return y, x + 2


def over_y(core, y, x):
    return 1 - y, x


TEAMS = [
    [lang * 8 + y * 4 + odd + 2 * half for lang in range(16) for y in range(2) for half in range(2)]
    for odd in range(2)
]


def shards(queries, routes, corpus):
    far = lax.ppermute(corpus, AXES, moves(pair))
    outbox, slots = outbox_of(queries, routes.reshape(1, Q))
    mine = lax.all_to_all(outbox, "lang", split_axis=0, concat_axis=0, tiled=True)
    cx = lax.ppermute(mine, AXES, moves(over_x))
    cy = lax.ppermute(mine, AXES, moves(over_y))
    cd0 = lax.ppermute(cx[:8], AXES, moves(over_y))
    cd1 = lax.ppermute(cy[8:], AXES, moves(over_x))
    first = early((mine,), corpus, far)
    second = early((cx, cy), corpus, far)
    shard = lax.axis_index("shard")
    at = (shard // 4 * 2 + shard % 4 // 2).astype(jnp.int32).reshape(1)
    found = late(at, mine, cx, cy, cd0, cd1, corpus, far, first, second)
    back = lax.all_to_all(
        found.reshape(LANGS * 4, ROWS, TOPK), AXES, 0, 0, axis_index_groups=TEAMS, tiled=True
    )
    return join(back.reshape(LANGS, 4, ROWS, TOPK), slots)


def solution(mesh):
    placed = (P(AXES, None), P(AXES, None), P(AXES, None))
    return jax.shard_map(shards, mesh=mesh, in_specs=placed, out_specs=P(AXES, None), check_vma=False)
```

time: 129 us -> 94.5 us (0.73)
  waiting for transfers between devices: 35.1 us -> 11.5 us
  local copies, waits for them, and re-layouts: 8.21 us -> 1.62 us
  other arithmetic: 5.25 us -> 0 us
  Pallas kernels: 24.9 us -> 28.4 us
  starting transfers between devices: 15.9 us -> 12.5 us
    all_to_all x0 -> x1, blocking collectives: none -> 22.6 us  [shards(): lax.all_to_all(found.reshape(LANGS * 4, ROWS, TOPK), AXES, 0, 0, axis_ind...]
    all_to_all x1, blocking collectives: 39.7 us -> 17.5 us  [shards(): lax.all_to_all(outbox, 'lang', split_axis=0, concat_axis=0, tiled=True)]
    ppermute x7 -> x5, waiting for transfers between devices: 28.4 us -> 11.5 us  [the longest x1 11.3 us: shards(): cy = lax.ppermute(mine, AXES, moves(over_y))]
    all_to_all x1 -> x0, waiting for transfers between devices: 6.64 us -> none  [shards(): lax.all_to_all(owned, 'lang', split_axis=0, concat_axis=0, tiled=True)]
    all_to_all x1 -> x0, starting transfers between devices: 4.59 us -> none  [shards(): lax.all_to_all(owned, 'lang', split_axis=0, concat_axis=0, tiled=True)]
    pallas_call x2 -> x5, Pallas kernels: 24.9 us -> 28.4 us  [the longest x2 15.6 us: early(): pl.pallas_call(functools.partial(early_kernel, count), out_shape=jax.Shap...]
    squeeze x5 -> x0, local copies, waits for them, and re-layouts: 3.19 us -> none  [the longest x3 1.87 us: shards(): tails.append(back[2])]
    slice x3 -> x2, local copies, waits for them, and re-layouts: 1.96 us -> 0.04 us  [the longest x1 0.02 us: shards(): cd1 = lax.ppermute(cy[8:], AXES, moves(over_x))]
  transfers between devices with their start and end apart: 8 -> 5, of which waited for: 5 -> 2; matrix products, arithmetic and copies ran while one was open for 6% -> 0% of each run, Pallas kernels for 0% -> 17%
where the time goes in v2:
time: 94.5 us; the launch traced here: 94.2 us
  blocking collectives  40.1 us (42%)
  Pallas kernels  28.4 us (30%)
  starting transfers between devices  12.5 us (13%)
  waiting for transfers between devices  11.5 us (12%)
  local copies, waits for them, and re-layouts  1.62 us (2%)
    all_to_all x1, blocking collectives, shards(): lax.all_to_all(found.reshape(LANGS * 4, ROWS, TOPK), AXES, 0, 0, axis_ind...  22.6 us
    all_to_all x1, blocking collectives, shards(): lax.all_to_all(outbox, 'lang', split_axis=0, concat_axis=0, tiled=True)  17.5 us
    pallas_call x2, Pallas kernels, early(): pl.pallas_call(functools.partial(early_kernel, count), out_shape=jax.Shap...  15.6 us
    ppermute x1, waiting for transfers between devices, shards(): cy = lax.ppermute(mine, AXES, moves(over_y))  11.3 us
    pallas_call x1, Pallas kernels, late(): pl.pallas_call(late_kernel, out_shape=jax.ShapeDtypeStruct((LANGS, 4, ROW...  10.6 us
    ppermute x1, starting transfers between devices, shards(): far = lax.ppermute(corpus, AXES, moves(pair))  3.3 us
    ppermute x1, starting transfers between devices, shards(): cy = lax.ppermute(mine, AXES, moves(over_y))  2.62 us
    ppermute x1, starting transfers between devices, shards(): cd0 = lax.ppermute(cx[:8], AXES, moves(over_y))  2.49 us
  transfers between devices with their start and end apart: 5, of which 2 were waited for; matrix products, arithmetic and copies ran while one was open for 0% of the time, Pallas kernels for 17%

profile of v2, /device:TPU:1, one launch (start us, length us, event | category | flops | bytes accessed | tf_op | source)
XLA Modules:
  0.0 94.2 jit_solution(9692707448033164448)
XLA Ops:
  0.0 3.3 %collective-permute-start.4 = (bf16[1024,768]{1,0:T(8,128)(2,1)}, bf16[1024,768]{1,0:T(8,128)(2,1)}, u32[]{:S(2)}, u32[]{:S(2)}) collective-permute-start(bf16[1024,768]{1,0:T(8,128)(2,1)} %own.1), channel_id=1, source_target_pairs={{0,1},{1,0},{2,3},{3,2},{4,5},{5,4},{6,7},{7,6},{8,11},{9,10},{10,... | collective-permute-start | bytes 4718600 | tf_op jit(solution)/shard_map/ppermute | solution.py:358
  3.3 0.0 copy-start
  3.3 0.9 copy-done
  4.2 0.0 copy-start.1
  4.2 0.7 copy-done.1
  4.9 0.0 copy-start.2
  4.9 0.5 outbox.1
  5.3 17.5 %all_to_all.10.refs_0_.mine = bf16[16,24,768]{2,1,0:T(8,128)(2,1)S(1)} all-to-all(bf16[16,24,768]{2,1,0:T(8,128)(2,1)S(1)} %get-tuple-element.7), channel_id=1, replica_groups=mesh['lang'=16,'shard'=8] {'lang'}, dimensions={0} | all-to-all | bytes 1179648 | tf_op jit(solution)/shard_map/all_to_all | solution.py:360
  22.8 2.6 %collective-permute-start.1 = (bf16[16,24,768]{2,1,0:T(8,128)(2,1)S(1)}, bf16[16,24,768]{2,1,0:T(8,128)(2,1)S(1)}, u32[]{:S(2)}, u32[]{:S(2)}) collective-permute-start(bf16[16,24,768]{2,1,0:T(8,128)(2,1)S(1)} %all_to_all.10.refs_0_.mine), channel_id=1, source_target_pairs={{0,4},{1,5},{2,6},{3,7},{4,0},{5,1},{6,2},{7,3},{8,12},{9,13},{10,... | collective-permute-start | bytes 1769480 | tf_op jit(solution)/shard_map/ppermute | solution.py:362
  25.4 2.0 %collective-permute-start = (bf16[16,24,768]{2,1,0:T(8,128)(2,1)S(1)}, bf16[16,24,768]{2,1,0:T(8,128)(2,1)S(1)}, u32[]{:S(2)}, u32[]{:S(2)}) collective-permute-start(bf16[16,24,768]{2,1,0:T(8,128)(2,1)S(1)} %all_to_all.10.refs_0_.mine), channel_id=1, source_target_pairs={{0,2},{1,3},{2,0},{3,1},{4,6},{5,7},{6,4},{7,5},{8,10},{9,11},{10,... | collective-permute-start | bytes 1769480 | tf_op jit(solution)/shard_map/ppermute | solution.py:361
  27.5 11.3 %collective-permute-done.1.refs_1_.cy = bf16[16,24,768]{2,1,0:T(8,128)(2,1)S(1)} collective-permute-done((bf16[16,24,768]{2,1,0:T(8,128)(2,1)S(1)}, bf16[16,24,768]{2,1,0:T(8,128)(2,1)S(1)}, u32[]{:S(2)}, u32[]{:S(2)}) %collective-permute-start.1) | collective-permute-done | bytes 589856 | tf_op jit(solution)/shard_map/ppermute | solution.py:362
  38.8 2.1 %collective-permute-start.3 = (bf16[8,24,768]{2,1,0:T(8,128)(2,1)S(1)}, bf16[8,24,768]{2,1,0:T(8,128)(2,1)S(1)}, u32[]{:S(2)}, u32[]{:S(2)}) collective-permute-start(bf16[8,24,768]{2,1,0:T(8,128)(2,1)S(1)} %slice.9), channel_id=1, source_target_pairs={{0,2},{1,3},{2,0},{3,1},{4,6},{5,7},{6,4},{7,5},{8,10},{9,11},{10,... | collective-permute-start | bytes 884744 | tf_op jit(solution)/shard_map/ppermute | solution.py:364
  40.9 0.2 collective-permute-done.refs_0_.cx
  41.1 2.5 %collective-permute-start.2 = (bf16[8,24,768]{2,1,0:T(8,128)(2,1)S(1)}, bf16[8,24,768]{2,1,0:T(8,128)(2,1)S(1)}, u32[]{:S(2)}, u32[]{:S(2)}) collective-permute-start(bf16[8,24,768]{2,1,0:T(8,128)(2,1)S(1)} %slice.8), channel_id=1, source_target_pairs={{0,4},{1,5},{2,6},{3,7},{4,0},{5,1},{6,2},{7,3},{8,12},{9,13},{10,... | collective-permute-start | bytes 884744 | tf_op jit(solution)/shard_map/ppermute | solution.py:363
  43.6 0.0 collective-permute-done.4.refs_2_.refs_3_.far
  43.6 0.0 copy-done.2
  43.6 10.0 %early.3.second = f32[2,256,128]{2,1,0:T(8,128)S(1)} custom-call(bf16[16,24,768]{2,1,0:T(8,128)(2,1)S(1)} %collective-permute-done.refs_0_.cx, bf16[16,24,768]{2,1,0:T(8,128)(2,1)S(1)} %collective-permute-done.1.refs_1_.cy, bf16[1024,768]{1,0:T(8,128)(2,1)S(1)} %copy-done.2, bf16[1024,768]{1,0:T(8,128)(2,1)} %collective-permute-done.4.refs_2_.refs_3_.far), custom_call_target="tpu_custom_call" | custom-call | flops 12884901888 | bytes 1048576 | tf_op jit(solution)/shard_map/early/pallas_call | solution.py:233
  53.6 5.7 %early.2.first = f32[1,256,128]{2,1,0:T(8,128)S(1)} custom-call(bf16[16,24,768]{2,1,0:T(8,128)(2,1)S(1)} %all_to_all.10.refs_0_.mine, bf16[1024,768]{1,0:T(8,128)(2,1)S(1)} %copy-done.2, bf16[1024,768]{1,0:T(8,128)(2,1)} %collective-permute-done.4.refs_2_.refs_3_.far), custom_call_target="tpu_custom_call" | custom-call | flops 6442450944 | bytes 1048576 | tf_op jit(solution)/shard_map/early/pallas_call | solution.py:233
  59.3 0.0 collective-permute-done.3.cd1
  59.3 0.0 collective-permute-done.2.cd0
  59.3 10.6 %late.1 = f32[16,4,24,128]{3,2,1,0:T(8,128)S(1)} custom-call(s32[1]{0:T(128)} %bitcast.at, bf16[16,24,768]{2,1,0:T(8,128)(2,1)S(1)} %all_to_all.10.refs_0_.mine, bf16[16,24,768]{2,1,0:T(8,128)(2,1)S(1)} %collective-permute-done.refs_0_.cx, bf16[16,24,768]{2,1,0:T(8,128)(2,1)S(1)} %collective-permute-done.1.refs_1_.cy, ...), custom_call_target="tpu_custom_call" | custom-call | flops 12884901888 | bytes 1048576 | tf_op jit(solution)/shard_map/late/pallas_call | solution.py:246
  69.9 22.6 %all_to_all.11 = f32[64,24,128]{2,1,0:T(8,128)S(1)} all-to-all(f32[64,24,128]{2,1,0:T(8,128)S(1)} %bitcast.5), channel_id=1, replica_groups={{0,2,4,6,8,10,12,14,16,18,20,22,24,26,28,30,32,34,36,38,40,42,44,46,48,..., dimensions={0} | all-to-all | bytes 1572864 | tf_op jit(solution)/shard_map/all_to_all | solution.py:370
  92.5 1.7 %join.1 = f32[128,128]{1,0:T(8,128)} custom-call(f32[16,4,24,128]{3,2,1,0:T(8,128)S(1)} %bitcast.4, s32[1,128]{1,0:T(1,128)S(1)} %get-tuple-element.8.slots), custom_call_target="tpu_custom_call" | custom-call | tf_op jit(solution)/shard_map/join/pallas_call | solution.py:315
  (2 shorter events, 0.0 us)
Async XLA Ops:
  0.0 43.6 %collective-permute-start.4 = (bf16[1024,768]{1,0:T(8,128)(2,1)}, bf16[1024,768]{1,0:T(8,128)(2,1)}, u32[]{:S(2)}, u32[]{:S(2)}) collective-permute-start(bf16[1024,768]{1,0:T(8,128)(2,1)} %own.1), channel_id=1, source_target_pairs={{0,1},{1,0},{2,3},{3,2},{4,5},{5,4},{6,7},{7,6},{8,11},{9,10},{10,... | collective-permute-start | bytes 4718600 | tf_op jit(solution)/shard_map/ppermute | solution.py:358
  3.3 0.9 copy-start
  4.2 0.7 copy-start.1
  4.9 38.7 %copy-start.2 = (bf16[1024,768]{1,0:T(8,128)(2,1)S(1)}, bf16[1024,768]{1,0:T(8,128)(2,1)}, u32[]{:S(2)}) copy-start(bf16[1024,768]{1,0:T(8,128)(2,1)} %own.1) | copy-start | bytes 4718596
  22.8 16.0 %collective-permute-start.1 = (bf16[16,24,768]{2,1,0:T(8,128)(2,1)S(1)}, bf16[16,24,768]{2,1,0:T(8,128)(2,1)S(1)}, u32[]{:S(2)}, u32[]{:S(2)}) collective-permute-start(bf16[16,24,768]{2,1,0:T(8,128)(2,1)S(1)} %all_to_all.10.refs_0_.mine), channel_id=1, source_target_pairs={{0,4},{1,5},{2,6},{3,7},{4,0},{5,1},{6,2},{7,3},{8,12},{9,13},{10,... | collective-permute-start | bytes 1769480 | tf_op jit(solution)/shard_map/ppermute | solution.py:362
  25.4 15.7 %collective-permute-start = (bf16[16,24,768]{2,1,0:T(8,128)(2,1)S(1)}, bf16[16,24,768]{2,1,0:T(8,128)(2,1)S(1)}, u32[]{:S(2)}, u32[]{:S(2)}) collective-permute-start(bf16[16,24,768]{2,1,0:T(8,128)(2,1)S(1)} %all_to_all.10.refs_0_.mine), channel_id=1, source_target_pairs={{0,2},{1,3},{2,0},{3,1},{4,6},{5,7},{6,4},{7,5},{8,10},{9,11},{10,... | collective-permute-start | bytes 1769480 | tf_op jit(solution)/shard_map/ppermute | solution.py:361
  38.8 20.5 %collective-permute-start.3 = (bf16[8,24,768]{2,1,0:T(8,128)(2,1)S(1)}, bf16[8,24,768]{2,1,0:T(8,128)(2,1)S(1)}, u32[]{:S(2)}, u32[]{:S(2)}) collective-permute-start(bf16[8,24,768]{2,1,0:T(8,128)(2,1)S(1)} %slice.9), channel_id=1, source_target_pairs={{0,2},{1,3},{2,0},{3,1},{4,6},{5,7},{6,4},{7,5},{8,10},{9,11},{10,... | collective-permute-start | bytes 884744 | tf_op jit(solution)/shard_map/ppermute | solution.py:364
  41.1 18.2 %collective-permute-start.2 = (bf16[8,24,768]{2,1,0:T(8,128)(2,1)S(1)}, bf16[8,24,768]{2,1,0:T(8,128)(2,1)S(1)}, u32[]{:S(2)}, u32[]{:S(2)}) collective-permute-start(bf16[8,24,768]{2,1,0:T(8,128)(2,1)S(1)} %slice.8), channel_id=1, source_target_pairs={{0,4},{1,5},{2,6},{3,7},{4,0},{5,1},{6,2},{7,3},{8,12},{9,13},{10,... | collective-permute-start | bytes 884744 | tf_op jit(solution)/shard_map/ppermute | solution.py:363

commit v3 on v2

--- a/solution.py
+++ b/solution.py
@@ -176,7 +176,24 @@
     )
 
 
-def late_kernel(at, mine, cx, cy, cd0, cd1, own, far, first, second, out, rows, tails, s, u, w):
+STEPS = 800.0
+FLOOR = 32.5
+LN2 = 0.6931471805599453
+
+
+def coded(v):
+    level = jnp.round(jnp.log(jnp.abs(v)) * (STEPS / LN2) + STEPS * FLOOR)
+    level = jnp.clip(level, 0.0, 32767.0)
+    return jnp.where(v < 0, -level, level)
+
+
+def decoded(c):
+    level = jnp.abs(c)
+    v = jnp.where(level > 0, jnp.exp(level * (LN2 / STEPS) - FLOOR * LN2), 0.0)
+    return jnp.where(c < 0, -v, v)
+
+
+def late_kernel(at, mine, cx, cy, cd0, cd1, own, far, first, second, out, rows, tails, box, s, u, w):
     rows[0:128, :] = main_rows(cd0)
     rows[128:256, :] = main_rows(cd1)
     slot = lax.broadcasted_iota(jnp.int32, (64, LANGS * ROWS), 1)
@@ -209,10 +226,11 @@
                 main = tails[0, lang // 8, lang % 8 * MAIN : (lang % 8 + 1) * MAIN, :]
             else:
                 main = (first.at[0] if k == 0 else second.at[k - 1])[lang * MAIN : (lang + 1) * MAIN, :]
-            out[lang, owner[k], 0:MAIN, :] = main
+            box[k, 0:MAIN, :] = main
             start = k % 2 * 64 + lang * TAIL
-            out[lang, owner[k], MAIN:CAP, :] = tails[1, k // 2, start : start + TAIL, :]
-            out[lang, owner[k], CAP:ROWS, :] = none
+            box[k, MAIN:CAP, :] = tails[1, k // 2, start : start + TAIL, :]
+            box[k, CAP:ROWS, :] = none
+            out[lang, owner[k]] = coded(box[k]).astype(jnp.int32).astype(jnp.int16)
 
 
 COST = 2 * 256 * 2048 * 768 * 8
@@ -245,12 +263,13 @@
 def late(at, mine, cx, cy, cd0, cd1, own, far, first, second):
     return pl.pallas_call(
         late_kernel,
-        out_shape=jax.ShapeDtypeStruct((LANGS, 4, ROWS, TOPK), jnp.float32),
+        out_shape=jax.ShapeDtypeStruct((LANGS, 4, ROWS, TOPK), jnp.int16),
         in_specs=[pl.BlockSpec(memory_space=pltpu.SMEM)] + [VMEM] * 9,
         out_specs=VMEM,
         scratch_shapes=[
             pltpu.VMEM((512, WIDTH), jnp.bfloat16),
             pltpu.VMEM((2, 2, Q, TOPK), jnp.float32),
+            pltpu.VMEM((4, ROWS, TOPK), jnp.float32),
         ]
         + work(2),
         compiler_params=LIMIT,
@@ -297,13 +316,13 @@
     picks = jnp.concatenate([picks[i * Q : (i + 1) * Q, :].T for i in range(total // Q)], axis=1)
     picks = picks.astype(jnp.bfloat16)
     for k in range(4):
-        left = back[:, k].reshape(total, TOPK)
-        rows = jnp.zeros((Q, TOPK), jnp.float32)
-        for _ in range(3):
-            part = left.astype(jnp.bfloat16)
-            left = left - part.astype(jnp.float32)
-            rows = rows + jnp.dot(picks, part, preferred_element_type=jnp.float32)
-        ranks = rows.T
+        code = back[:, k].astype(jnp.int32).astype(jnp.float32).reshape(total, TOPK)
+        high = code.astype(jnp.bfloat16)
+        low = (code - high.astype(jnp.float32)).astype(jnp.bfloat16)
+        rows = jnp.dot(picks, high, preferred_element_type=jnp.float32) + jnp.dot(
+            picks, low, preferred_element_type=jnp.float32
+        )
+        ranks = decoded(rows).T
         a[pl.ds(k, TOPK, stride=8), :] = ranks
         a[pl.ds(k + 4, TOPK, stride=8), :] = ranks
     merge_top(a, 0, a, 0, b, 0, turn=2)
@@ -360,9 +379,10 @@
     mine = lax.all_to_all(outbox, "lang", split_axis=0, concat_axis=0, tiled=True)
     cx = lax.ppermute(mine, AXES, moves(over_x))
     cy = lax.ppermute(mine, AXES, moves(over_y))
+    first = early((mine,), corpus, far)
+    cx, cy, first = lax.optimization_barrier((cx, cy, first))
     cd0 = lax.ppermute(cx[:8], AXES, moves(over_y))
     cd1 = lax.ppermute(cy[8:], AXES, moves(over_x))
-    first = early((mine,), corpus, far)
     second = early((cx, cy), corpus, far)
     shard = lax.axis_index("shard")
     at = (shard // 4 * 2 + shard % 4 // 2).astype(jnp.int32).reshape(1)

time: 94.5 us -> 84.9 us (0.90)
  blocking collectives: 40.1 us -> 21.9 us
  waiting for transfers between devices: 11.5 us -> 17.6 us
  starting transfers between devices: 12.5 us -> 16.8 us
  Pallas kernels: 28.4 us -> 25.2 us
  local copies, waits for them, and re-layouts: 1.62 us -> 3.03 us
    all_to_all x1 -> x0, blocking collectives: 17.5 us -> none  [shards(): lax.all_to_all(outbox, 'lang', split_axis=0, concat_axis=0, tiled=True)]
    all_to_all x0 -> x1, waiting for transfers between devices: none -> 10.4 us  [shards(): lax.all_to_all(outbox, 'lang', split_axis=0, concat_axis=0, tiled=True)]
    ppermute x1, waiting for transfers between devices: 11.3 us -> 4.81 us  [shards(): cy = lax.ppermute(mine, AXES, moves(over_y))]
    all_to_all x0 -> x1, starting transfers between devices: none -> 6.45 us  [shards(): lax.all_to_all(outbox, 'lang', split_axis=0, concat_axis=0, tiled=True)]
    pallas_call x2, Pallas kernels: 15.6 us -> 12.8 us  [early(): pl.pallas_call(functools.partial(early_kernel, count), out_shape=jax.Shap...]
    ppermute x1, starting transfers between devices: 2.49 us -> 0.35 us  [shards(): cd0 = lax.ppermute(cx[:8], AXES, moves(over_y))]
    ppermute x1, waiting for transfers between devices: 0.21 us -> 2.34 us  [shards(): cx = lax.ppermute(mine, AXES, moves(over_x))]
    unnamed x6, local copies, waits for them, and re-layouts: 1.58 us -> 2.99 us
  transfers between devices with their start and end apart: 5 -> 6, of which waited for: 2 -> 3; matrix products, arithmetic and copies ran while one was open for 0% -> 0% of each run, Pallas kernels for 17% -> 17%
where the time goes in v3:
time: 84.9 us; the launch traced here: 84.6 us
  Pallas kernels  25.2 us (30%)
  blocking collectives  21.9 us (26%)
  waiting for transfers between devices  17.6 us (21%)
  starting transfers between devices  16.8 us (20%)
  local copies, waits for them, and re-layouts  3.03 us (4%)
    all_to_all x1, blocking collectives, shards(): lax.all_to_all(found.reshape(LANGS * 4, ROWS, TOPK), AXES, 0, 0, axis_ind...  21.9 us
    pallas_call x2, Pallas kernels, early(): pl.pallas_call(functools.partial(early_kernel, count), out_shape=jax.Shap...  12.8 us
    all_to_all x1, waiting for transfers between devices, shards(): lax.all_to_all(outbox, 'lang', split_axis=0, concat_axis=0, tiled=True)  10.4 us
    pallas_call x1, Pallas kernels, late(): pl.pallas_call(late_kernel, out_shape=jax.ShapeDtypeStruct((LANGS, 4, ROW...  9.5 us
    all_to_all x1, starting transfers between devices, shards(): lax.all_to_all(outbox, 'lang', split_axis=0, concat_axis=0, tiled=True)  6.45 us
    ppermute x1, waiting for transfers between devices, shards(): cy = lax.ppermute(mine, AXES, moves(over_y))  4.81 us
    ppermute x1, starting transfers between devices, shards(): far = lax.ppermute(corpus, AXES, moves(pair))  3.3 us
    unnamed x6, local copies, waits for them, and re-layouts  2.99 us
  transfers between devices with their start and end apart: 6, of which 3 were waited for; matrix products, arithmetic and copies ran while one was open for 0% of the time, Pallas kernels for 17%

profile of v3, /device:TPU:1, one launch (start us, length us, event | category | flops | bytes accessed | tf_op | source)
XLA Modules:
  0.0 84.6 jit_solution(5039726914236881684)
XLA Ops:
  0.0 3.3 %collective-permute-start.2 = (bf16[1024,768]{1,0:T(8,128)(2,1)}, bf16[1024,768]{1,0:T(8,128)(2,1)S(1)}, u32[]{:S(2)}, u32[]{:S(2)}) collective-permute-start(bf16[1024,768]{1,0:T(8,128)(2,1)} %own.1), channel_id=1, source_target_pairs={{0,1},{1,0},{2,3},{3,2},{4,5},{5,4},{6,7},{7,6},{8,11},{9,10},{10,... | collective-permute-start | bytes 4718600 | tf_op jit(solution)/shard_map/ppermute | solution.py:377
  3.3 0.0 copy-start
  3.3 0.9 %copy-done = bf16[128,768]{1,0:T(8,128)(2,1)S(1)} copy-done((bf16[128,768]{1,0:T(8,128)(2,1)S(1)}, bf16[128,768]{1,0:T(8,128)(2,1)}, u32[]{:S(2)}) %copy-start) | copy-done | bytes 196632
  4.2 0.0 copy-start.1
  4.2 0.7 copy-done.1
  4.9 1.3 %outbox.1 = (bf16[16,24,768]{2,1,0:T(8,128)(2,1)}, s32[1,128]{1,0:T(1,128)S(1)}) custom-call(bf16[128,768]{1,0:T(8,128)(2,1)S(1)} %copy-done, s32[1,128]{1,0:T(1,128)S(1)} %bitcast.6), custom_call_target="tpu_custom_call" | custom-call | tf_op jit(solution)/shard_map/outbox/pallas_call | solution.py:299
  6.2 6.5 %all-to-all-start = ((bf16[16,24,768]{2,1,0:T(8,128)(2,1)}), bf16[16,24,768]{2,1,0:T(8,128)(2,1)S(1)}, u32[]{:S(2)}, u32[]{:S(2)}) async-start(bf16[16,24,768]{2,1,0:T(8,128)(2,1)} %get-tuple-element.10), calls=%async_computation | async-start | bytes 1179648 | tf_op jit(solution)/shard_map/all_to_all | solution.py:379
  12.6 10.4 %all-to-all-done.refs_0_.mine = bf16[16,24,768]{2,1,0:T(8,128)(2,1)S(1)} async-done(((bf16[16,24,768]{2,1,0:T(8,128)(2,1)}), bf16[16,24,768]{2,1,0:T(8,128)(2,1)S(1)}, u32[]{:S(2)}, u32[]{:S(2)}) %all-to-all-start) | async-done | bytes 589856 | tf_op jit(solution)/shard_map/all_to_all | solution.py:379
  23.0 2.6 %collective-permute-start.1 = (bf16[16,24,768]{2,1,0:T(8,128)(2,1)S(1)}, bf16[16,24,768]{2,1,0:T(8,128)(2,1)S(1)}, u32[]{:S(2)}, u32[]{:S(2)}) collective-permute-start(bf16[16,24,768]{2,1,0:T(8,128)(2,1)S(1)} %all-to-all-done.refs_0_.mine), channel_id=1, source_target_pairs={{0,4},{1,5},{2,6},{3,7},{4,0},{5,1},{6,2},{7,3},{8,12},{9,13},{10,... | collective-permute-start | bytes 1769480 | tf_op jit(solution)/shard_map/ppermute | solution.py:381
  25.6 2.0 %collective-permute-start = (bf16[16,24,768]{2,1,0:T(8,128)(2,1)S(1)}, bf16[16,24,768]{2,1,0:T(8,128)(2,1)S(1)}, u32[]{:S(2)}, u32[]{:S(2)}) collective-permute-start(bf16[16,24,768]{2,1,0:T(8,128)(2,1)S(1)} %all-to-all-done.refs_0_.mine), channel_id=1, source_target_pairs={{0,2},{1,3},{2,0},{3,1},{4,6},{5,7},{6,4},{7,5},{8,10},{9,11},{10,... | collective-permute-start | bytes 1769480 | tf_op jit(solution)/shard_map/ppermute | solution.py:380
  27.7 0.0 collective-permute-done.2.refs_2_.refs_3_.far
  27.7 0.0 copy-start.2
  27.7 1.4 %copy-done.2 = bf16[1024,768]{1,0:T(8,128)(2,1)S(1)} copy-done((bf16[1024,768]{1,0:T(8,128)(2,1)S(1)}, bf16[1024,768]{1,0:T(8,128)(2,1)}, u32[]{:S(2)}) %copy-start.2) | copy-done | bytes 1572888
  29.1 4.2 %early.2.first = f32[1,256,128]{2,1,0:T(8,128)S(1)} custom-call(bf16[16,24,768]{2,1,0:T(8,128)(2,1)S(1)} %all-to-all-done.refs_0_.mine, bf16[1024,768]{1,0:T(8,128)(2,1)S(1)} %copy-done.2, bf16[1024,768]{1,0:T(8,128)(2,1)S(1)} %collective-permute-done.2.refs_2_.refs_3_.far), custom_call_target="tpu_custom_call" | custom-call | flops 6442450944 | bytes 1048576 | tf_op jit(solution)/shard_map/early/pallas_call | solution.py:251
  33.3 4.8 %collective-permute-done.1.refs_1_.cy = bf16[16,24,768]{2,1,0:T(8,128)(2,1)S(1)} collective-permute-done((bf16[16,24,768]{2,1,0:T(8,128)(2,1)S(1)}, bf16[16,24,768]{2,1,0:T(8,128)(2,1)S(1)}, u32[]{:S(2)}, u32[]{:S(2)}) %collective-permute-start.1) | collective-permute-done | bytes 589856 | tf_op jit(solution)/shard_map/ppermute | solution.py:381
  38.1 2.3 %collective-permute-done.refs_0_.cx = bf16[16,24,768]{2,1,0:T(8,128)(2,1)S(1)} collective-permute-done((bf16[16,24,768]{2,1,0:T(8,128)(2,1)S(1)}, bf16[16,24,768]{2,1,0:T(8,128)(2,1)S(1)}, u32[]{:S(2)}, u32[]{:S(2)}) %collective-permute-start) | collective-permute-done | bytes 589856 | tf_op jit(solution)/shard_map/ppermute | solution.py:380
  40.5 2.1 %collective-permute-start.4 = (bf16[8,24,768]{2,1,0:T(8,128)(2,1)S(1)}, bf16[8,24,768]{2,1,0:T(8,128)(2,1)S(1)}, u32[]{:S(2)}, u32[]{:S(2)}) collective-permute-start(bf16[8,24,768]{2,1,0:T(8,128)(2,1)S(1)} %slice.7), channel_id=1, source_target_pairs={{0,2},{1,3},{2,0},{3,1},{4,6},{5,7},{6,4},{7,5},{8,10},{9,11},{10,... | collective-permute-start | bytes 884744 | tf_op jit(solution)/shard_map/ppermute | solution.py:385
  42.6 0.3 collective-permute-start.3
  43.0 8.6 %early.3.second = f32[2,256,128]{2,1,0:T(8,128)S(1)} custom-call(bf16[16,24,768]{2,1,0:T(8,128)(2,1)S(1)} %collective-permute-done.refs_0_.cx, bf16[16,24,768]{2,1,0:T(8,128)(2,1)S(1)} %collective-permute-done.1.refs_1_.cy, bf16[1024,768]{1,0:T(8,128)(2,1)S(1)} %copy-done.2, bf16[1024,768]{1,0:T(8,128)(2,1)S(1)} %collective-permute-done.2.refs_2_.refs_3_.far), custom_call_target="tpu_custom_call" | custom-call | flops 12884901888 | bytes 1048576 | tf_op jit(solution)/shard_map/early/pallas_call | solution.py:251
  51.6 0.0 collective-permute-done.4.cd1
  51.6 0.0 collective-permute-done.3.cd0
  51.6 9.5 %late.1 = s16[16,4,24,128]{3,2,1,0:T(8,128)(2,1)S(1)} custom-call(s32[1]{0:T(128)} %bitcast.at, bf16[16,24,768]{2,1,0:T(8,128)(2,1)S(1)} %all-to-all-done.refs_0_.mine, bf16[16,24,768]{2,1,0:T(8,128)(2,1)S(1)} %collective-permute-done.refs_0_.cx, bf16[16,24,768]{2,1,0:T(8,128)(2,1)S(1)} %collective-permute-done.1.refs_1_.cy, ...), custom_call_target="tpu_custom_call" | custom-call | flops 12884901888 | bytes 1048576 | tf_op jit(solution)/shard_map/late/pallas_call | solution.py:264
  61.1 21.9 %all_to_all.10 = s16[64,24,128]{2,1,0:T(8,128)(2,1)S(1)} all-to-all(s16[64,24,128]{2,1,0:T(8,128)(2,1)S(1)} %bitcast.5), channel_id=1, replica_groups={{0,2,4,6,8,10,12,14,16,18,20,22,24,26,28,30,32,34,36,38,40,42,44,46,48,..., dimensions={0} | all-to-all | bytes 786432 | tf_op jit(solution)/shard_map/all_to_all | solution.py:390
  83.0 1.6 %join.1 = f32[128,128]{1,0:T(8,128)} custom-call(s16[16,4,24,128]{3,2,1,0:T(8,128)(2,1)S(1)} %bitcast.4, s32[1,128]{1,0:T(1,128)S(1)} %get-tuple-element.14.slots), custom_call_target="tpu_custom_call" | custom-call | tf_op jit(solution)/shard_map/join/pallas_call | solution.py:334
  (2 shorter events, 0.0 us)
Async XLA Ops:
  0.0 27.7 %collective-permute-start.2 = (bf16[1024,768]{1,0:T(8,128)(2,1)}, bf16[1024,768]{1,0:T(8,128)(2,1)S(1)}, u32[]{:S(2)}, u32[]{:S(2)}) collective-permute-start(bf16[1024,768]{1,0:T(8,128)(2,1)} %own.1), channel_id=1, source_target_pairs={{0,1},{1,0},{2,3},{3,2},{4,5},{5,4},{6,7},{7,6},{8,11},{9,10},{10,... | collective-permute-start | bytes 4718600 | tf_op jit(solution)/shard_map/ppermute | solution.py:377
  3.3 0.9 %copy-start = (bf16[128,768]{1,0:T(8,128)(2,1)S(1)}, bf16[128,768]{1,0:T(8,128)(2,1)}, u32[]{:S(2)}) copy-start(bf16[128,768]{1,0:T(8,128)(2,1)} %queries.1) | copy-start | bytes 589828
  4.2 0.7 copy-start.1
  6.2 16.9 %all-to-all-start = ((bf16[16,24,768]{2,1,0:T(8,128)(2,1)}), bf16[16,24,768]{2,1,0:T(8,128)(2,1)S(1)}, u32[]{:S(2)}, u32[]{:S(2)}) async-start(bf16[16,24,768]{2,1,0:T(8,128)(2,1)} %get-tuple-element.10), calls=%async_computation | async-start | bytes 1179648 | tf_op jit(solution)/shard_map/all_to_all | solution.py:379
  23.0 15.1 %collective-permute-start.1 = (bf16[16,24,768]{2,1,0:T(8,128)(2,1)S(1)}, bf16[16,24,768]{2,1,0:T(8,128)(2,1)S(1)}, u32[]{:S(2)}, u32[]{:S(2)}) collective-permute-start(bf16[16,24,768]{2,1,0:T(8,128)(2,1)S(1)} %all-to-all-done.refs_0_.mine), channel_id=1, source_target_pairs={{0,4},{1,5},{2,6},{3,7},{4,0},{5,1},{6,2},{7,3},{8,12},{9,13},{10,... | collective-permute-start | bytes 1769480 | tf_op jit(solution)/shard_map/ppermute | solution.py:381
  25.6 14.8 %collective-permute-start = (bf16[16,24,768]{2,1,0:T(8,128)(2,1)S(1)}, bf16[16,24,768]{2,1,0:T(8,128)(2,1)S(1)}, u32[]{:S(2)}, u32[]{:S(2)}) collective-permute-start(bf16[16,24,768]{2,1,0:T(8,128)(2,1)S(1)} %all-to-all-done.refs_0_.mine), channel_id=1, source_target_pairs={{0,2},{1,3},{2,0},{3,1},{4,6},{5,7},{6,4},{7,5},{8,10},{9,11},{10,... | collective-permute-start | bytes 1769480 | tf_op jit(solution)/shard_map/ppermute | solution.py:380
  27.7 1.4 %copy-start.2 = (bf16[1024,768]{1,0:T(8,128)(2,1)S(1)}, bf16[1024,768]{1,0:T(8,128)(2,1)}, u32[]{:S(2)}) copy-start(bf16[1024,768]{1,0:T(8,128)(2,1)} %own.1) | copy-start | bytes 4718596
  40.5 11.0 %collective-permute-start.4 = (bf16[8,24,768]{2,1,0:T(8,128)(2,1)S(1)}, bf16[8,24,768]{2,1,0:T(8,128)(2,1)S(1)}, u32[]{:S(2)}, u32[]{:S(2)}) collective-permute-start(bf16[8,24,768]{2,1,0:T(8,128)(2,1)S(1)} %slice.7), channel_id=1, source_target_pairs={{0,2},{1,3},{2,0},{3,1},{4,6},{5,7},{6,4},{7,5},{8,10},{9,11},{10,... | collective-permute-start | bytes 884744 | tf_op jit(solution)/shard_map/ppermute | solution.py:385
  42.6 9.0 %collective-permute-start.3 = (bf16[8,24,768]{2,1,0:T(8,128)(2,1)S(1)}, bf16[8,24,768]{2,1,0:T(8,128)(2,1)S(1)}, u32[]{:S(2)}, u32[]{:S(2)}) collective-permute-start(bf16[8,24,768]{2,1,0:T(8,128)(2,1)S(1)} %slice.6), channel_id=1, source_target_pairs={{0,4},{1,5},{2,6},{3,7},{4,0},{5,1},{6,2},{7,3},{8,12},{9,13},{10,... | collective-permute-start | bytes 884744 | tf_op jit(solution)/shard_map/ppermute | solution.py:384

commit v4 on v3

--- a/solution.py
+++ b/solution.py
@@ -163,17 +163,25 @@
     return chunk[:, 0:MAIN, :].reshape(-1, WIDTH)
 
 
-def early_kernel(count, *refs):
-    chunks, (own, far, out, rows, s, u, w) = refs[:count], refs[count:]
-    for k, chunk in enumerate(chunks):
-        rows[k * 256 : (k + 1) * 256, :] = main_rows(chunk)
+def first_kernel(chunk, own, far, out, both, rows, s, u, w):
+    rows[...] = main_rows(chunk)
+    both[0] = own[...]
+    both[1] = far[...]
 
     def emit(g, half, value):
-        out[g, half * Q : (half + 1) * Q, :] = value
-
-    leaders(
-        lambda g: rows[pl.ds(pl.multiple_of(g * 256, 256), 256), :], count, own, far, s, u, w, emit
-    )
+        out[half * Q : (half + 1) * Q, :] = value
+
+    leaders(lambda g: rows[...], 1, own, far, s, u, w, emit)
+
+
+def early_kernel(half0, half1, both, out, rows, s, u, w):
+    rows[0:128, :] = main_rows(half0)
+    rows[128:256, :] = main_rows(half1)
+
+    def emit(g, half, value):
+        out[half * Q : (half + 1) * Q, :] = value
+
+    leaders(lambda g: rows[...], 1, both.at[0], both.at[1], s, u, w, emit)
 
 
 STEPS = 800.0
@@ -193,7 +201,8 @@
     return jnp.where(c < 0, -v, v)
 
 
-def late_kernel(at, mine, cx, cy, cd0, cd1, own, far, first, second, out, rows, tails, box, s, u, w):
+def late_kernel(at, mine, cx0, cx1, cy0, cy1, cd0, cd1, both, r0, r1, r2, out, *scratch):
+    rows, tails, box, s, u, w = scratch
     rows[0:128, :] = main_rows(cd0)
     rows[128:256, :] = main_rows(cd1)
     slot = lax.broadcasted_iota(jnp.int32, (64, LANGS * ROWS), 1)
@@ -205,27 +214,29 @@
         flat = chunk[...].reshape(-1, WIDTH)
         return jnp.dot(sel, flat, preferred_element_type=jnp.float32).astype(jnp.bfloat16)
 
-    for k, chunk in enumerate((mine, cx, cy)):
-        rows[256 + k * 64 : 256 + (k + 1) * 64, :] = tail_of(chunk, picks)
-    rows[448:480, :] = tail_of(cd0, half_picks)
-    rows[480:512, :] = tail_of(cd1, half_picks)
-
+    rows[256:320, :] = tail_of(mine, picks)
+    for k, chunk in enumerate((cx0, cx1, cy0, cy1, cd0, cd1)):
+        rows[320 + k * 32 : 352 + k * 32, :] = tail_of(chunk, half_picks)
+
+    def emit(g, half, value):
+        tails[g, half] = value
+
+    leaders(
+        lambda g: rows[pl.ds(pl.multiple_of(g * 256, 256), 256), :], 2, both.at[0], both.at[1], s, u, w, emit
+    )
     me = at[0]
     owner = (me, me ^ 1, me ^ 2, me ^ 3)
-
-    def emit(g, half, value):
-        tails[g, half] = value
-
-    leaders(
-        lambda g: rows[pl.ds(pl.multiple_of(g * 256, 256), 256), :], 2, own, far, s, u, w, emit
-    )
     none = jnp.zeros((ROWS - CAP, TOPK), jnp.float32)
     for k in range(4):
         for lang in range(LANGS):
-            if k == 3:
-                main = tails[0, lang // 8, lang % 8 * MAIN : (lang % 8 + 1) * MAIN, :]
+            half, start = lang // 8, lang % 8 * MAIN
+            if k == 0:
+                main = r0[lang * MAIN : (lang + 1) * MAIN, :]
+            elif k < 3:
+                start += (k - 1) * Q
+                main = (r1, r2)[half][start : start + MAIN, :]
             else:
-                main = (first.at[0] if k == 0 else second.at[k - 1])[lang * MAIN : (lang + 1) * MAIN, :]
+                main = tails[0, half, start : start + MAIN, :]
             box[k, 0:MAIN, :] = main
             start = k % 2 * 64 + lang * TAIL
             box[k, MAIN:CAP, :] = tails[1, k // 2, start : start + TAIL, :]
@@ -235,50 +246,70 @@
 
 COST = 2 * 256 * 2048 * 768 * 8
 VMEM = pl.BlockSpec(memory_space=pltpu.VMEM)
-LIMIT = pltpu.CompilerParams(vmem_limit_bytes=40 << 20)
-
-
-def work(groups):
-    return [
-        pltpu.VMEM((256 * 8, 128), jnp.float32),
-        pltpu.VMEM((256 * 8, 128), jnp.float32),
-        pltpu.VMEM((128 * 8, 128), jnp.float32),
-    ]
-
-
-def early(chunks, own, far):
-    count = len(chunks)
+LIMIT = pltpu.CompilerParams(vmem_limit_bytes=14 << 20)
+WORK = [
+    pltpu.VMEM((256 * 8, 128), jnp.float32),
+    pltpu.VMEM((256 * 8, 128), jnp.float32),
+    pltpu.VMEM((128 * 8, 128), jnp.float32),
+]
+
+
+def first(chunk, own, far):
     return pl.pallas_call(
-        functools.partial(early_kernel, count),
-        out_shape=jax.ShapeDtypeStruct((count, 256, TOPK), jnp.float32),
-        in_specs=[VMEM] * (count + 2),
+        first_kernel,
+        out_shape=(
+            jax.ShapeDtypeStruct((256, TOPK), jnp.float32),
+            jax.ShapeDtypeStruct((2, 1024, WIDTH), jnp.bfloat16),
+        ),
+        in_specs=[VMEM] * 3,
+        out_specs=(VMEM, VMEM),
+        scratch_shapes=[pltpu.VMEM((256, WIDTH), jnp.bfloat16)] + WORK,
+        compiler_params=LIMIT,
+        cost_estimate=pl.CostEstimate(flops=COST, bytes_accessed=1 << 20, transcendentals=0),
+        name="first",
+    )(chunk, own, far)
+
+
+def early(half0, half1, both):
+    return pl.pallas_call(
+        early_kernel,
+        out_shape=jax.ShapeDtypeStruct((256, TOPK), jnp.float32),
+        in_specs=[VMEM] * 3,
         out_specs=VMEM,
-        scratch_shapes=[pltpu.VMEM((256 * count, WIDTH), jnp.bfloat16)] + work(count),
+        scratch_shapes=[pltpu.VMEM((256, WIDTH), jnp.bfloat16)] + WORK,
         compiler_params=LIMIT,
-        cost_estimate=pl.CostEstimate(flops=COST * count, bytes_accessed=1 << 20, transcendentals=0),
+        cost_estimate=pl.CostEstimate(flops=COST, bytes_accessed=1 << 20, transcendentals=0),
         name="early",
-    )(*chunks, own, far)
-
-
-def late(at, mine, cx, cy, cd0, cd1, own, far, first, second):
+    )(half0, half1, both)
+
+
+def late(at, chunks, both, results):
     return pl.pallas_call(
         late_kernel,
         out_shape=jax.ShapeDtypeStruct((LANGS, 4, ROWS, TOPK), jnp.int16),
-        in_specs=[pl.BlockSpec(memory_space=pltpu.SMEM)] + [VMEM] * 9,
+        in_specs=[pl.BlockSpec(memory_space=pltpu.SMEM)] + [VMEM] * 11,
         out_specs=VMEM,
         scratch_shapes=[
             pltpu.VMEM((512, WIDTH), jnp.bfloat16),
             pltpu.VMEM((2, 2, Q, TOPK), jnp.float32),
             pltpu.VMEM((4, ROWS, TOPK), jnp.float32),
         ]
-        + work(2),
+        + WORK,
         compiler_params=LIMIT,
         cost_estimate=pl.CostEstimate(flops=COST * 2, bytes_accessed=1 << 20, transcendentals=0),
         name="late",
-    )(at, mine, cx, cy, cd0, cd1, own, far, first, second)
-
-
-def outbox_kernel(queries, routes, out, slots):
+    )(at, *chunks, both, *results)
+
+
+def outbox_kernel(queries_in, routes_in, out, slots, queries, routes, sems):
+    copies = (
+        pltpu.make_async_copy(routes_in, routes, sems.at[0]),
+        pltpu.make_async_copy(queries_in, queries, sems.at[1]),
+    )
+    for copy in copies:
+        copy.start()
+    for copy in copies:
+        copy.wait()
     x = queries[...].astype(jnp.float32)
     unit = (x * lax.rsqrt(jnp.mean(x * x, axis=1, keepdims=True) + epsilon)).astype(jnp.bfloat16)
     along = jnp.broadcast_to(routes[...].astype(jnp.float32), (Q, Q))
@@ -302,8 +333,13 @@
             jax.ShapeDtypeStruct((LANGS, ROWS, WIDTH), jnp.bfloat16),
             jax.ShapeDtypeStruct((1, Q), jnp.int32),
         ),
-        in_specs=[VMEM] * 2,
+        in_specs=[pl.BlockSpec(memory_space=pltpu.HBM)] * 2,
         out_specs=(VMEM, VMEM),
+        scratch_shapes=[
+            pltpu.VMEM((Q, WIDTH), jnp.bfloat16),
+            pltpu.VMEM((1, Q), jnp.int32),
+            pltpu.SemaphoreType.DMA((2,)),
+        ],
         compiler_params=LIMIT,
         name="outbox",
     )(queries, routes)
@@ -377,16 +413,19 @@
     far = lax.ppermute(corpus, AXES, moves(pair))
     outbox, slots = outbox_of(queries, routes.reshape(1, Q))
     mine = lax.all_to_all(outbox, "lang", split_axis=0, concat_axis=0, tiled=True)
-    cx = lax.ppermute(mine, AXES, moves(over_x))
-    cy = lax.ppermute(mine, AXES, moves(over_y))
-    first = early((mine,), corpus, far)
-    cx, cy, first = lax.optimization_barrier((cx, cy, first))
-    cd0 = lax.ppermute(cx[:8], AXES, moves(over_y))
-    cd1 = lax.ppermute(cy[8:], AXES, moves(over_x))
-    second = early((cx, cy), corpus, far)
+    cx0, cy0, cx1, cy1 = (
+        lax.ppermute(part, AXES, moves(over)) for part in (mine[:8], mine[8:]) for over in (over_x, over_y)
+    )
+    r0, both = first(mine, corpus, far)
+    cx0, cy0, r0 = lax.optimization_barrier((cx0, cy0, r0))
+    cd0 = lax.ppermute(cx0, AXES, moves(over_y))
+    r1 = early(cx0, cy0, both)
+    cx1, cy1, r1 = lax.optimization_barrier((cx1, cy1, r1))
+    cd1 = lax.ppermute(cy1, AXES, moves(over_x))
+    r2 = early(cx1, cy1, both)
     shard = lax.axis_index("shard")
-    at = (shard // 4 * 2 + shard % 4 // 2).astype(jnp.int32).reshape(1)
-    found = late(at, mine, cx, cy, cd0, cd1, corpus, far, first, second)
+    at = (lax.shift_right_logical(shard, 2) * 2 + (lax.shift_right_logical(shard, 1) & 1)).reshape(1)
+    found = late(at, (mine, cx0, cx1, cy0, cy1, cd0, cd1), both, (r0, r1, r2))
     back = lax.all_to_all(
         found.reshape(LANGS * 4, ROWS, TOPK), AXES, 0, 0, axis_index_groups=TEAMS, tiled=True
     )

time: 84.9 us -> 83.1 us (0.979)
  waiting for transfers between devices: 17.6 us -> 11.2 us
  starting transfers between devices: 16.8 us -> 20.8 us
  Pallas kernels: 25.2 us -> 27 us
  local copies, waits for them, and re-layouts: 3.03 us -> 1.62 us
    ppermute x4 -> x6, waiting for transfers between devices: 7.16 us -> 0.81 us  [the longest x1 0.8 us: shards(): cd1 = lax.ppermute(cy1, AXES, moves(over_x))]
    ppermute x4 -> x6, starting transfers between devices: 7.1 us -> 11 us  [the longest x4 6.02 us: shards(): lax.ppermute(part, AXES, moves(over))]
    pallas_call x2 -> x3, Pallas kernels: 12.8 us -> 14.4 us  [the longest x2 8.51 us: early(): pl.pallas_call(early_kernel, out_shape=jax.ShapeDtypeStruct((256, TOPK),...]
    unnamed x6, local copies, waits for them, and re-layouts: 2.99 us -> 1.58 us
  transfers between devices with their start and end apart: 6 -> 8, of which waited for: 3 -> 2; matrix products, arithmetic and copies ran while one was open for 0% -> 0% of each run, Pallas kernels for 17% -> 19%
where the time goes in v4:
time: 83.1 us; the launch traced here: 82.8 us
  Pallas kernels  27 us (32%)
  blocking collectives  22.1 us (27%)
  starting transfers between devices  20.8 us (25%)
  waiting for transfers between devices  11.2 us (13%)
  local copies, waits for them, and re-layouts  1.62 us (2%)
    all_to_all x1, blocking collectives, shards(): lax.all_to_all(found.reshape(LANGS * 4, ROWS, TOPK), AXES, 0, 0, axis_ind...  22.1 us
    all_to_all x1, waiting for transfers between devices, shards(): lax.all_to_all(outbox, 'lang', split_axis=0, concat_axis=0, tiled=True)  10.4 us
    pallas_call x1, Pallas kernels, late(): pl.pallas_call(late_kernel, out_shape=jax.ShapeDtypeStruct((LANGS, 4, ROW...  9.45 us
    pallas_call x2, Pallas kernels, early(): pl.pallas_call(early_kernel, out_shape=jax.ShapeDtypeStruct((256, TOPK),...  8.51 us
    all_to_all x1, starting transfers between devices, shards(): lax.all_to_all(outbox, 'lang', split_axis=0, concat_axis=0, tiled=True)  6.46 us
    ppermute x4, starting transfers between devices, shards(): lax.ppermute(part, AXES, moves(over))  6.02 us
    pallas_call x1, Pallas kernels, first(): pl.pallas_call(first_kernel, out_shape=(jax.ShapeDtypeStruct((256, TOPK),...  5.86 us
    ppermute x1, starting transfers between devices, shards(): far = lax.ppermute(corpus, AXES, moves(pair))  3.3 us
  transfers between devices with their start and end apart: 8, of which 2 were waited for; matrix products, arithmetic and copies ran while one was open for 0% of the time, Pallas kernels for 19%

profile of v4, /device:TPU:1, one launch (start us, length us, event | category | flops | bytes accessed | tf_op | source)
XLA Modules:
  0.0 82.8 jit_solution(1711096437946157146)
XLA Ops:
  0.0 3.3 %collective-permute-start.2 = (bf16[1024,768]{1,0:T(8,128)(2,1)}, bf16[1024,768]{1,0:T(8,128)(2,1)}, u32[]{:S(2)}, u32[]{:S(2)}) collective-permute-start(bf16[1024,768]{1,0:T(8,128)(2,1)} %own.1), channel_id=1, source_target_pairs={{0,1},{1,0},{2,3},{3,2},{4,5},{5,4},{6,7},{7,6},{8,11},{9,10},{10,... | collective-permute-start | bytes 4718600 | tf_op jit(solution)/shard_map/ppermute | solution.py:413
  3.3 0.0 copy-start
  3.3 0.9 %copy-done = bf16[128,768]{1,0:T(8,128)(2,1)S(1)} copy-done((bf16[128,768]{1,0:T(8,128)(2,1)S(1)}, bf16[128,768]{1,0:T(8,128)(2,1)}, u32[]{:S(2)}) %copy-start) | copy-done | bytes 196632
  4.2 0.0 copy-start.1
  4.2 0.7 copy-done.1
  4.9 0.0 copy-start.2
  4.9 1.6 %outbox.1 = (bf16[16,24,768]{2,1,0:T(8,128)(2,1)}, s32[1,128]{1,0:T(1,128)S(1)}) custom-call(bf16[128,768]{1,0:T(8,128)(2,1)S(1)} %copy-done, s32[1,128]{1,0:T(1,128)S(1)} %bitcast.6), custom_call_target="tpu_custom_call" | custom-call | tf_op jit(solution)/shard_map/outbox/pallas_call | solution.py:330
  6.4 6.5 %all-to-all-start = ((bf16[16,24,768]{2,1,0:T(8,128)(2,1)}), bf16[16,24,768]{2,1,0:T(8,128)(2,1)S(1)}, u32[]{:S(2)}, u32[]{:S(2)}) async-start(bf16[16,24,768]{2,1,0:T(8,128)(2,1)} %get-tuple-element.15), calls=%async_computation | async-start | bytes 1179648 | tf_op jit(solution)/shard_map/all_to_all | solution.py:415
  12.9 10.4 %all-to-all-done.chunk.mine = bf16[16,24,768]{2,1,0:T(8,128)(2,1)S(1)} async-done(((bf16[16,24,768]{2,1,0:T(8,128)(2,1)}), bf16[16,24,768]{2,1,0:T(8,128)(2,1)S(1)}, u32[]{:S(2)}, u32[]{:S(2)}) %all-to-all-start) | async-done | bytes 589856 | tf_op jit(solution)/shard_map/all_to_all | solution.py:415
  23.4 2.1 %collective-permute-start = (bf16[8,24,768]{2,1,0:T(8,128)(2,1)S(1)}, bf16[8,24,768]{2,1,0:T(8,128)(2,1)S(1)}, u32[]{:S(2)}, u32[]{:S(2)}) collective-permute-start(bf16[8,24,768]{2,1,0:T(8,128)(2,1)S(1)} %get-tuple-element.26), channel_id=1, source_target_pairs={{0,2},{1,3},{2,0},{3,1},{4,6},{5,7},{6,4},{7,5},{8,10},{9,11},{10,... | collective-permute-start | bytes 884744 | tf_op jit(solution)/shard_map/ppermute | solution.py:417
  25.5 2.6 %collective-permute-start.1 = (bf16[8,24,768]{2,1,0:T(8,128)(2,1)S(1)}, bf16[8,24,768]{2,1,0:T(8,128)(2,1)S(1)}, u32[]{:S(2)}, u32[]{:S(2)}) collective-permute-start(bf16[8,24,768]{2,1,0:T(8,128)(2,1)S(1)} %get-tuple-element.26), channel_id=1, source_target_pairs={{0,4},{1,5},{2,6},{3,7},{4,0},{5,1},{6,2},{7,3},{8,12},{9,13},{10,... | collective-permute-start | bytes 884744 | tf_op jit(solution)/shard_map/ppermute | solution.py:417
  28.1 0.9 %collective-permute-start.3 = (bf16[8,24,768]{2,1,0:T(8,128)(2,1)S(1)}, bf16[8,24,768]{2,1,0:T(8,128)(2,1)S(1)}, u32[]{:S(2)}, u32[]{:S(2)}) collective-permute-start(bf16[8,24,768]{2,1,0:T(8,128)(2,1)S(1)} %get-tuple-element.25), channel_id=1, source_target_pairs={{0,2},{1,3},{2,0},{3,1},{4,6},{5,7},{6,4},{7,5},{8,10},{9,11},{10,... | collective-permute-start | bytes 884744 | tf_op jit(solution)/shard_map/ppermute | solution.py:417
  29.0 0.3 collective-permute-start.4
  29.4 0.0 collective-permute-done.2.far
  29.4 0.0 copy-done.2
  29.4 5.9 %first.1 = (f32[256,128]{1,0:T(8,128)S(1)}, bf16[2,1024,768]{2,1,0:T(8,128)(2,1)S(1)}) custom-call(bf16[16,24,768]{2,1,0:T(8,128)(2,1)S(1)} %all-to-all-done.chunk.mine, bf16[1024,768]{1,0:T(8,128)(2,1)S(1)} %copy-done.2, bf16[1024,768]{1,0:T(8,128)(2,1)} %collective-permute-done.2.far), custom_call_target="tpu_custom_call" | custom-call | flops 6442450944 | bytes 1048576 | tf_op jit(solution)/shard_map/first/pallas_call | solution.py:258
  35.3 0.0 collective-permute-done.half0.cx0
  35.3 0.0 collective-permute-done.1.half1.cy0
  35.3 2.7 %collective-permute-start.5 = (bf16[8,24,768]{2,1,0:T(8,128)(2,1)S(1)}, bf16[8,24,768]{2,1,0:T(8,128)(2,1)S(1)}, u32[]{:S(2)}, u32[]{:S(2)}) collective-permute-start(bf16[8,24,768]{2,1,0:T(8,128)(2,1)S(1)} %collective-permute-done.half0.cx0), channel_id=1, source_target_pairs={{0,4},{1,5},{2,6},{3,7},{4,0},{5,1},{6,2},{7,3},{8,12},{9,13},{10,... | collective-permute-start | bytes 884744 | tf_op jit(solution)/shard_map/ppermute | solution.py:421
  38.0 4.3 %early.2.r1 = f32[256,128]{1,0:T(8,128)S(1)} custom-call(bf16[8,24,768]{2,1,0:T(8,128)(2,1)S(1)} %collective-permute-done.half0.cx0, bf16[8,24,768]{2,1,0:T(8,128)(2,1)S(1)} %collective-permute-done.1.half1.cy0, bf16[2,1024,768]{2,1,0:T(8,128)(2,1)S(1)} %get-tuple-element.19.both), custom_call_target="tpu_custom_call" | custom-call | flops 6442450944 | bytes 1048576 | tf_op jit(solution)/shard_map/early/pallas_call | solution.py:274
  42.2 0.0 collective-permute-done.3.half0.cx1
  42.3 0.0 collective-permute-done.4.half1.cy1
  42.3 2.3 %collective-permute-start.6 = (bf16[8,24,768]{2,1,0:T(8,128)(2,1)S(1)}, bf16[8,24,768]{2,1,0:T(8,128)(2,1)S(1)}, u32[]{:S(2)}, u32[]{:S(2)}) collective-permute-start(bf16[8,24,768]{2,1,0:T(8,128)(2,1)S(1)} %collective-permute-done.4.half1.cy1), channel_id=1, source_target_pairs={{0,2},{1,3},{2,0},{3,1},{4,6},{5,7},{6,4},{7,5},{8,10},{9,11},{10,... | collective-permute-start | bytes 884744 | tf_op jit(solution)/shard_map/ppermute | solution.py:424
  44.6 4.2 %early.3.r2 = f32[256,128]{1,0:T(8,128)S(1)} custom-call(bf16[8,24,768]{2,1,0:T(8,128)(2,1)S(1)} %collective-permute-done.3.half0.cx1, bf16[8,24,768]{2,1,0:T(8,128)(2,1)S(1)} %collective-permute-done.4.half1.cy1, bf16[2,1024,768]{2,1,0:T(8,128)(2,1)S(1)} %get-tuple-element.19.both), custom_call_target="tpu_custom_call" | custom-call | flops 6442450944 | bytes 1048576 | tf_op jit(solution)/shard_map/early/pallas_call | solution.py:274
  48.8 0.8 collective-permute-done.6.cd1
  49.6 0.0 collective-permute-done.5.cd0
  49.6 9.5 %late.1 = s16[16,4,24,128]{3,2,1,0:T(8,128)(2,1)S(1)} custom-call(s32[1]{0:T(128)} %bitcast.at, bf16[16,24,768]{2,1,0:T(8,128)(2,1)S(1)} %all-to-all-done.chunk.mine, bf16[8,24,768]{2,1,0:T(8,128)(2,1)S(1)} %collective-permute-done.half0.cx0, bf16[8,24,768]{2,1,0:T(8,128)(2,1)S(1)} %collective-permute-done.3.half0.cx1, ...), custom_call_target="tpu_custom_call" | custom-call | flops 12884901888 | bytes 1048576 | tf_op jit(solution)/shard_map/late/pallas_call | solution.py:287
  59.1 22.1 %all_to_all.10 = s16[64,24,128]{2,1,0:T(8,128)(2,1)S(1)} all-to-all(s16[64,24,128]{2,1,0:T(8,128)(2,1)S(1)} %bitcast.5), channel_id=1, replica_groups={{0,2,4,6,8,10,12,14,16,18,20,22,24,26,28,30,32,34,36,38,40,42,44,46,48,..., dimensions={0} | all-to-all | bytes 786432 | tf_op jit(solution)/shard_map/all_to_all | solution.py:429
  81.1 1.6 %join.1 = f32[128,128]{1,0:T(8,128)} custom-call(s16[16,4,24,128]{3,2,1,0:T(8,128)(2,1)S(1)} %bitcast.4, s32[1,128]{1,0:T(1,128)S(1)} %get-tuple-element.24.slots), custom_call_target="tpu_custom_call" | custom-call | tf_op jit(solution)/shard_map/join/pallas_call | solution.py:370
  (1 shorter events, 0.0 us)
Async XLA Ops:
  0.0 29.4 %collective-permute-start.2 = (bf16[1024,768]{1,0:T(8,128)(2,1)}, bf16[1024,768]{1,0:T(8,128)(2,1)}, u32[]{:S(2)}, u32[]{:S(2)}) collective-permute-start(bf16[1024,768]{1,0:T(8,128)(2,1)} %own.1), channel_id=1, source_target_pairs={{0,1},{1,0},{2,3},{3,2},{4,5},{5,4},{6,7},{7,6},{8,11},{9,10},{10,... | collective-permute-start | bytes 4718600 | tf_op jit(solution)/shard_map/ppermute | solution.py:413
  3.3 0.9 %copy-start = (bf16[128,768]{1,0:T(8,128)(2,1)S(1)}, bf16[128,768]{1,0:T(8,128)(2,1)}, u32[]{:S(2)}) copy-start(bf16[128,768]{1,0:T(8,128)(2,1)} %queries_in.1) | copy-start | bytes 589828
  4.2 0.7 copy-start.1
  4.9 24.5 %copy-start.2 = (bf16[1024,768]{1,0:T(8,128)(2,1)S(1)}, bf16[1024,768]{1,0:T(8,128)(2,1)}, u32[]{:S(2)}) copy-start(bf16[1024,768]{1,0:T(8,128)(2,1)} %own.1) | copy-start | bytes 4718596
  6.4 16.9 %all-to-all-start = ((bf16[16,24,768]{2,1,0:T(8,128)(2,1)}), bf16[16,24,768]{2,1,0:T(8,128)(2,1)S(1)}, u32[]{:S(2)}, u32[]{:S(2)}) async-start(bf16[16,24,768]{2,1,0:T(8,128)(2,1)} %get-tuple-element.15), calls=%async_computation | async-start | bytes 1179648 | tf_op jit(solution)/shard_map/all_to_all | solution.py:415
  23.4 11.9 %collective-permute-start = (bf16[8,24,768]{2,1,0:T(8,128)(2,1)S(1)}, bf16[8,24,768]{2,1,0:T(8,128)(2,1)S(1)}, u32[]{:S(2)}, u32[]{:S(2)}) collective-permute-start(bf16[8,24,768]{2,1,0:T(8,128)(2,1)S(1)} %get-tuple-element.26), channel_id=1, source_target_pairs={{0,2},{1,3},{2,0},{3,1},{4,6},{5,7},{6,4},{7,5},{8,10},{9,11},{10,... | collective-permute-start | bytes 884744 | tf_op jit(solution)/shard_map/ppermute | solution.py:417
  25.5 9.8 %collective-permute-start.1 = (bf16[8,24,768]{2,1,0:T(8,128)(2,1)S(1)}, bf16[8,24,768]{2,1,0:T(8,128)(2,1)S(1)}, u32[]{:S(2)}, u32[]{:S(2)}) collective-permute-start(bf16[8,24,768]{2,1,0:T(8,128)(2,1)S(1)} %get-tuple-element.26), channel_id=1, source_target_pairs={{0,4},{1,5},{2,6},{3,7},{4,0},{5,1},{6,2},{7,3},{8,12},{9,13},{10,... | collective-permute-start | bytes 884744 | tf_op jit(solution)/shard_map/ppermute | solution.py:417
  28.1 14.2 %collective-permute-start.3 = (bf16[8,24,768]{2,1,0:T(8,128)(2,1)S(1)}, bf16[8,24,768]{2,1,0:T(8,128)(2,1)S(1)}, u32[]{:S(2)}, u32[]{:S(2)}) collective-permute-start(bf16[8,24,768]{2,1,0:T(8,128)(2,1)S(1)} %get-tuple-element.25), channel_id=1, source_target_pairs={{0,2},{1,3},{2,0},{3,1},{4,6},{5,7},{6,4},{7,5},{8,10},{9,11},{10,... | collective-permute-start | bytes 884744 | tf_op jit(solution)/shard_map/ppermute | solution.py:417
  29.0 13.2 %collective-permute-start.4 = (bf16[8,24,768]{2,1,0:T(8,128)(2,1)S(1)}, bf16[8,24,768]{2,1,0:T(8,128)(2,1)S(1)}, u32[]{:S(2)}, u32[]{:S(2)}) collective-permute-start(bf16[8,24,768]{2,1,0:T(8,128)(2,1)S(1)} %get-tuple-element.25), channel_id=1, source_target_pairs={{0,4},{1,5},{2,6},{3,7},{4,0},{5,1},{6,2},{7,3},{8,12},{9,13},{10,... | collective-permute-start | bytes 884744 | tf_op jit(solution)/shard_map/ppermute | solution.py:417
  35.3 14.3 %collective-permute-start.5 = (bf16[8,24,768]{2,1,0:T(8,128)(2,1)S(1)}, bf16[8,24,768]{2,1,0:T(8,128)(2,1)S(1)}, u32[]{:S(2)}, u32[]{:S(2)}) collective-permute-start(bf16[8,24,768]{2,1,0:T(8,128)(2,1)S(1)} %collective-permute-done.half0.cx0), channel_id=1, source_target_pairs={{0,4},{1,5},{2,6},{3,7},{4,0},{5,1},{6,2},{7,3},{8,12},{9,13},{10,... | collective-permute-start | bytes 884744 | tf_op jit(solution)/shard_map/ppermute | solution.py:421
  42.3 7.3 %collective-permute-start.6 = (bf16[8,24,768]{2,1,0:T(8,128)(2,1)S(1)}, bf16[8,24,768]{2,1,0:T(8,128)(2,1)S(1)}, u32[]{:S(2)}, u32[]{:S(2)}) collective-permute-start(bf16[8,24,768]{2,1,0:T(8,128)(2,1)S(1)} %collective-permute-done.4.half1.cy1), channel_id=1, source_target_pairs={{0,2},{1,3},{2,0},{3,1},{4,6},{5,7},{6,4},{7,5},{8,10},{9,11},{10,... | collective-permute-start | bytes 884744 | tf_op jit(solution)/shard_map/ppermute | solution.py:424

commit v5 on v4

--- a/solution.py
+++ b/solution.py
@@ -35,6 +35,7 @@
 
 
 SORT32 = batcher(32)
+SORT16 = batcher(16)
 
 
 def wire(ref, base, i):
@@ -124,16 +125,20 @@
     lax.fori_loop(0, n, step, 0)
 
 
+def quarter_scores(corpus, rows, s, quarter):
+    part = lax.dot_general(
+        corpus[quarter * 256 : (quarter + 1) * 256, :],
+        rows,
+        (((1,), (1,)), ((), ())),
+        preferred_element_type=jnp.float32,
+    )
+    for half in range(2):
+        s[pl.ds(quarter * 2 + half, 256, stride=8), :] = part[:, half * 128 : (half + 1) * 128]
+
+
 def score(corpus, rows, s):
     for quarter in range(4):
-        part = lax.dot_general(
-            corpus[quarter * 256 : (quarter + 1) * 256, :],
-            rows,
-            (((1,), (1,)), ((), ())),
-            preferred_element_type=jnp.float32,
-        )
-        for half in range(2):
-            s[pl.ds(quarter * 2 + half, 256, stride=8), :] = part[:, half * 128 : (half + 1) * 128]
+        quarter_scores(corpus, rows, s, quarter)
 
 
 def order(s, u, dst):
@@ -143,27 +148,116 @@
     merge_top(s, 0, s, 128, dst, 0)
 
 
-def leaders(rows_of, groups, own, far, s, u, w, emit):
-    def group(g):
-        rows = rows_of(g)
-        score(own, rows, s)
-        order(s, u, w)
-        score(far, rows, s)
-        order(s, u, u)
-        merge_top(w, 0, u, 0, s, 0)
-        merge_top(s, 0, s, 0, u, 0, turn=4)
-        merge_top(u, 0, u, 0, s, 0, turn=2)
+def network(v, pairs):
+    for i, j in pairs:
+        v[i], v[j] = jnp.maximum(v[i], v[j]), jnp.minimum(v[i], v[j])
+    return v
+
+
+def best16(ref, base):
+    a = network([wire(ref, base, i) for i in range(16)], SORT16)
+    b = network([wire(ref, base, i) for i in range(16, 32)], SORT16)
+    return clean([jnp.maximum(a[i], b[15 - i]) for i in range(16)])
+
+
+def shorten(src, base, dst, dst_base):
+    a = best16(src, base)
+    b = best16(src, base + 32)
+    peak = jnp.maximum(a[15], b[15])
+    high = clean([jnp.maximum(a[i], b[15 - i]) for i in range(16)])
+    low = clean([jnp.minimum(a[i], b[15 - i]) for i in range(16)])
+    for i in range(16):
+        put(dst, dst_base, i, high[i])
+        put(dst, dst_base, 16 + i, low[i])
+    return peak
+
+
+def best32(src, base, dst, dst_base):
+    v = clean([jnp.maximum(wire(src, base, i), wire(src, base, 63 - i)) for i in range(32)])
+    for i in range(32):
+        put(dst, dst_base, i, v[i])
+    return v[31]
+
+
+def best64(src, dst):
+    v = []
+    for i in range(32):
+        a = jnp.maximum(wire(src, 0, i), wire(src, 0, 127 - i))
+        b = jnp.maximum(wire(src, 0, i + 32), wire(src, 0, 95 - i))
+        v.append(jnp.maximum(a, b))
+        put(dst, 32, i, jnp.minimum(a, b))
+    v = clean(v)
+    for i in range(32):
+        put(dst, 0, i, v[i])
+    clean_at(dst, 32)
+    return wire(dst, 63, 0)
+
+
+def merge_turned(src, dst, turn):
+    for op, at in ((jnp.maximum, 0), (jnp.minimum, 64)):
+        v = []
+        for i in range(32):
+            a = op(wire(src, 0, i), pltpu.roll(wire(src, 0, 63 - i), turn, 0))
+            b = op(wire(src, 0, i + 32), pltpu.roll(wire(src, 0, 31 - i), turn, 0))
+            v.append(jnp.maximum(a, b))
+            put(dst, at + 32, i, jnp.minimum(a, b))
+        v = clean(v)
+        for i in range(32):
+            put(dst, at, i, v[i])
+        clean_at(dst, at + 32)
+
+
+def leaders(groups, own, far, s, s2, u, w, emit):
+    units = [(g, corpus) for g in range(len(groups)) for corpus in (own, far)]
+    buffers = (s, s2)
+    score(own, groups[0](), s)
+    peak = None
+    for k, (g, _) in enumerate(units):
+        here = buffers[k % 2]
+        ahead = units[k + 1] if k + 1 < len(units) else None
+        ahead_rows = groups[ahead[0]]() if ahead else None
+        base = (k % 2) * 128
+        for i in range(4):
+            if ahead:
+                quarter_scores(ahead[1], ahead_rows, buffers[(k + 1) % 2], i)
+            now = shorten(here, i * 64, u, base + i * 32)
+            peak = now if peak is None else jnp.maximum(peak, now)
+        if k % 2 == 0:
+            continue
+        for i in range(4):
+            peak = jnp.maximum(peak, best32(u, i * 64, w, i * 32))
+        loop(2, lambda i: merge64(w, i * 64, u))
+        peak = jnp.maximum(peak, best64(u, w))
+        merge_turned(w, u, 4)
+        merge_top(u, 0, u, 0, w, 0, turn=2)
+        peak = jnp.maximum(peak, pltpu.roll(peak, 4, 0))
+        peak = jnp.maximum(peak, pltpu.roll(peak, 2, 0))
+        unsure = jnp.max(jnp.where(peak > wire(w, 127, 0), 1.0, 0.0)) > 0.0
+        peak = None
+
+        @pl.when(unsure)
+        def _():
+            long_way(groups[g](), own, far, s2, u, w)
+
         for half in range(2):
-            emit(g, half, s[pl.ds(half, TOPK, stride=8), :].T)
-
-    loop(groups, group)
+            emit(g, half, w[pl.ds(half, TOPK, stride=8), :].T)
+
+
+def long_way(rows, own, far, s, u, w):
+    score(own, rows, s)
+    order(s, u, w)
+    score(far, rows, s)
+    order(s, u, u)
+    merge_top(w, 0, u, 0, s, 0)
+    merge_top(s, 0, s, 0, u, 0, turn=4)
+    merge_top(u, 0, u, 0, w, 0, turn=2)
 
 
 def main_rows(chunk):
     return chunk[:, 0:MAIN, :].reshape(-1, WIDTH)
 
 
-def first_kernel(chunk, own, far, out, both, rows, s, u, w):
+def first_kernel(chunk, own, far, out, both, rows, *work):
     rows[...] = main_rows(chunk)
     both[0] = own[...]
     both[1] = far[...]
@@ -171,17 +265,17 @@
     def emit(g, half, value):
         out[half * Q : (half + 1) * Q, :] = value
 
-    leaders(lambda g: rows[...], 1, own, far, s, u, w, emit)
-
-
-def early_kernel(half0, half1, both, out, rows, s, u, w):
+    leaders([lambda: rows[...]], own, far, *work, emit)
+
+
+def early_kernel(half0, half1, both, out, rows, *work):
     rows[0:128, :] = main_rows(half0)
     rows[128:256, :] = main_rows(half1)
 
     def emit(g, half, value):
         out[half * Q : (half + 1) * Q, :] = value
 
-    leaders(lambda g: rows[...], 1, both.at[0], both.at[1], s, u, w, emit)
+    leaders([lambda: rows[...]], both.at[0], both.at[1], *work, emit)
 
 
 STEPS = 800.0
@@ -202,7 +296,7 @@
 
 
 def late_kernel(at, mine, cx0, cx1, cy0, cy1, cd0, cd1, both, r0, r1, r2, out, *scratch):
-    rows, tails, box, s, u, w = scratch
+    rows, tails, box, *work = scratch
     rows[0:128, :] = main_rows(cd0)
     rows[128:256, :] = main_rows(cd1)
     slot = lax.broadcasted_iota(jnp.int32, (64, LANGS * ROWS), 1)
@@ -222,7 +316,7 @@
         tails[g, half] = value
 
     leaders(
-        lambda g: rows[pl.ds(pl.multiple_of(g * 256, 256), 256), :], 2, both.at[0], both.at[1], s, u, w, emit
+        [lambda: rows[0:256, :], lambda: rows[256:512, :]], both.at[0], both.at[1], *work, emit
     )
     me = at[0]
     owner = (me, me ^ 1, me ^ 2, me ^ 3)
@@ -248,6 +342,7 @@
 VMEM = pl.BlockSpec(memory_space=pltpu.VMEM)
 LIMIT = pltpu.CompilerParams(vmem_limit_bytes=14 << 20)
 WORK = [
+    pltpu.VMEM((256 * 8, 128), jnp.float32),
     pltpu.VMEM((256 * 8, 128), jnp.float32),
     pltpu.VMEM((256 * 8, 128), jnp.float32),
     pltpu.VMEM((128 * 8, 128), jnp.float32),

time: 83.1 us -> 79.7 us (0.959)
  Pallas kernels: 27 us -> 18.5 us
  waiting for transfers between devices: 11.2 us -> 15.5 us
  blocking collectives: 22.1 us -> 24 us
  starting transfers between devices: 20.8 us -> 19.7 us
    pallas_call x2, Pallas kernels: 8.51 us -> 5.06 us  [early(): pl.pallas_call(early_kernel, out_shape=jax.ShapeDtypeStruct((256, TOPK),...]
    pallas_call x1, Pallas kernels: 9.45 us -> 6.07 us  [late(): pl.pallas_call(late_kernel, out_shape=jax.ShapeDtypeStruct((LANGS, 4, ROW...]
    ppermute x1, waiting for transfers between devices: 0.8 us -> 3.56 us  [shards(): cd1 = lax.ppermute(cy1, AXES, moves(over_x))]
    all_to_all x1, blocking collectives: 22.1 us -> 24 us  [shards(): lax.all_to_all(found.reshape(LANGS * 4, ROWS, TOPK), AXES, 0, 0, axis_ind...]
    pallas_call x1, Pallas kernels: 5.86 us -> 4.18 us  [first(): pl.pallas_call(first_kernel, out_shape=(jax.ShapeDtypeStruct((256, TOPK),...]
    ppermute x4, waiting for transfers between devices: 0.01 us -> 1.56 us  [shards(): lax.ppermute(part, AXES, moves(over))]
    ppermute x1, starting transfers between devices: 2.28 us -> 1.28 us  [shards(): cd1 = lax.ppermute(cy1, AXES, moves(over_x))]
  transfers between devices with their start and end apart: 8 -> 8, of which waited for: 2 -> 4; matrix products, arithmetic and copies ran while one was open for 0% -> 0% of each run, Pallas kernels for 19% -> 14%
where the time goes in v5:
time: 79.7 us; the launch traced here: 79.4 us
  blocking collectives  24 us (30%)
  starting transfers between devices  19.7 us (25%)
  Pallas kernels  18.5 us (23%)
  waiting for transfers between devices  15.5 us (19%)
  local copies, waits for them, and re-layouts  1.62 us (2%)
    all_to_all x1, blocking collectives, shards(): lax.all_to_all(found.reshape(LANGS * 4, ROWS, TOPK), AXES, 0, 0, axis_ind...  24 us
    all_to_all x1, waiting for transfers between devices, shards(): lax.all_to_all(outbox, 'lang', split_axis=0, concat_axis=0, tiled=True)  10.4 us
    all_to_all x1, starting transfers between devices, shards(): lax.all_to_all(outbox, 'lang', split_axis=0, concat_axis=0, tiled=True)  6.46 us
    pallas_call x1, Pallas kernels, late(): pl.pallas_call(late_kernel, out_shape=jax.ShapeDtypeStruct((LANGS, 4, ROW...  6.07 us
    ppermute x4, starting transfers between devices, shards(): lax.ppermute(part, AXES, moves(over))  6.02 us
    pallas_call x2, Pallas kernels, early(): pl.pallas_call(early_kernel, out_shape=jax.ShapeDtypeStruct((256, TOPK),...  5.06 us
    pallas_call x1, Pallas kernels, first(): pl.pallas_call(first_kernel, out_shape=(jax.ShapeDtypeStruct((256, TOPK),...  4.18 us
    ppermute x1, waiting for transfers between devices, shards(): cd1 = lax.ppermute(cy1, AXES, moves(over_x))  3.56 us
  transfers between devices with their start and end apart: 8, of which 4 were waited for; matrix products, arithmetic and copies ran while one was open for 0% of the time, Pallas kernels for 14%

profile of v5, /device:TPU:1, one launch (start us, length us, event | category | flops | bytes accessed | tf_op | source)
XLA Modules:
  0.0 79.4 jit_solution(12062220509443448265)
XLA Ops:
  0.0 3.3 %collective-permute-start.2 = (bf16[1024,768]{1,0:T(8,128)(2,1)}, bf16[1024,768]{1,0:T(8,128)(2,1)}, u32[]{:S(2)}, u32[]{:S(2)}) collective-permute-start(bf16[1024,768]{1,0:T(8,128)(2,1)} %own.1), channel_id=1, source_target_pairs={{0,1},{1,0},{2,3},{3,2},{4,5},{5,4},{6,7},{7,6},{8,11},{9,10},{10,... | collective-permute-start | bytes 4718600 | tf_op jit(solution)/shard_map/ppermute | solution.py:508
  3.3 0.0 copy-start
  3.3 0.9 %copy-done = bf16[128,768]{1,0:T(8,128)(2,1)S(1)} copy-done((bf16[128,768]{1,0:T(8,128)(2,1)S(1)}, bf16[128,768]{1,0:T(8,128)(2,1)}, u32[]{:S(2)}) %copy-start) | copy-done | bytes 196632
  4.2 0.0 copy-start.1
  4.2 0.7 copy-done.1
  4.9 0.0 copy-start.2
  4.9 1.6 %outbox.1 = (bf16[16,24,768]{2,1,0:T(8,128)(2,1)}, s32[1,128]{1,0:T(1,128)S(1)}) custom-call(bf16[128,768]{1,0:T(8,128)(2,1)S(1)} %copy-done, s32[1,128]{1,0:T(1,128)S(1)} %bitcast.6), custom_call_target="tpu_custom_call" | custom-call | tf_op jit(solution)/shard_map/outbox/pallas_call | solution.py:425
  6.4 6.5 %all-to-all-start = ((bf16[16,24,768]{2,1,0:T(8,128)(2,1)}), bf16[16,24,768]{2,1,0:T(8,128)(2,1)S(1)}, u32[]{:S(2)}, u32[]{:S(2)}) async-start(bf16[16,24,768]{2,1,0:T(8,128)(2,1)} %get-tuple-element.15), calls=%async_computation | async-start | bytes 1179648 | tf_op jit(solution)/shard_map/all_to_all | solution.py:510
  12.9 10.4 %all-to-all-done.chunk.mine = bf16[16,24,768]{2,1,0:T(8,128)(2,1)S(1)} async-done(((bf16[16,24,768]{2,1,0:T(8,128)(2,1)}), bf16[16,24,768]{2,1,0:T(8,128)(2,1)S(1)}, u32[]{:S(2)}, u32[]{:S(2)}) %all-to-all-start) | async-done | bytes 589856 | tf_op jit(solution)/shard_map/all_to_all | solution.py:510
  23.4 2.1 %collective-permute-start = (bf16[8,24,768]{2,1,0:T(8,128)(2,1)S(1)}, bf16[8,24,768]{2,1,0:T(8,128)(2,1)S(1)}, u32[]{:S(2)}, u32[]{:S(2)}) collective-permute-start(bf16[8,24,768]{2,1,0:T(8,128)(2,1)S(1)} %get-tuple-element.26), channel_id=1, source_target_pairs={{0,2},{1,3},{2,0},{3,1},{4,6},{5,7},{6,4},{7,5},{8,10},{9,11},{10,... | collective-permute-start | bytes 884744 | tf_op jit(solution)/shard_map/ppermute | solution.py:512
  25.5 2.6 %collective-permute-start.1 = (bf16[8,24,768]{2,1,0:T(8,128)(2,1)S(1)}, bf16[8,24,768]{2,1,0:T(8,128)(2,1)S(1)}, u32[]{:S(2)}, u32[]{:S(2)}) collective-permute-start(bf16[8,24,768]{2,1,0:T(8,128)(2,1)S(1)} %get-tuple-element.26), channel_id=1, source_target_pairs={{0,4},{1,5},{2,6},{3,7},{4,0},{5,1},{6,2},{7,3},{8,12},{9,13},{10,... | collective-permute-start | bytes 884744 | tf_op jit(solution)/shard_map/ppermute | solution.py:512
  28.1 0.9 %collective-permute-start.3 = (bf16[8,24,768]{2,1,0:T(8,128)(2,1)S(1)}, bf16[8,24,768]{2,1,0:T(8,128)(2,1)S(1)}, u32[]{:S(2)}, u32[]{:S(2)}) collective-permute-start(bf16[8,24,768]{2,1,0:T(8,128)(2,1)S(1)} %get-tuple-element.25), channel_id=1, source_target_pairs={{0,2},{1,3},{2,0},{3,1},{4,6},{5,7},{6,4},{7,5},{8,10},{9,11},{10,... | collective-permute-start | bytes 884744 | tf_op jit(solution)/shard_map/ppermute | solution.py:512
  29.0 0.3 collective-permute-start.4
  29.4 0.0 collective-permute-done.2.far
  29.4 0.0 copy-done.2
  29.4 4.2 %first.1 = (f32[256,128]{1,0:T(8,128)S(1)}, bf16[2,1024,768]{2,1,0:T(8,128)(2,1)S(1)}) custom-call(bf16[16,24,768]{2,1,0:T(8,128)(2,1)S(1)} %all-to-all-done.chunk.mine, bf16[1024,768]{1,0:T(8,128)(2,1)S(1)} %copy-done.2, bf16[1024,768]{1,0:T(8,128)(2,1)} %collective-permute-done.2.far), custom_call_target="tpu_custom_call" | custom-call | flops 6442450944 | bytes 1048576 | tf_op jit(solution)/shard_map/first/pallas_call | solution.py:353
  33.6 0.0 collective-permute-done.half0.cx0
  33.6 0.4 collective-permute-done.1.half1.cy0
  34.0 2.6 %collective-permute-start.5 = (bf16[8,24,768]{2,1,0:T(8,128)(2,1)S(1)}, bf16[8,24,768]{2,1,0:T(8,128)(2,1)S(1)}, u32[]{:S(2)}, u32[]{:S(2)}) collective-permute-start(bf16[8,24,768]{2,1,0:T(8,128)(2,1)S(1)} %collective-permute-done.half0.cx0), channel_id=1, source_target_pairs={{0,4},{1,5},{2,6},{3,7},{4,0},{5,1},{6,2},{7,3},{8,12},{9,13},{10,... | collective-permute-start | bytes 884744 | tf_op jit(solution)/shard_map/ppermute | solution.py:516
  36.6 2.5 %early.2.r1 = f32[256,128]{1,0:T(8,128)S(1)} custom-call(bf16[8,24,768]{2,1,0:T(8,128)(2,1)S(1)} %collective-permute-done.half0.cx0, bf16[8,24,768]{2,1,0:T(8,128)(2,1)S(1)} %collective-permute-done.1.half1.cy0, bf16[2,1024,768]{2,1,0:T(8,128)(2,1)S(1)} %get-tuple-element.19.both), custom_call_target="tpu_custom_call" | custom-call | flops 6442450944 | bytes 1048576 | tf_op jit(solution)/shard_map/early/pallas_call | solution.py:369
  39.1 0.0 collective-permute-done.3.half0.cx1
  39.2 1.2 %collective-permute-done.4.half1.cy1 = bf16[8,24,768]{2,1,0:T(8,128)(2,1)S(1)} collective-permute-done((bf16[8,24,768]{2,1,0:T(8,128)(2,1)S(1)}, bf16[8,24,768]{2,1,0:T(8,128)(2,1)S(1)}, u32[]{:S(2)}, u32[]{:S(2)}) %collective-permute-start.4) | collective-permute-done | bytes 294944 | tf_op jit(solution)/shard_map/ppermute | solution.py:512
  40.3 1.3 %collective-permute-start.6 = (bf16[8,24,768]{2,1,0:T(8,128)(2,1)S(1)}, bf16[8,24,768]{2,1,0:T(8,128)(2,1)S(1)}, u32[]{:S(2)}, u32[]{:S(2)}) collective-permute-start(bf16[8,24,768]{2,1,0:T(8,128)(2,1)S(1)} %collective-permute-done.4.half1.cy1), channel_id=1, source_target_pairs={{0,2},{1,3},{2,0},{3,1},{4,6},{5,7},{6,4},{7,5},{8,10},{9,11},{10,... | collective-permute-start | bytes 884744 | tf_op jit(solution)/shard_map/ppermute | solution.py:519
  41.6 2.5 %early.3.r2 = f32[256,128]{1,0:T(8,128)S(1)} custom-call(bf16[8,24,768]{2,1,0:T(8,128)(2,1)S(1)} %collective-permute-done.3.half0.cx1, bf16[8,24,768]{2,1,0:T(8,128)(2,1)S(1)} %collective-permute-done.4.half1.cy1, bf16[2,1024,768]{2,1,0:T(8,128)(2,1)S(1)} %get-tuple-element.19.both), custom_call_target="tpu_custom_call" | custom-call | flops 6442450944 | bytes 1048576 | tf_op jit(solution)/shard_map/early/pallas_call | solution.py:369
  44.1 3.6 %collective-permute-done.6.cd1 = bf16[8,24,768]{2,1,0:T(8,128)(2,1)S(1)} collective-permute-done((bf16[8,24,768]{2,1,0:T(8,128)(2,1)S(1)}, bf16[8,24,768]{2,1,0:T(8,128)(2,1)S(1)}, u32[]{:S(2)}, u32[]{:S(2)}) %collective-permute-start.6) | collective-permute-done | bytes 294944 | tf_op jit(solution)/shard_map/ppermute | solution.py:519
  47.7 0.0 collective-permute-done.5.cd0
  47.7 6.1 %late.1 = s16[16,4,24,128]{3,2,1,0:T(8,128)(2,1)S(1)} custom-call(s32[1]{0:T(128)} %bitcast.at, bf16[16,24,768]{2,1,0:T(8,128)(2,1)S(1)} %all-to-all-done.chunk.mine, bf16[8,24,768]{2,1,0:T(8,128)(2,1)S(1)} %collective-permute-done.half0.cx0, bf16[8,24,768]{2,1,0:T(8,128)(2,1)S(1)} %collective-permute-done.3.half0.cx1, ...), custom_call_target="tpu_custom_call" | custom-call | flops 12884901888 | bytes 1048576 | tf_op jit(solution)/shard_map/late/pallas_call | solution.py:382
  53.8 24.0 %all_to_all.10 = s16[64,24,128]{2,1,0:T(8,128)(2,1)S(1)} all-to-all(s16[64,24,128]{2,1,0:T(8,128)(2,1)S(1)} %bitcast.5), channel_id=1, replica_groups={{0,2,4,6,8,10,12,14,16,18,20,22,24,26,28,30,32,34,36,38,40,42,44,46,48,..., dimensions={0} | all-to-all | bytes 786432 | tf_op jit(solution)/shard_map/all_to_all | solution.py:524
  77.7 1.6 %join.1 = f32[128,128]{1,0:T(8,128)} custom-call(s16[16,4,24,128]{3,2,1,0:T(8,128)(2,1)S(1)} %bitcast.4, s32[1,128]{1,0:T(1,128)S(1)} %get-tuple-element.24.slots), custom_call_target="tpu_custom_call" | custom-call | tf_op jit(solution)/shard_map/join/pallas_call | solution.py:465
  (1 shorter events, 0.0 us)
Async XLA Ops:
  0.0 29.4 %collective-permute-start.2 = (bf16[1024,768]{1,0:T(8,128)(2,1)}, bf16[1024,768]{1,0:T(8,128)(2,1)}, u32[]{:S(2)}, u32[]{:S(2)}) collective-permute-start(bf16[1024,768]{1,0:T(8,128)(2,1)} %own.1), channel_id=1, source_target_pairs={{0,1},{1,0},{2,3},{3,2},{4,5},{5,4},{6,7},{7,6},{8,11},{9,10},{10,... | collective-permute-start | bytes 4718600 | tf_op jit(solution)/shard_map/ppermute | solution.py:508
  3.3 0.9 %copy-start = (bf16[128,768]{1,0:T(8,128)(2,1)S(1)}, bf16[128,768]{1,0:T(8,128)(2,1)}, u32[]{:S(2)}) copy-start(bf16[128,768]{1,0:T(8,128)(2,1)} %queries_in.1) | copy-start | bytes 589828
  4.2 0.7 copy-start.1
  4.9 24.5 %copy-start.2 = (bf16[1024,768]{1,0:T(8,128)(2,1)S(1)}, bf16[1024,768]{1,0:T(8,128)(2,1)}, u32[]{:S(2)}) copy-start(bf16[1024,768]{1,0:T(8,128)(2,1)} %own.1) | copy-start | bytes 4718596
  6.4 16.9 %all-to-all-start = ((bf16[16,24,768]{2,1,0:T(8,128)(2,1)}), bf16[16,24,768]{2,1,0:T(8,128)(2,1)S(1)}, u32[]{:S(2)}, u32[]{:S(2)}) async-start(bf16[16,24,768]{2,1,0:T(8,128)(2,1)} %get-tuple-element.15), calls=%async_computation | async-start | bytes 1179648 | tf_op jit(solution)/shard_map/all_to_all | solution.py:510
  23.4 10.2 %collective-permute-start = (bf16[8,24,768]{2,1,0:T(8,128)(2,1)S(1)}, bf16[8,24,768]{2,1,0:T(8,128)(2,1)S(1)}, u32[]{:S(2)}, u32[]{:S(2)}) collective-permute-start(bf16[8,24,768]{2,1,0:T(8,128)(2,1)S(1)} %get-tuple-element.26), channel_id=1, source_target_pairs={{0,2},{1,3},{2,0},{3,1},{4,6},{5,7},{6,4},{7,5},{8,10},{9,11},{10,... | collective-permute-start | bytes 884744 | tf_op jit(solution)/shard_map/ppermute | solution.py:512
  25.5 8.5 %collective-permute-start.1 = (bf16[8,24,768]{2,1,0:T(8,128)(2,1)S(1)}, bf16[8,24,768]{2,1,0:T(8,128)(2,1)S(1)}, u32[]{:S(2)}, u32[]{:S(2)}) collective-permute-start(bf16[8,24,768]{2,1,0:T(8,128)(2,1)S(1)} %get-tuple-element.26), channel_id=1, source_target_pairs={{0,4},{1,5},{2,6},{3,7},{4,0},{5,1},{6,2},{7,3},{8,12},{9,13},{10,... | collective-permute-start | bytes 884744 | tf_op jit(solution)/shard_map/ppermute | solution.py:512
  28.1 11.1 %collective-permute-start.3 = (bf16[8,24,768]{2,1,0:T(8,128)(2,1)S(1)}, bf16[8,24,768]{2,1,0:T(8,128)(2,1)S(1)}, u32[]{:S(2)}, u32[]{:S(2)}) collective-permute-start(bf16[8,24,768]{2,1,0:T(8,128)(2,1)S(1)} %get-tuple-element.25), channel_id=1, source_target_pairs={{0,2},{1,3},{2,0},{3,1},{4,6},{5,7},{6,4},{7,5},{8,10},{9,11},{10,... | collective-permute-start | bytes 884744 | tf_op jit(solution)/shard_map/ppermute | solution.py:512
  29.0 11.3 %collective-permute-start.4 = (bf16[8,24,768]{2,1,0:T(8,128)(2,1)S(1)}, bf16[8,24,768]{2,1,0:T(8,128)(2,1)S(1)}, u32[]{:S(2)}, u32[]{:S(2)}) collective-permute-start(bf16[8,24,768]{2,1,0:T(8,128)(2,1)S(1)} %get-tuple-element.25), channel_id=1, source_target_pairs={{0,4},{1,5},{2,6},{3,7},{4,0},{5,1},{6,2},{7,3},{8,12},{9,13},{10,... | collective-permute-start | bytes 884744 | tf_op jit(solution)/shard_map/ppermute | solution.py:512
  34.0 13.7 %collective-permute-start.5 = (bf16[8,24,768]{2,1,0:T(8,128)(2,1)S(1)}, bf16[8,24,768]{2,1,0:T(8,128)(2,1)S(1)}, u32[]{:S(2)}, u32[]{:S(2)}) collective-permute-start(bf16[8,24,768]{2,1,0:T(8,128)(2,1)S(1)} %collective-permute-done.half0.cx0), channel_id=1, source_target_pairs={{0,4},{1,5},{2,6},{3,7},{4,0},{5,1},{6,2},{7,3},{8,12},{9,13},{10,... | collective-permute-start | bytes 884744 | tf_op jit(solution)/shard_map/ppermute | solution.py:516
  40.3 7.4 %collective-permute-start.6 = (bf16[8,24,768]{2,1,0:T(8,128)(2,1)S(1)}, bf16[8,24,768]{2,1,0:T(8,128)(2,1)S(1)}, u32[]{:S(2)}, u32[]{:S(2)}) collective-permute-start(bf16[8,24,768]{2,1,0:T(8,128)(2,1)S(1)} %collective-permute-done.4.half1.cy1), channel_id=1, source_target_pairs={{0,2},{1,3},{2,0},{3,1},{4,6},{5,7},{6,4},{7,5},{8,10},{9,11},{10,... | collective-permute-start | bytes 884744 | tf_op jit(solution)/shard_map/ppermute | solution.py:519

commit v6 on v5

--- a/solution.py
+++ b/solution.py
@@ -15,6 +15,8 @@
 TAIL = CAP - MAIN
 Q = 128
 WIDTH = 768
+COLS = WIDTH // 128
+SENT = CAP * COLS
 
 epsilon = 1e-06
 
@@ -132,8 +134,12 @@
         (((1,), (1,)), ((), ())),
         preferred_element_type=jnp.float32,
     )
-    for half in range(2):
-        s[pl.ds(quarter * 2 + half, 256, stride=8), :] = part[:, half * 128 : (half + 1) * 128]
+    if rows.shape[0] == 256:
+        for half in range(2):
+            s[pl.ds(quarter * 2 + half, 256, stride=8), :] = part[:, half * 128 : (half + 1) * 128]
+    else:
+        for half in range(2):
+            s[pl.ds(quarter * 2 + half, 128, stride=8), :] = part[half * 128 : (half + 1) * 128, :]
 
 
 def score(corpus, rows, s):
@@ -141,11 +147,14 @@
         quarter_scores(corpus, rows, s, quarter)
 
 
-def order(s, u, dst):
-    loop(8, lambda i: sort32(s, i * 32))
-    loop(4, lambda i: merge64(s, i * 64, u))
-    loop(2, lambda i: merge128(u, i * 128, s))
-    merge_top(s, 0, s, 128, dst, 0)
+def order(blocks, s, u, dst):
+    loop(4 * blocks, lambda i: sort32(s, i * 32))
+    loop(2 * blocks, lambda i: merge64(s, i * 64, u))
+    if blocks == 1:
+        merge128(u, 0, dst)
+    else:
+        loop(2, lambda i: merge128(u, i * 128, s))
+        merge_top(s, 0, s, 128, dst, 0)
 
 
 def network(v, pairs):
@@ -179,11 +188,14 @@
     return v[31]
 
 
-def best64(src, dst):
+def best64(src, dst, turn=0):
+    def other(i):
+        return pltpu.roll(wire(src, 0, 63 - i), turn, 0) if turn else wire(src, 0, 127 - i)
+
     v = []
     for i in range(32):
-        a = jnp.maximum(wire(src, 0, i), wire(src, 0, 127 - i))
-        b = jnp.maximum(wire(src, 0, i + 32), wire(src, 0, 95 - i))
+        a = jnp.maximum(wire(src, 0, i), other(i))
+        b = jnp.maximum(wire(src, 0, i + 32), other(i + 32))
         v.append(jnp.maximum(a, b))
         put(dst, 32, i, jnp.minimum(a, b))
     v = clean(v)
@@ -210,51 +222,82 @@
 def leaders(groups, own, far, s, s2, u, w, emit):
     units = [(g, corpus) for g in range(len(groups)) for corpus in (own, far)]
     buffers = (s, s2)
-    score(own, groups[0](), s)
+    score(own, groups[0][1](), s)
     peak = None
     for k, (g, _) in enumerate(units):
+        blocks = groups[g][0]
         here = buffers[k % 2]
         ahead = units[k + 1] if k + 1 < len(units) else None
-        ahead_rows = groups[ahead[0]]() if ahead else None
-        base = (k % 2) * 128
+        ahead_rows = groups[ahead[0]][1]() if ahead else None
+        base = (k % 2) * 64 * blocks
         for i in range(4):
             if ahead:
                 quarter_scores(ahead[1], ahead_rows, buffers[(k + 1) % 2], i)
-            now = shorten(here, i * 64, u, base + i * 32)
-            peak = now if peak is None else jnp.maximum(peak, now)
+            if i < 2 * blocks:
+                now = shorten(here, i * 64, u, base + i * 32)
+                peak = now if peak is None else jnp.maximum(peak, now)
         if k % 2 == 0:
             continue
-        for i in range(4):
+        for i in range(2 * blocks):
             peak = jnp.maximum(peak, best32(u, i * 64, w, i * 32))
-        loop(2, lambda i: merge64(w, i * 64, u))
-        peak = jnp.maximum(peak, best64(u, w))
-        merge_turned(w, u, 4)
-        merge_top(u, 0, u, 0, w, 0, turn=2)
-        peak = jnp.maximum(peak, pltpu.roll(peak, 4, 0))
-        peak = jnp.maximum(peak, pltpu.roll(peak, 2, 0))
+        if blocks == 2:
+            loop(2, lambda i: merge64(w, i * 64, u))
+            peak = jnp.maximum(peak, best64(u, w))
+            turns = (4, 2)
+        else:
+            merge64(w, 0, u)
+            peak = jnp.maximum(peak, best64(u, w, turn=4))
+            turns = (2, 1)
+        merge_turned(w, u, turns[0])
+        merge_top(u, 0, u, 0, w, 0, turn=turns[1])
+        for turn in (4, 2, 1)[: 4 - blocks]:
+            peak = jnp.maximum(peak, pltpu.roll(peak, turn, 0))
         unsure = jnp.max(jnp.where(peak > wire(w, 127, 0), 1.0, 0.0)) > 0.0
         peak = None
 
         @pl.when(unsure)
         def _():
-            long_way(groups[g](), own, far, s2, u, w)
-
-        for half in range(2):
+            long_way(blocks, groups[g][1](), own, far, s if k + 1 == len(units) else s2, u, w)
+
+        for half in range(blocks):
             emit(g, half, w[pl.ds(half, TOPK, stride=8), :].T)
 
 
-def long_way(rows, own, far, s, u, w):
+def long_way(blocks, rows, own, far, s, u, w):
     score(own, rows, s)
-    order(s, u, w)
+    order(blocks, s, u, w)
     score(far, rows, s)
-    order(s, u, u)
-    merge_top(w, 0, u, 0, s, 0)
-    merge_top(s, 0, s, 0, u, 0, turn=4)
-    merge_top(u, 0, u, 0, w, 0, turn=2)
+    if blocks == 2:
+        order(blocks, s, u, u)
+        merge_top(w, 0, u, 0, s, 0)
+        merge_top(s, 0, s, 0, u, 0, turn=4)
+        merge_top(u, 0, u, 0, w, 0, turn=2)
+    else:
+        loop(4, lambda i: sort32(s, i * 32))
+        loop(2, lambda i: merge64(s, i * 64, u))
+        merge128(u, 0, s)
+        merge_top(w, 0, s, 0, u, 0)
+        merge_top(u, 0, u, 0, s, 0, turn=4)
+        merge_top(s, 0, s, 0, u, 0, turn=2)
+        merge_top(u, 0, u, 0, w, 0, turn=1)
 
 
 def main_rows(chunk):
-    return chunk[:, 0:MAIN, :].reshape(-1, WIDTH)
+    return jnp.concatenate(
+        [chunk[:, c * MAIN : (c + 1) * MAIN, :].reshape(-1, 128) for c in range(COLS)], axis=1
+    )
+
+
+def tail_rows(chunk):
+    langs = chunk.shape[0]
+    many, each = langs * TAIL, TAIL * COLS
+    shape, total = (COLS, many, langs * each), langs * each
+    col, row, at = (lax.broadcasted_iota(jnp.int32, shape, d) for d in range(3))
+    from_row = lax.shift_right_logical(row, 2) * each + col * TAIL + (row & 3)
+    picks = jnp.where(at == from_row, 1.0, 0.0).astype(jnp.bfloat16).reshape(total, total)
+    flat = chunk[:, MAIN * COLS : SENT, :].reshape(total, 128)
+    found = jnp.dot(picks, flat, preferred_element_type=jnp.float32).astype(jnp.bfloat16)
+    return jnp.concatenate([found[c * many : (c + 1) * many, :] for c in range(COLS)], axis=1)
 
 
 def first_kernel(chunk, own, far, out, both, rows, *work):
@@ -265,7 +308,7 @@
     def emit(g, half, value):
         out[half * Q : (half + 1) * Q, :] = value
 
-    leaders([lambda: rows[...]], own, far, *work, emit)
+    leaders([(2, lambda: rows[...])], own, far, *work, emit)
 
 
 def early_kernel(half0, half1, both, out, rows, *work):
@@ -275,7 +318,23 @@
     def emit(g, half, value):
         out[half * Q : (half + 1) * Q, :] = value
 
-    leaders([lambda: rows[...]], both.at[0], both.at[1], *work, emit)
+    leaders([(2, lambda: rows[...])], both.at[0], both.at[1], *work, emit)
+
+
+def middle_kernel(mine, cx0, cx1, cy0, cy1, both, out, tails, rows, *work):
+    rows[0:128, :] = main_rows(cx1)
+    rows[128:256, :] = main_rows(cy1)
+    rows[256:320, :] = tail_rows(mine)
+    for k, chunk in enumerate((cx0, cx1, cy0, cy1)):
+        rows[320 + k * 32 : 352 + k * 32, :] = tail_rows(chunk)
+    rows[448:512, :] = jnp.zeros((64, WIDTH), jnp.bfloat16)
+
+    def emit(g, half, value):
+        (out, tails)[g][half * Q : (half + 1) * Q, :] = value
+
+    leaders(
+        [(2, lambda: rows[0:256, :]), (2, lambda: rows[256:512, :])], both.at[0], both.at[1], *work, emit
+    )
 
 
 STEPS = 800.0
@@ -295,28 +354,18 @@
     return jnp.where(c < 0, -v, v)
 
 
-def late_kernel(at, mine, cx0, cx1, cy0, cy1, cd0, cd1, both, r0, r1, r2, out, *scratch):
-    rows, tails, box, *work = scratch
+def late_kernel(at, cd0, cd1, both, r0, r1, r2, tails, out, rows, last, box, *work):
     rows[0:128, :] = main_rows(cd0)
     rows[128:256, :] = main_rows(cd1)
-    slot = lax.broadcasted_iota(jnp.int32, (64, LANGS * ROWS), 1)
-    row = lax.broadcasted_iota(jnp.int32, (64, LANGS * ROWS), 0)
-    picks = (slot == row // TAIL * ROWS + MAIN + row % TAIL).astype(jnp.float32).astype(jnp.bfloat16)
-    half_picks = picks[0:32, 0 : 8 * ROWS]
-
-    def tail_of(chunk, sel):
-        flat = chunk[...].reshape(-1, WIDTH)
-        return jnp.dot(sel, flat, preferred_element_type=jnp.float32).astype(jnp.bfloat16)
-
-    rows[256:320, :] = tail_of(mine, picks)
-    for k, chunk in enumerate((cx0, cx1, cy0, cy1, cd0, cd1)):
-        rows[320 + k * 32 : 352 + k * 32, :] = tail_of(chunk, half_picks)
+    rows[256:288, :] = tail_rows(cd0)
+    rows[288:320, :] = tail_rows(cd1)
+    rows[320:384, :] = jnp.zeros((64, WIDTH), jnp.bfloat16)
 
     def emit(g, half, value):
-        tails[g, half] = value
+        last[g * 256 + half * Q : g * 256 + (half + 1) * Q, :] = value
 
     leaders(
-        [lambda: rows[0:256, :], lambda: rows[256:512, :]], both.at[0], both.at[1], *work, emit
+        [(2, lambda: rows[0:256, :]), (1, lambda: rows[256:384, :])], both.at[0], both.at[1], *work, emit
     )
     me = at[0]
     owner = (me, me ^ 1, me ^ 2, me ^ 3)
@@ -330,10 +379,13 @@
                 start += (k - 1) * Q
                 main = (r1, r2)[half][start : start + MAIN, :]
             else:
-                main = tails[0, half, start : start + MAIN, :]
+                main = last[lang * MAIN : (lang + 1) * MAIN, :]
             box[k, 0:MAIN, :] = main
-            start = k % 2 * 64 + lang * TAIL
-            box[k, MAIN:CAP, :] = tails[1, k // 2, start : start + TAIL, :]
+            start = k * 64 + lang * TAIL
+            if k < 3:
+                box[k, MAIN:CAP, :] = tails[start : start + TAIL, :]
+            else:
+                box[k, MAIN:CAP, :] = last[256 + lang * TAIL : 256 + (lang + 1) * TAIL, :]
             box[k, CAP:ROWS, :] = none
             out[lang, owner[k]] = coded(box[k]).astype(jnp.int32).astype(jnp.int16)
 
@@ -378,22 +430,35 @@
     )(half0, half1, both)
 
 
-def late(at, chunks, both, results):
+def middle(mine, halves, both):
+    return pl.pallas_call(
+        middle_kernel,
+        out_shape=[jax.ShapeDtypeStruct((256, TOPK), jnp.float32)] * 2,
+        in_specs=[VMEM] * 6,
+        out_specs=[VMEM] * 2,
+        scratch_shapes=[pltpu.VMEM((512, WIDTH), jnp.bfloat16)] + WORK,
+        compiler_params=LIMIT,
+        cost_estimate=pl.CostEstimate(flops=COST * 2, bytes_accessed=1 << 20, transcendentals=0),
+        name="middle",
+    )(mine, *halves, both)
+
+
+def late(at, halves, both, results):
     return pl.pallas_call(
         late_kernel,
         out_shape=jax.ShapeDtypeStruct((LANGS, 4, ROWS, TOPK), jnp.int16),
-        in_specs=[pl.BlockSpec(memory_space=pltpu.SMEM)] + [VMEM] * 11,
+        in_specs=[pl.BlockSpec(memory_space=pltpu.SMEM)] + [VMEM] * 7,
         out_specs=VMEM,
         scratch_shapes=[
-            pltpu.VMEM((512, WIDTH), jnp.bfloat16),
-            pltpu.VMEM((2, 2, Q, TOPK), jnp.float32),
+            pltpu.VMEM((384, WIDTH), jnp.bfloat16),
+            pltpu.VMEM((384, TOPK), jnp.float32),
             pltpu.VMEM((4, ROWS, TOPK), jnp.float32),
         ]
         + WORK,
         compiler_params=LIMIT,
         cost_estimate=pl.CostEstimate(flops=COST * 2, bytes_accessed=1 << 20, transcendentals=0),
         name="late",
-    )(at, *chunks, both, *results)
+    )(at, *halves, both, *results)
 
 
 def outbox_kernel(queries_in, routes_in, out, slots, queries, routes, sems):
@@ -411,21 +476,33 @@
     down = along.T
     before = lax.broadcasted_iota(jnp.int32, (Q, Q), 0) < lax.broadcasted_iota(jnp.int32, (Q, Q), 1)
     earlier = jnp.where(before & (along == down), 1.0, 0.0)
-    rank = jnp.sum(earlier, axis=0, keepdims=True)
-    place = routes[...] * ROWS + rank.astype(jnp.int32)
-    slots[...] = place
-    total = LANGS * ROWS
-    hits = lax.broadcasted_iota(jnp.int32, (total, Q), 0) == jnp.broadcast_to(place, (total, Q))
+    rank = jnp.sum(earlier, axis=0, keepdims=True).astype(jnp.int32)
+    lang = routes[...]
+    slots[...] = lang * ROWS + rank
+    main_at = jnp.where(rank < MAIN, lang * MAIN + rank, -1)
+    hits = lax.broadcasted_iota(jnp.int32, (LANGS * MAIN, Q), 0) == jnp.broadcast_to(main_at, (LANGS * MAIN, Q))
     picks = jnp.where(hits, 1.0, 0.0).astype(jnp.bfloat16)
     box = jnp.dot(picks, unit, preferred_element_type=jnp.float32).astype(jnp.bfloat16)
-    out[...] = box.reshape(LANGS, ROWS, WIDTH)
+    for c in range(COLS):
+        out[:, c * MAIN : (c + 1) * MAIN, :] = box[:, c * 128 : (c + 1) * 128].reshape(LANGS, MAIN, 128)
+    each = TAIL * COLS
+    tail_at = jnp.where(rank < MAIN, -1, lang * TAIL + rank - MAIN)
+    shape = (LANGS, each, Q)
+    of_lang, row = (lax.broadcasted_iota(jnp.int32, shape, d) for d in range(2))
+    hits = of_lang * TAIL + (row & 3) == jnp.broadcast_to(tail_at.reshape(1, 1, Q), shape)
+    tail = jnp.zeros((LANGS * each, 128), jnp.float32)
+    for c in range(COLS):
+        picks = jnp.where(hits & (lax.shift_right_logical(row, 2) == c), 1.0, 0.0)
+        picks = picks.astype(jnp.bfloat16).reshape(LANGS * each, Q)
+        tail = tail + jnp.dot(picks, unit[:, c * 128 : (c + 1) * 128], preferred_element_type=jnp.float32)
+    out[:, MAIN * COLS : SENT, :] = tail.astype(jnp.bfloat16).reshape(LANGS, each, 128)
 
 
 def outbox_of(queries, routes):
     return pl.pallas_call(
         outbox_kernel,
         out_shape=(
-            jax.ShapeDtypeStruct((LANGS, ROWS, WIDTH), jnp.bfloat16),
+            jax.ShapeDtypeStruct((LANGS, SENT, 128), jnp.bfloat16),
             jax.ShapeDtypeStruct((1, Q), jnp.int32),
         ),
         in_specs=[pl.BlockSpec(memory_space=pltpu.HBM)] * 2,
@@ -517,10 +594,10 @@
     r1 = early(cx0, cy0, both)
     cx1, cy1, r1 = lax.optimization_barrier((cx1, cy1, r1))
     cd1 = lax.ppermute(cy1, AXES, moves(over_x))
-    r2 = early(cx1, cy1, both)
+    r2, tails = middle(mine, (cx0, cx1, cy0, cy1), both)
     shard = lax.axis_index("shard")
     at = (lax.shift_right_logical(shard, 2) * 2 + (lax.shift_right_logical(shard, 1) & 1)).reshape(1)
-    found = late(at, (mine, cx0, cx1, cy0, cy1, cd0, cd1), both, (r0, r1, r2))
+    found = late(at, (cd0, cd1), both, (r0, r1, r2, tails))
     back = lax.all_to_all(
         found.reshape(LANGS * 4, ROWS, TOPK), AXES, 0, 0, axis_index_groups=TEAMS, tiled=True
     )

time: 79.7 us -> 74.4 us (0.934)
  waiting for transfers between devices: 15.5 us -> 9.33 us
  blocking collectives: 24 us -> 21.9 us
  Pallas kernels: 18.5 us -> 20.3 us
  starting transfers between devices: 19.7 us -> 20.8 us
    pallas_call x1 -> x2, Pallas kernels: 1.55 us -> 6.87 us  [the longest x1 5.25 us: middle(): pl.pallas_call(middle_kernel, out_shape=[jax.ShapeDtypeStruct((256, TOPK)...]
    ppermute x1, waiting for transfers between devices: 3.56 us -> 0.01 us  [shards(): cd1 = lax.ppermute(cy1, AXES, moves(over_x))]
    pallas_call x2 -> x1, Pallas kernels: 5.06 us -> 2.53 us  [early(): pl.pallas_call(early_kernel, out_shape=jax.ShapeDtypeStruct((256, TOPK),...]
    all_to_all x1, blocking collectives: 24 us -> 21.9 us  [shards(): lax.all_to_all(found.reshape(LANGS * 4, ROWS, TOPK), AXES, 0, 0, axis_ind...]
    ppermute x4, waiting for transfers between devices: 1.56 us -> 0.01 us  [shards(): lax.ppermute(part, AXES, moves(over))]
    all_to_all x1, waiting for transfers between devices: 10.4 us -> 9.31 us  [shards(): lax.all_to_all(outbox, 'lang', split_axis=0, concat_axis=0, tiled=True)]
    ppermute x1, starting transfers between devices: 1.28 us -> 2.28 us  [shards(): cd1 = lax.ppermute(cy1, AXES, moves(over_x))]
    pallas_call x1, Pallas kernels: 6.07 us -> 5.12 us  [late(): pl.pallas_call(late_kernel, out_shape=jax.ShapeDtypeStruct((LANGS, 4, ROW...]
  transfers between devices with their start and end apart: 8 -> 8, of which waited for: 4 -> 1; matrix products, arithmetic and copies ran while one was open for 0% -> 0% of each run, Pallas kernels for 14% -> 18%
where the time goes in v6:
time: 74.4 us; the launch traced here: 74.1 us
  blocking collectives  21.9 us (29%)
  starting transfers between devices  20.8 us (28%)
  Pallas kernels  20.3 us (27%)
  waiting for transfers between devices  9.33 us (13%)
  local copies, waits for them, and re-layouts  1.62 us (2%)
    all_to_all x1, blocking collectives, shards(): lax.all_to_all(found.reshape(LANGS * 4, ROWS, TOPK), AXES, 0, 0, axis_ind...  21.9 us
    all_to_all x1, waiting for transfers between devices, shards(): lax.all_to_all(outbox, 'lang', split_axis=0, concat_axis=0, tiled=True)  9.31 us
    all_to_all x1, starting transfers between devices, shards(): lax.all_to_all(outbox, 'lang', split_axis=0, concat_axis=0, tiled=True)  6.47 us
    ppermute x4, starting transfers between devices, shards(): lax.ppermute(part, AXES, moves(over))  6.02 us
    pallas_call x1, Pallas kernels, middle(): pl.pallas_call(middle_kernel, out_shape=[jax.ShapeDtypeStruct((256, TOPK)...  5.25 us
    pallas_call x1, Pallas kernels, late(): pl.pallas_call(late_kernel, out_shape=jax.ShapeDtypeStruct((LANGS, 4, ROW...  5.12 us
    pallas_call x1, Pallas kernels, first(): pl.pallas_call(first_kernel, out_shape=(jax.ShapeDtypeStruct((256, TOPK),...  4.18 us
    ppermute x1, starting transfers between devices, shards(): far = lax.ppermute(corpus, AXES, moves(pair))  3.3 us
  transfers between devices with their start and end apart: 8, of which 1 were waited for; matrix products, arithmetic and copies ran while one was open for 0% of the time, Pallas kernels for 18%

profile of v6, /device:TPU:1, one launch (start us, length us, event | category | flops | bytes accessed | tf_op | source)
XLA Modules:
  0.0 74.1 jit_solution(4528110619031072337)
XLA Ops:
  0.0 3.3 %collective-permute-start.2 = (bf16[1024,768]{1,0:T(8,128)(2,1)}, bf16[1024,768]{1,0:T(8,128)(2,1)}, u32[]{:S(2)}, u32[]{:S(2)}) collective-permute-start(bf16[1024,768]{1,0:T(8,128)(2,1)} %own.1), channel_id=1, source_target_pairs={{0,1},{1,0},{2,3},{3,2},{4,5},{5,4},{6,7},{7,6},{8,11},{9,10},{10,... | collective-permute-start | bytes 4718600 | tf_op jit(solution)/shard_map/ppermute | solution.py:585
  3.3 0.0 copy-start
  3.3 0.9 %copy-done = bf16[128,768]{1,0:T(8,128)(2,1)S(1)} copy-done((bf16[128,768]{1,0:T(8,128)(2,1)S(1)}, bf16[128,768]{1,0:T(8,128)(2,1)}, u32[]{:S(2)}) %copy-start) | copy-done | bytes 196632
  4.2 0.0 copy-start.1
  4.2 0.7 copy-done.1
  4.9 0.0 copy-start.2
  4.9 1.6 %outbox.1 = (bf16[16,120,128]{2,1,0:T(8,128)(2,1)}, s32[1,128]{1,0:T(1,128)S(1)}) custom-call(bf16[128,768]{1,0:T(8,128)(2,1)S(1)} %copy-done, s32[1,128]{1,0:T(1,128)S(1)} %bitcast.6), custom_call_target="tpu_custom_call" | custom-call | tf_op jit(solution)/shard_map/outbox/pallas_call | solution.py:502
  6.5 6.5 %all-to-all-start = ((bf16[16,120,128]{2,1,0:T(8,128)(2,1)}), bf16[16,120,128]{2,1,0:T(8,128)(2,1)S(1)}, u32[]{:S(2)}, u32[]{:S(2)}) async-start(bf16[16,120,128]{2,1,0:T(8,128)(2,1)} %get-tuple-element.17), calls=%async_computation | async-start | bytes 983040 | tf_op jit(solution)/shard_map/all_to_all | solution.py:587
  13.0 9.3 %all-to-all-done.chunk.mine = bf16[16,120,128]{2,1,0:T(8,128)(2,1)S(1)} async-done(((bf16[16,120,128]{2,1,0:T(8,128)(2,1)}), bf16[16,120,128]{2,1,0:T(8,128)(2,1)S(1)}, u32[]{:S(2)}, u32[]{:S(2)}) %all-to-all-start) | async-done | bytes 491552 | tf_op jit(solution)/shard_map/all_to_all | solution.py:587
  22.3 2.1 %collective-permute-start = (bf16[8,120,128]{2,1,0:T(8,128)(2,1)S(1)}, bf16[8,120,128]{2,1,0:T(8,128)(2,1)S(1)}, u32[]{:S(2)}, u32[]{:S(2)}) collective-permute-start(bf16[8,120,128]{2,1,0:T(8,128)(2,1)S(1)} %get-tuple-element.30), channel_id=1, source_target_pairs={{0,2},{1,3},{2,0},{3,1},{4,6},{5,7},{6,4},{7,5},{8,10},{9,11},{10,... | collective-permute-start | bytes 737288 | tf_op jit(solution)/shard_map/ppermute | solution.py:589
  24.4 2.6 %collective-permute-start.1 = (bf16[8,120,128]{2,1,0:T(8,128)(2,1)S(1)}, bf16[8,120,128]{2,1,0:T(8,128)(2,1)S(1)}, u32[]{:S(2)}, u32[]{:S(2)}) collective-permute-start(bf16[8,120,128]{2,1,0:T(8,128)(2,1)S(1)} %get-tuple-element.30), channel_id=1, source_target_pairs={{0,4},{1,5},{2,6},{3,7},{4,0},{5,1},{6,2},{7,3},{8,12},{9,13},{10,... | collective-permute-start | bytes 737288 | tf_op jit(solution)/shard_map/ppermute | solution.py:589
  27.1 0.9 %collective-permute-start.4 = (bf16[8,120,128]{2,1,0:T(8,128)(2,1)S(1)}, bf16[8,120,128]{2,1,0:T(8,128)(2,1)S(1)}, u32[]{:S(2)}, u32[]{:S(2)}) collective-permute-start(bf16[8,120,128]{2,1,0:T(8,128)(2,1)S(1)} %get-tuple-element.29), channel_id=1, source_target_pairs={{0,2},{1,3},{2,0},{3,1},{4,6},{5,7},{6,4},{7,5},{8,10},{9,11},{10,... | collective-permute-start | bytes 737288 | tf_op jit(solution)/shard_map/ppermute | solution.py:589
  28.0 0.3 collective-permute-start.5
  28.3 0.0 collective-permute-done.2.far
  28.4 0.0 copy-done.2
  28.4 4.2 %first.1 = (f32[256,128]{1,0:T(8,128)S(1)}, bf16[2,1024,768]{2,1,0:T(8,128)(2,1)S(1)}) custom-call(bf16[16,120,128]{2,1,0:T(8,128)(2,1)S(1)} %all-to-all-done.chunk.mine, bf16[1024,768]{1,0:T(8,128)(2,1)S(1)} %copy-done.2, bf16[1024,768]{1,0:T(8,128)(2,1)} %collective-permute-done.2.far), custom_call_target="tpu_custom_call" | custom-call | flops 6442450944 | bytes 1048576 | tf_op jit(solution)/shard_map/first/pallas_call | solution.py:405
  32.5 0.0 collective-permute-done.half0.cx0
  32.5 0.0 collective-permute-done.1.half1.cy0
  32.6 2.7 %collective-permute-start.3 = (bf16[8,120,128]{2,1,0:T(8,128)(2,1)S(1)}, bf16[8,120,128]{2,1,0:T(8,128)(2,1)S(1)}, u32[]{:S(2)}, u32[]{:S(2)}) collective-permute-start(bf16[8,120,128]{2,1,0:T(8,128)(2,1)S(1)} %collective-permute-done.half0.cx0), channel_id=1, source_target_pairs={{0,4},{1,5},{2,6},{3,7},{4,0},{5,1},{6,2},{7,3},{8,12},{9,13},{10,... | collective-permute-start | bytes 737288 | tf_op jit(solution)/shard_map/ppermute | solution.py:593
  35.3 2.5 %early.1.r1 = f32[256,128]{1,0:T(8,128)S(1)} custom-call(bf16[8,120,128]{2,1,0:T(8,128)(2,1)S(1)} %collective-permute-done.half0.cx0, bf16[8,120,128]{2,1,0:T(8,128)(2,1)S(1)} %collective-permute-done.1.half1.cy0, bf16[2,1024,768]{2,1,0:T(8,128)(2,1)S(1)} %get-tuple-element.21.both), custom_call_target="tpu_custom_call" | custom-call | flops 6442450944 | bytes 1048576 | tf_op jit(solution)/shard_map/early/pallas_call | solution.py:421
  37.8 0.0 collective-permute-done.4.cx1
  37.8 0.0 collective-permute-done.5.cy1
  37.8 2.3 %collective-permute-start.6 = (bf16[8,120,128]{2,1,0:T(8,128)(2,1)S(1)}, bf16[8,120,128]{2,1,0:T(8,128)(2,1)S(1)}, u32[]{:S(2)}, u32[]{:S(2)}) collective-permute-start(bf16[8,120,128]{2,1,0:T(8,128)(2,1)S(1)} %collective-permute-done.5.cy1), channel_id=1, source_target_pairs={{0,2},{1,3},{2,0},{3,1},{4,6},{5,7},{6,4},{7,5},{8,10},{9,11},{10,... | collective-permute-start | bytes 737288 | tf_op jit(solution)/shard_map/ppermute | solution.py:596
  40.1 5.3 %middle.1 = (f32[256,128]{1,0:T(8,128)S(1)}, f32[256,128]{1,0:T(8,128)S(1)}) custom-call(bf16[16,120,128]{2,1,0:T(8,128)(2,1)S(1)} %all-to-all-done.chunk.mine, bf16[8,120,128]{2,1,0:T(8,128)(2,1)S(1)} %collective-permute-done.half0.cx0, bf16[8,120,128]{2,1,0:T(8,128)(2,1)S(1)} %collective-permute-done.4.cx1, ...), custom_call_target="tpu_custom_call" | custom-call | flops 12884901888 | bytes 1048576 | tf_op jit(solution)/shard_map/middle/pallas_call | solution.py:434
  45.4 0.0 collective-permute-done.6.cd1
  45.4 0.0 collective-permute-done.3.cd0
  45.4 5.1 %late.1 = s16[16,4,24,128]{3,2,1,0:T(8,128)(2,1)S(1)} custom-call(s32[1]{0:T(128)} %bitcast.at, bf16[8,120,128]{2,1,0:T(8,128)(2,1)S(1)} %collective-permute-done.3.cd0, bf16[8,120,128]{2,1,0:T(8,128)(2,1)S(1)} %collective-permute-done.6.cd1, bf16[2,1024,768]{2,1,0:T(8,128)(2,1)S(1)} %get-tuple-element.21.both, f32[256,128]{1,0:T(8,128)S(1)} %get-tuple-element.23.r0, ...), custom_call_target="tpu_custom_call" | custom-call | flops 12884901888 | bytes 1048576 | tf_op jit(solution)/shard_map/late/pallas_call | solution.py:447
  50.5 21.9 %all_to_all.10 = s16[64,24,128]{2,1,0:T(8,128)(2,1)S(1)} all-to-all(s16[64,24,128]{2,1,0:T(8,128)(2,1)S(1)} %bitcast.5), channel_id=1, replica_groups={{0,2,4,6,8,10,12,14,16,18,20,22,24,26,28,30,32,34,36,38,40,42,44,46,48,..., dimensions={0} | all-to-all | bytes 786432 | tf_op jit(solution)/shard_map/all_to_all | solution.py:601
  72.4 1.6 %join.1 = f32[128,128]{1,0:T(8,128)} custom-call(s16[16,4,24,128]{3,2,1,0:T(8,128)(2,1)S(1)} %bitcast.4, s32[1,128]{1,0:T(1,128)S(1)} %get-tuple-element.28.slots), custom_call_target="tpu_custom_call" | custom-call | tf_op jit(solution)/shard_map/join/pallas_call | solution.py:542
  (1 shorter events, 0.0 us)
Async XLA Ops:
  0.0 28.3 %collective-permute-start.2 = (bf16[1024,768]{1,0:T(8,128)(2,1)}, bf16[1024,768]{1,0:T(8,128)(2,1)}, u32[]{:S(2)}, u32[]{:S(2)}) collective-permute-start(bf16[1024,768]{1,0:T(8,128)(2,1)} %own.1), channel_id=1, source_target_pairs={{0,1},{1,0},{2,3},{3,2},{4,5},{5,4},{6,7},{7,6},{8,11},{9,10},{10,... | collective-permute-start | bytes 4718600 | tf_op jit(solution)/shard_map/ppermute | solution.py:585
  3.3 0.9 %copy-start = (bf16[128,768]{1,0:T(8,128)(2,1)S(1)}, bf16[128,768]{1,0:T(8,128)(2,1)}, u32[]{:S(2)}) copy-start(bf16[128,768]{1,0:T(8,128)(2,1)} %queries_in.1) | copy-start | bytes 589828
  4.2 0.7 copy-start.1
  4.9 23.5 %copy-start.2 = (bf16[1024,768]{1,0:T(8,128)(2,1)S(1)}, bf16[1024,768]{1,0:T(8,128)(2,1)}, u32[]{:S(2)}) copy-start(bf16[1024,768]{1,0:T(8,128)(2,1)} %own.1) | copy-start | bytes 4718596
  6.5 15.8 %all-to-all-start = ((bf16[16,120,128]{2,1,0:T(8,128)(2,1)}), bf16[16,120,128]{2,1,0:T(8,128)(2,1)S(1)}, u32[]{:S(2)}, u32[]{:S(2)}) async-start(bf16[16,120,128]{2,1,0:T(8,128)(2,1)} %get-tuple-element.17), calls=%async_computation | async-start | bytes 983040 | tf_op jit(solution)/shard_map/all_to_all | solution.py:587
  22.3 10.2 %collective-permute-start = (bf16[8,120,128]{2,1,0:T(8,128)(2,1)S(1)}, bf16[8,120,128]{2,1,0:T(8,128)(2,1)S(1)}, u32[]{:S(2)}, u32[]{:S(2)}) collective-permute-start(bf16[8,120,128]{2,1,0:T(8,128)(2,1)S(1)} %get-tuple-element.30), channel_id=1, source_target_pairs={{0,2},{1,3},{2,0},{3,1},{4,6},{5,7},{6,4},{7,5},{8,10},{9,11},{10,... | collective-permute-start | bytes 737288 | tf_op jit(solution)/shard_map/ppermute | solution.py:589
  24.4 8.1 %collective-permute-start.1 = (bf16[8,120,128]{2,1,0:T(8,128)(2,1)S(1)}, bf16[8,120,128]{2,1,0:T(8,128)(2,1)S(1)}, u32[]{:S(2)}, u32[]{:S(2)}) collective-permute-start(bf16[8,120,128]{2,1,0:T(8,128)(2,1)S(1)} %get-tuple-element.30), channel_id=1, source_target_pairs={{0,4},{1,5},{2,6},{3,7},{4,0},{5,1},{6,2},{7,3},{8,12},{9,13},{10,... | collective-permute-start | bytes 737288 | tf_op jit(solution)/shard_map/ppermute | solution.py:589
  27.1 10.7 %collective-permute-start.4 = (bf16[8,120,128]{2,1,0:T(8,128)(2,1)S(1)}, bf16[8,120,128]{2,1,0:T(8,128)(2,1)S(1)}, u32[]{:S(2)}, u32[]{:S(2)}) collective-permute-start(bf16[8,120,128]{2,1,0:T(8,128)(2,1)S(1)} %get-tuple-element.29), channel_id=1, source_target_pairs={{0,2},{1,3},{2,0},{3,1},{4,6},{5,7},{6,4},{7,5},{8,10},{9,11},{10,... | collective-permute-start | bytes 737288 | tf_op jit(solution)/shard_map/ppermute | solution.py:589
  28.0 9.8 %collective-permute-start.5 = (bf16[8,120,128]{2,1,0:T(8,128)(2,1)S(1)}, bf16[8,120,128]{2,1,0:T(8,128)(2,1)S(1)}, u32[]{:S(2)}, u32[]{:S(2)}) collective-permute-start(bf16[8,120,128]{2,1,0:T(8,128)(2,1)S(1)} %get-tuple-element.29), channel_id=1, source_target_pairs={{0,4},{1,5},{2,6},{3,7},{4,0},{5,1},{6,2},{7,3},{8,12},{9,13},{10,... | collective-permute-start | bytes 737288 | tf_op jit(solution)/shard_map/ppermute | solution.py:589
  32.6 12.8 %collective-permute-start.3 = (bf16[8,120,128]{2,1,0:T(8,128)(2,1)S(1)}, bf16[8,120,128]{2,1,0:T(8,128)(2,1)S(1)}, u32[]{:S(2)}, u32[]{:S(2)}) collective-permute-start(bf16[8,120,128]{2,1,0:T(8,128)(2,1)S(1)} %collective-permute-done.half0.cx0), channel_id=1, source_target_pairs={{0,4},{1,5},{2,6},{3,7},{4,0},{5,1},{6,2},{7,3},{8,12},{9,13},{10,... | collective-permute-start | bytes 737288 | tf_op jit(solution)/shard_map/ppermute | solution.py:593
  37.8 7.5 %collective-permute-start.6 = (bf16[8,120,128]{2,1,0:T(8,128)(2,1)S(1)}, bf16[8,120,128]{2,1,0:T(8,128)(2,1)S(1)}, u32[]{:S(2)}, u32[]{:S(2)}) collective-permute-start(bf16[8,120,128]{2,1,0:T(8,128)(2,1)S(1)} %collective-permute-done.5.cy1), channel_id=1, source_target_pairs={{0,2},{1,3},{2,0},{3,1},{4,6},{5,7},{6,4},{7,5},{8,10},{9,11},{10,... | collective-permute-start | bytes 737288 | tf_op jit(solution)/shard_map/ppermute | solution.py:596

commit v7 on v6

--- a/solution.py
+++ b/solution.py
@@ -38,6 +38,7 @@
 
 SORT32 = batcher(32)
 SORT16 = batcher(16)
+AHEAD = 2
 
 
 def wire(ref, base, i):
@@ -127,24 +128,26 @@
     lax.fori_loop(0, n, step, 0)
 
 
-def quarter_scores(corpus, rows, s, quarter):
-    part = lax.dot_general(
-        corpus[quarter * 256 : (quarter + 1) * 256, :],
+def wires_of(corpus, rows, parts, i, whole=False):
+    blocks = rows.shape[0] // 128
+    apart, nth, kind = (256, i, 0) if blocks == 2 else (128, i // 2, i % 2 * 4)
+    starts = [(kind + k) * apart + nth * 64 for k in range(4)]
+    scores = lax.dot_general(
+        jnp.concatenate([corpus[at : at + 64, :] for at in starts], axis=0),
         rows,
         (((1,), (1,)), ((), ())),
         preferred_element_type=jnp.float32,
     )
-    if rows.shape[0] == 256:
-        for half in range(2):
-            s[pl.ds(quarter * 2 + half, 256, stride=8), :] = part[:, half * 128 : (half + 1) * 128]
-    else:
-        for half in range(2):
-            s[pl.ds(quarter * 2 + half, 128, stride=8), :] = part[half * 128 : (half + 1) * 128, :]
+    ref, at = (parts, nth * 512) if whole else (parts[nth], 0)
+    for k in range(4):
+        for half in range(blocks):
+            place = pl.ds(at + (kind + k) * blocks + half, 64, stride=8)
+            ref[place, :] = scores[k * 64 : (k + 1) * 64, half * 128 : (half + 1) * 128]
 
 
 def score(corpus, rows, s):
-    for quarter in range(4):
-        quarter_scores(corpus, rows, s, quarter)
+    for i in range(4):
+        wires_of(corpus, rows, s, i, whole=True)
 
 
 def order(blocks, s, u, dst):
@@ -219,29 +222,32 @@
         clean_at(dst, at + 32)
 
 
-def leaders(groups, own, far, s, s2, u, w, emit):
-    units = [(g, corpus) for g in range(len(groups)) for corpus in (own, far)]
-    buffers = (s, s2)
-    score(own, groups[0][1](), s)
+def leaders(groups, own, far, *work, emit):
+    near_parts, far_parts, (s, u, w) = work[:4], work[4:8], work[8:]
+    sides = (near_parts, far_parts)
+    parts = [(g, side, i) for g in range(len(groups)) for side in range(2) for i in range(4)]
+
+    def scored(k):
+        if k < len(parts):
+            g, side, i = parts[k]
+            wires_of((own, far)[side](), groups[g][1](), sides[side], i)
+
+    for k in range(AHEAD):
+        scored(k)
     peak = None
-    for k, (g, _) in enumerate(units):
+    for k, (g, side, i) in enumerate(parts):
+        scored(k + AHEAD)
         blocks = groups[g][0]
-        here = buffers[k % 2]
-        ahead = units[k + 1] if k + 1 < len(units) else None
-        ahead_rows = groups[ahead[0]][1]() if ahead else None
-        base = (k % 2) * 64 * blocks
-        for i in range(4):
-            if ahead:
-                quarter_scores(ahead[1], ahead_rows, buffers[(k + 1) % 2], i)
-            if i < 2 * blocks:
-                now = shorten(here, i * 64, u, base + i * 32)
-                peak = now if peak is None else jnp.maximum(peak, now)
-        if k % 2 == 0:
+        if blocks == 2 or i % 2 == 1:
+            nth = i if blocks == 2 else i // 2
+            now = shorten(sides[side][nth], 0, u, side * 64 * blocks + nth * 32)
+            peak = now if peak is None else jnp.maximum(peak, now)
+        if side == 0 or i < 3:
             continue
-        for i in range(2 * blocks):
-            peak = jnp.maximum(peak, best32(u, i * 64, w, i * 32))
+        for j in range(2 * blocks):
+            peak = jnp.maximum(peak, best32(u, j * 64, w, j * 32))
         if blocks == 2:
-            loop(2, lambda i: merge64(w, i * 64, u))
+            loop(2, lambda j: merge64(w, j * 64, u))
             peak = jnp.maximum(peak, best64(u, w))
             turns = (4, 2)
         else:
@@ -257,7 +263,7 @@
 
         @pl.when(unsure)
         def _():
-            long_way(blocks, groups[g][1](), own, far, s if k + 1 == len(units) else s2, u, w)
+            long_way(blocks, groups[g][1](), own(), far(), s, u, w)
 
         for half in range(blocks):
             emit(g, half, w[pl.ds(half, TOPK, stride=8), :].T)
@@ -300,28 +306,35 @@
     return jnp.concatenate([found[c * many : (c + 1) * many, :] for c in range(COLS)], axis=1)
 
 
-def first_kernel(chunk, own, far, out, both, rows, *work):
+def first_kernel(chunk, own, far_in, out, far, rows, sem, *work):
+    copy = pltpu.make_async_copy(far_in, far, sem)
+    copy.start()
     rows[...] = main_rows(chunk)
-    both[0] = own[...]
-    both[1] = far[...]
+    waited = []
+
+    def partner():
+        if not waited:
+            copy.wait()
+            waited.append(True)
+        return far
 
     def emit(g, half, value):
         out[half * Q : (half + 1) * Q, :] = value
 
-    leaders([(2, lambda: rows[...])], own, far, *work, emit)
-
-
-def early_kernel(half0, half1, both, out, rows, *work):
+    leaders([(2, lambda: rows[...])], lambda: own, partner, *work, emit=emit)
+
+
+def early_kernel(half0, half1, own, far, out, rows, *work):
     rows[0:128, :] = main_rows(half0)
     rows[128:256, :] = main_rows(half1)
 
     def emit(g, half, value):
         out[half * Q : (half + 1) * Q, :] = value
 
-    leaders([(2, lambda: rows[...])], both.at[0], both.at[1], *work, emit)
-
-
-def middle_kernel(mine, cx0, cx1, cy0, cy1, both, out, tails, rows, *work):
+    leaders([(2, lambda: rows[...])], lambda: own, lambda: far, *work, emit=emit)
+
+
+def middle_kernel(mine, cx0, cx1, cy0, cy1, own, far, out, tails, rows, *work):
     rows[0:128, :] = main_rows(cx1)
     rows[128:256, :] = main_rows(cy1)
     rows[256:320, :] = tail_rows(mine)
@@ -333,7 +346,7 @@
         (out, tails)[g][half * Q : (half + 1) * Q, :] = value
 
     leaders(
-        [(2, lambda: rows[0:256, :]), (2, lambda: rows[256:512, :])], both.at[0], both.at[1], *work, emit
+        [(2, lambda: rows[0:256, :]), (2, lambda: rows[256:512, :])], lambda: own, lambda: far, *work, emit=emit
     )
 
 
@@ -354,7 +367,7 @@
     return jnp.where(c < 0, -v, v)
 
 
-def late_kernel(at, cd0, cd1, both, r0, r1, r2, tails, out, rows, last, box, *work):
+def late_kernel(at, cd0, cd1, own, far, r0, r1, r2, tails, out, rows, last, box, *work):
     rows[0:128, :] = main_rows(cd0)
     rows[128:256, :] = main_rows(cd1)
     rows[256:288, :] = tail_rows(cd0)
@@ -365,7 +378,7 @@
         last[g * 256 + half * Q : g * 256 + (half + 1) * Q, :] = value
 
     leaders(
-        [(2, lambda: rows[0:256, :]), (1, lambda: rows[256:384, :])], both.at[0], both.at[1], *work, emit
+        [(2, lambda: rows[0:256, :]), (1, lambda: rows[256:384, :])], lambda: own, lambda: far, *work, emit=emit
     )
     me = at[0]
     owner = (me, me ^ 1, me ^ 2, me ^ 3)
@@ -393,8 +406,7 @@
 COST = 2 * 256 * 2048 * 768 * 8
 VMEM = pl.BlockSpec(memory_space=pltpu.VMEM)
 LIMIT = pltpu.CompilerParams(vmem_limit_bytes=14 << 20)
-WORK = [
-    pltpu.VMEM((256 * 8, 128), jnp.float32),
+WORK = [pltpu.VMEM((64 * 8, 128), jnp.float32)] * 8 + [
     pltpu.VMEM((256 * 8, 128), jnp.float32),
     pltpu.VMEM((256 * 8, 128), jnp.float32),
     pltpu.VMEM((128 * 8, 128), jnp.float32),
@@ -406,48 +418,48 @@
         first_kernel,
         out_shape=(
             jax.ShapeDtypeStruct((256, TOPK), jnp.float32),
-            jax.ShapeDtypeStruct((2, 1024, WIDTH), jnp.bfloat16),
+            jax.ShapeDtypeStruct((1024, WIDTH), jnp.bfloat16),
         ),
-        in_specs=[VMEM] * 3,
+        in_specs=[VMEM, VMEM, pl.BlockSpec(memory_space=pl.ANY)],
         out_specs=(VMEM, VMEM),
-        scratch_shapes=[pltpu.VMEM((256, WIDTH), jnp.bfloat16)] + WORK,
+        scratch_shapes=[pltpu.VMEM((256, WIDTH), jnp.bfloat16), pltpu.SemaphoreType.DMA] + WORK,
         compiler_params=LIMIT,
         cost_estimate=pl.CostEstimate(flops=COST, bytes_accessed=1 << 20, transcendentals=0),
         name="first",
     )(chunk, own, far)
 
 
-def early(half0, half1, both):
+def early(half0, half1, own, far):
     return pl.pallas_call(
         early_kernel,
         out_shape=jax.ShapeDtypeStruct((256, TOPK), jnp.float32),
-        in_specs=[VMEM] * 3,
+        in_specs=[VMEM] * 4,
         out_specs=VMEM,
         scratch_shapes=[pltpu.VMEM((256, WIDTH), jnp.bfloat16)] + WORK,
         compiler_params=LIMIT,
         cost_estimate=pl.CostEstimate(flops=COST, bytes_accessed=1 << 20, transcendentals=0),
         name="early",
-    )(half0, half1, both)
-
-
-def middle(mine, halves, both):
+    )(half0, half1, own, far)
+
+
+def middle(mine, halves, own, far):
     return pl.pallas_call(
         middle_kernel,
         out_shape=[jax.ShapeDtypeStruct((256, TOPK), jnp.float32)] * 2,
-        in_specs=[VMEM] * 6,
+        in_specs=[VMEM] * 7,
         out_specs=[VMEM] * 2,
         scratch_shapes=[pltpu.VMEM((512, WIDTH), jnp.bfloat16)] + WORK,
         compiler_params=LIMIT,
         cost_estimate=pl.CostEstimate(flops=COST * 2, bytes_accessed=1 << 20, transcendentals=0),
         name="middle",
-    )(mine, *halves, both)
-
-
-def late(at, halves, both, results):
+    )(mine, *halves, own, far)
+
+
+def late(at, halves, own, far, results):
     return pl.pallas_call(
         late_kernel,
         out_shape=jax.ShapeDtypeStruct((LANGS, 4, ROWS, TOPK), jnp.int16),
-        in_specs=[pl.BlockSpec(memory_space=pltpu.SMEM)] + [VMEM] * 7,
+        in_specs=[pl.BlockSpec(memory_space=pltpu.SMEM)] + [VMEM] * 8,
         out_specs=VMEM,
         scratch_shapes=[
             pltpu.VMEM((384, WIDTH), jnp.bfloat16),
@@ -458,7 +470,7 @@
         compiler_params=LIMIT,
         cost_estimate=pl.CostEstimate(flops=COST * 2, bytes_accessed=1 << 20, transcendentals=0),
         name="late",
-    )(at, *halves, both, *results)
+    )(at, *halves, own, far, *results)
 
 
 def outbox_kernel(queries_in, routes_in, out, slots, queries, routes, sems):
@@ -512,7 +524,7 @@
             pltpu.VMEM((1, Q), jnp.int32),
             pltpu.SemaphoreType.DMA((2,)),
         ],
-        compiler_params=LIMIT,
+        compiler_params=pltpu.CompilerParams(vmem_limit_bytes=60 << 20),
         name="outbox",
     )(queries, routes)
 
@@ -588,16 +600,16 @@
     cx0, cy0, cx1, cy1 = (
         lax.ppermute(part, AXES, moves(over)) for part in (mine[:8], mine[8:]) for over in (over_x, over_y)
     )
-    r0, both = first(mine, corpus, far)
+    r0, far = first(mine, corpus, far)
     cx0, cy0, r0 = lax.optimization_barrier((cx0, cy0, r0))
     cd0 = lax.ppermute(cx0, AXES, moves(over_y))
-    r1 = early(cx0, cy0, both)
+    r1 = early(cx0, cy0, corpus, far)
     cx1, cy1, r1 = lax.optimization_barrier((cx1, cy1, r1))
     cd1 = lax.ppermute(cy1, AXES, moves(over_x))
-    r2, tails = middle(mine, (cx0, cx1, cy0, cy1), both)
+    r2, tails = middle(mine, (cx0, cx1, cy0, cy1), corpus, far)
     shard = lax.axis_index("shard")
     at = (lax.shift_right_logical(shard, 2) * 2 + (lax.shift_right_logical(shard, 1) & 1)).reshape(1)
-    found = late(at, (cd0, cd1), both, (r0, r1, r2, tails))
+    found = late(at, (cd0, cd1), corpus, far, (r0, r1, r2, tails))
     back = lax.all_to_all(
         found.reshape(LANGS * 4, ROWS, TOPK), AXES, 0, 0, axis_index_groups=TEAMS, tiled=True
     )

time: 74.4 us -> 74.3 us (level); the launches traced: 74.1 us -> 73 us
  local copies, waits for them, and re-layouts: 1.62 us -> 0.04 us
  blocking collectives: 21.9 us -> 22.8 us
    unnamed x6 -> x4, local copies, waits for them, and re-layouts: 1.58 us -> 0.01 us
    all_to_all x1, blocking collectives: 21.9 us -> 22.8 us  [shards(): lax.all_to_all(found.reshape(LANGS * 4, ROWS, TOPK), AXES, 0, 0, axis_ind...]
  transfers between devices with their start and end apart: 8 -> 8, of which waited for: 1 -> 2; matrix products, arithmetic and copies ran while one was open for 0% -> 0% of each run, Pallas kernels for 18% -> 18%
where the time goes in v7:
time: 74.3 us; the launch traced here: 73 us
  blocking collectives  22.8 us (31%)
  starting transfers between devices  20.5 us (28%)
  Pallas kernels  19.9 us (27%)
  waiting for transfers between devices  9.61 us (13%)
    all_to_all x1, blocking collectives, shards(): lax.all_to_all(found.reshape(LANGS * 4, ROWS, TOPK), AXES, 0, 0, axis_ind...  22.8 us
    all_to_all x1, waiting for transfers between devices, shards(): lax.all_to_all(outbox, 'lang', split_axis=0, concat_axis=0, tiled=True)  9.31 us
    all_to_all x1, starting transfers between devices, shards(): lax.all_to_all(outbox, 'lang', split_axis=0, concat_axis=0, tiled=True)  6.46 us
    ppermute x4, starting transfers between devices, shards(): lax.ppermute(part, AXES, moves(over))  6.02 us
    pallas_call x1, Pallas kernels, middle(): pl.pallas_call(middle_kernel, out_shape=[jax.ShapeDtypeStruct((256, TOPK)...  4.99 us
    pallas_call x1, Pallas kernels, late(): pl.pallas_call(late_kernel, out_shape=jax.ShapeDtypeStruct((LANGS, 4, ROW...  4.89 us
    pallas_call x1, Pallas kernels, first(): pl.pallas_call(first_kernel, out_shape=(jax.ShapeDtypeStruct((256, TOPK),...  3.53 us
    ppermute x1, starting transfers between devices, shards(): far = lax.ppermute(corpus, AXES, moves(pair))  3.3 us
  transfers between devices with their start and end apart: 8, of which 2 were waited for; matrix products, arithmetic and copies ran while one was open for 0% of the time, Pallas kernels for 18%

profile of v7, /device:TPU:1, one launch (start us, length us, event | category | flops | bytes accessed | tf_op | source)
XLA Modules:
  0.0 73.0 jit_solution(5937986186736440774)
XLA Ops:
  0.0 0.0 copy-start.1
  0.0 3.3 %collective-permute-start.2 = (bf16[1024,768]{1,0:T(8,128)(2,1)}, bf16[1024,768]{1,0:T(8,128)(2,1)}, u32[]{:S(2)}, u32[]{:S(2)}) collective-permute-start(bf16[1024,768]{1,0:T(8,128)(2,1)} %own.7), channel_id=1, source_target_pairs={{0,1},{1,0},{2,3},{3,2},{4,5},{5,4},{6,7},{7,6},{8,11},{9,10},{10,... | collective-permute-start | bytes 4718600 | tf_op jit(solution)/shard_map/ppermute | solution.py:597
  3.3 2.3 %outbox.1 = (bf16[16,120,128]{2,1,0:T(8,128)(2,1)}, s32[1,128]{1,0:T(1,128)}) custom-call(bf16[128,768]{1,0:T(8,128)(2,1)} %queries_in.1, s32[1,128]{1,0:T(1,128)} %bitcast.6), custom_call_target="tpu_custom_call" | custom-call | tf_op jit(solution)/shard_map/outbox/pallas_call | solution.py:514
  5.6 6.5 %all-to-all-start = ((bf16[16,120,128]{2,1,0:T(8,128)(2,1)}), bf16[16,120,128]{2,1,0:T(8,128)(2,1)S(1)}, u32[]{:S(2)}, u32[]{:S(2)}) async-start(bf16[16,120,128]{2,1,0:T(8,128)(2,1)} %get-tuple-element.17), calls=%async_computation | async-start | bytes 983040 | tf_op jit(solution)/shard_map/all_to_all | solution.py:599
  12.1 9.3 %all-to-all-done.chunk.mine = bf16[16,120,128]{2,1,0:T(8,128)(2,1)S(1)} async-done(((bf16[16,120,128]{2,1,0:T(8,128)(2,1)}), bf16[16,120,128]{2,1,0:T(8,128)(2,1)S(1)}, u32[]{:S(2)}, u32[]{:S(2)}) %all-to-all-start) | async-done | bytes 491552 | tf_op jit(solution)/shard_map/all_to_all | solution.py:599
  21.4 2.1 %collective-permute-start = (bf16[8,120,128]{2,1,0:T(8,128)(2,1)S(1)}, bf16[8,120,128]{2,1,0:T(8,128)(2,1)S(1)}, u32[]{:S(2)}, u32[]{:S(2)}) collective-permute-start(bf16[8,120,128]{2,1,0:T(8,128)(2,1)S(1)} %get-tuple-element.30), channel_id=1, source_target_pairs={{0,2},{1,3},{2,0},{3,1},{4,6},{5,7},{6,4},{7,5},{8,10},{9,11},{10,... | collective-permute-start | bytes 737288 | tf_op jit(solution)/shard_map/ppermute | solution.py:601
  23.6 2.6 %collective-permute-start.1 = (bf16[8,120,128]{2,1,0:T(8,128)(2,1)S(1)}, bf16[8,120,128]{2,1,0:T(8,128)(2,1)S(1)}, u32[]{:S(2)}, u32[]{:S(2)}) collective-permute-start(bf16[8,120,128]{2,1,0:T(8,128)(2,1)S(1)} %get-tuple-element.30), channel_id=1, source_target_pairs={{0,4},{1,5},{2,6},{3,7},{4,0},{5,1},{6,2},{7,3},{8,12},{9,13},{10,... | collective-permute-start | bytes 737288 | tf_op jit(solution)/shard_map/ppermute | solution.py:601
  26.2 0.9 %collective-permute-start.4 = (bf16[8,120,128]{2,1,0:T(8,128)(2,1)S(1)}, bf16[8,120,128]{2,1,0:T(8,128)(2,1)S(1)}, u32[]{:S(2)}, u32[]{:S(2)}) collective-permute-start(bf16[8,120,128]{2,1,0:T(8,128)(2,1)S(1)} %get-tuple-element.29), channel_id=1, source_target_pairs={{0,2},{1,3},{2,0},{3,1},{4,6},{5,7},{6,4},{7,5},{8,10},{9,11},{10,... | collective-permute-start | bytes 737288 | tf_op jit(solution)/shard_map/ppermute | solution.py:601
  27.1 0.3 collective-permute-start.5
  27.5 0.0 collective-permute-done.2.far_in
  27.5 0.0 copy-done.1
  27.5 3.5 %first.1 = (f32[256,128]{1,0:T(8,128)S(1)}, bf16[1024,768]{1,0:T(8,128)(2,1)S(1)}) custom-call(bf16[16,120,128]{2,1,0:T(8,128)(2,1)S(1)} %all-to-all-done.chunk.mine, bf16[1024,768]{1,0:T(8,128)(2,1)S(1)} %copy-done.1, bf16[1024,768]{1,0:T(8,128)(2,1)} %collective-permute-done.2.far_in), custom_call_target="tpu_custom_call" | custom-call | flops 6442450944 | bytes 1048576 | tf_op jit(solution)/shard_map/first/pallas_call | solution.py:417
  31.0 0.0 collective-permute-done.half0.cx0
  31.0 0.0 collective-permute-done.1.half1.cy0
  31.0 2.7 %collective-permute-start.3 = (bf16[8,120,128]{2,1,0:T(8,128)(2,1)S(1)}, bf16[8,120,128]{2,1,0:T(8,128)(2,1)S(1)}, u32[]{:S(2)}, u32[]{:S(2)}) collective-permute-start(bf16[8,120,128]{2,1,0:T(8,128)(2,1)S(1)} %collective-permute-done.half0.cx0), channel_id=1, source_target_pairs={{0,4},{1,5},{2,6},{3,7},{4,0},{5,1},{6,2},{7,3},{8,12},{9,13},{10,... | collective-permute-start | bytes 737288 | tf_op jit(solution)/shard_map/ppermute | solution.py:605
  33.7 2.6 %early.1.r1 = f32[256,128]{1,0:T(8,128)S(1)} custom-call(bf16[8,120,128]{2,1,0:T(8,128)(2,1)S(1)} %collective-permute-done.half0.cx0, bf16[8,120,128]{2,1,0:T(8,128)(2,1)S(1)} %collective-permute-done.1.half1.cy0, bf16[1024,768]{1,0:T(8,128)(2,1)S(1)} %copy-done.1, bf16[1024,768]{1,0:T(8,128)(2,1)S(1)} %get-tuple-element.21.far), custom_call_target="tpu_custom_call" | custom-call | flops 6442450944 | bytes 1048576 | tf_op jit(solution)/shard_map/early/pallas_call | solution.py:433
  36.3 0.0 collective-permute-done.4.cx1
  36.3 0.3 collective-permute-done.5.cy1
  36.6 2.0 %collective-permute-start.6 = (bf16[8,120,128]{2,1,0:T(8,128)(2,1)S(1)}, bf16[8,120,128]{2,1,0:T(8,128)(2,1)S(1)}, u32[]{:S(2)}, u32[]{:S(2)}) collective-permute-start(bf16[8,120,128]{2,1,0:T(8,128)(2,1)S(1)} %collective-permute-done.5.cy1), channel_id=1, source_target_pairs={{0,2},{1,3},{2,0},{3,1},{4,6},{5,7},{6,4},{7,5},{8,10},{9,11},{10,... | collective-permute-start | bytes 737288 | tf_op jit(solution)/shard_map/ppermute | solution.py:608
  38.6 5.0 %middle.1 = (f32[256,128]{1,0:T(8,128)S(1)}, f32[256,128]{1,0:T(8,128)S(1)}) custom-call(bf16[16,120,128]{2,1,0:T(8,128)(2,1)S(1)} %all-to-all-done.chunk.mine, bf16[8,120,128]{2,1,0:T(8,128)(2,1)S(1)} %collective-permute-done.half0.cx0, bf16[8,120,128]{2,1,0:T(8,128)(2,1)S(1)} %collective-permute-done.4.cx1, ...), custom_call_target="tpu_custom_call" | custom-call | flops 12884901888 | bytes 1048576 | tf_op jit(solution)/shard_map/middle/pallas_call | solution.py:446
  43.6 0.0 collective-permute-done.6.cd1
  43.6 0.0 collective-permute-done.3.cd0
  43.6 0.0 copy-start
  43.6 4.9 %late.1 = s16[16,4,24,128]{3,2,1,0:T(8,128)(2,1)S(1)} custom-call(s32[1]{0:T(128)} %bitcast.at, bf16[8,120,128]{2,1,0:T(8,128)(2,1)S(1)} %collective-permute-done.3.cd0, bf16[8,120,128]{2,1,0:T(8,128)(2,1)S(1)} %collective-permute-done.6.cd1, bf16[1024,768]{1,0:T(8,128)(2,1)S(1)} %copy-done.1, bf16[1024,768]{1,0:T(8,128)(2,1)S(1)} %get-tuple-element.21.far, ...), custom_call_target="tpu_custom_call" | custom-call | flops 12884901888 | bytes 1048576 | tf_op jit(solution)/shard_map/late/pallas_call | solution.py:459
  48.5 22.8 %all_to_all.10 = s16[64,24,128]{2,1,0:T(8,128)(2,1)S(1)} all-to-all(s16[64,24,128]{2,1,0:T(8,128)(2,1)S(1)} %bitcast.5), channel_id=1, replica_groups={{0,2,4,6,8,10,12,14,16,18,20,22,24,26,28,30,32,34,36,38,40,42,44,46,48,..., dimensions={0} | all-to-all | bytes 786432 | tf_op jit(solution)/shard_map/all_to_all | solution.py:613
  71.3 0.0 copy-done
  71.3 1.6 %join.1 = f32[128,128]{1,0:T(8,128)} custom-call(s16[16,4,24,128]{3,2,1,0:T(8,128)(2,1)S(1)} %bitcast.4, s32[1,128]{1,0:T(1,128)S(1)} %copy-done), custom_call_target="tpu_custom_call" | custom-call | tf_op jit(solution)/shard_map/join/pallas_call | solution.py:554
  (1 shorter events, 0.0 us)
Async XLA Ops:
  0.0 27.5 %copy-start.1 = (bf16[1024,768]{1,0:T(8,128)(2,1)S(1)}, bf16[1024,768]{1,0:T(8,128)(2,1)}, u32[]{:S(2)}) copy-start(bf16[1024,768]{1,0:T(8,128)(2,1)} %own.7) | copy-start | bytes 4718596
  0.0 27.5 %collective-permute-start.2 = (bf16[1024,768]{1,0:T(8,128)(2,1)}, bf16[1024,768]{1,0:T(8,128)(2,1)}, u32[]{:S(2)}, u32[]{:S(2)}) collective-permute-start(bf16[1024,768]{1,0:T(8,128)(2,1)} %own.7), channel_id=1, source_target_pairs={{0,1},{1,0},{2,3},{3,2},{4,5},{5,4},{6,7},{7,6},{8,11},{9,10},{10,... | collective-permute-start | bytes 4718600 | tf_op jit(solution)/shard_map/ppermute | solution.py:597
  5.6 15.8 %all-to-all-start = ((bf16[16,120,128]{2,1,0:T(8,128)(2,1)}), bf16[16,120,128]{2,1,0:T(8,128)(2,1)S(1)}, u32[]{:S(2)}, u32[]{:S(2)}) async-start(bf16[16,120,128]{2,1,0:T(8,128)(2,1)} %get-tuple-element.17), calls=%async_computation | async-start | bytes 983040 | tf_op jit(solution)/shard_map/all_to_all | solution.py:599
  21.4 9.6 %collective-permute-start = (bf16[8,120,128]{2,1,0:T(8,128)(2,1)S(1)}, bf16[8,120,128]{2,1,0:T(8,128)(2,1)S(1)}, u32[]{:S(2)}, u32[]{:S(2)}) collective-permute-start(bf16[8,120,128]{2,1,0:T(8,128)(2,1)S(1)} %get-tuple-element.30), channel_id=1, source_target_pairs={{0,2},{1,3},{2,0},{3,1},{4,6},{5,7},{6,4},{7,5},{8,10},{9,11},{10,... | collective-permute-start | bytes 737288 | tf_op jit(solution)/shard_map/ppermute | solution.py:601
  23.6 7.5 %collective-permute-start.1 = (bf16[8,120,128]{2,1,0:T(8,128)(2,1)S(1)}, bf16[8,120,128]{2,1,0:T(8,128)(2,1)S(1)}, u32[]{:S(2)}, u32[]{:S(2)}) collective-permute-start(bf16[8,120,128]{2,1,0:T(8,128)(2,1)S(1)} %get-tuple-element.30), channel_id=1, source_target_pairs={{0,4},{1,5},{2,6},{3,7},{4,0},{5,1},{6,2},{7,3},{8,12},{9,13},{10,... | collective-permute-start | bytes 737288 | tf_op jit(solution)/shard_map/ppermute | solution.py:601
  26.2 10.1 %collective-permute-start.4 = (bf16[8,120,128]{2,1,0:T(8,128)(2,1)S(1)}, bf16[8,120,128]{2,1,0:T(8,128)(2,1)S(1)}, u32[]{:S(2)}, u32[]{:S(2)}) collective-permute-start(bf16[8,120,128]{2,1,0:T(8,128)(2,1)S(1)} %get-tuple-element.29), channel_id=1, source_target_pairs={{0,2},{1,3},{2,0},{3,1},{4,6},{5,7},{6,4},{7,5},{8,10},{9,11},{10,... | collective-permute-start | bytes 737288 | tf_op jit(solution)/shard_map/ppermute | solution.py:601
  27.1 9.5 %collective-permute-start.5 = (bf16[8,120,128]{2,1,0:T(8,128)(2,1)S(1)}, bf16[8,120,128]{2,1,0:T(8,128)(2,1)S(1)}, u32[]{:S(2)}, u32[]{:S(2)}) collective-permute-start(bf16[8,120,128]{2,1,0:T(8,128)(2,1)S(1)} %get-tuple-element.29), channel_id=1, source_target_pairs={{0,4},{1,5},{2,6},{3,7},{4,0},{5,1},{6,2},{7,3},{8,12},{9,13},{10,... | collective-permute-start | bytes 737288 | tf_op jit(solution)/shard_map/ppermute | solution.py:601
  31.0 12.6 %collective-permute-start.3 = (bf16[8,120,128]{2,1,0:T(8,128)(2,1)S(1)}, bf16[8,120,128]{2,1,0:T(8,128)(2,1)S(1)}, u32[]{:S(2)}, u32[]{:S(2)}) collective-permute-start(bf16[8,120,128]{2,1,0:T(8,128)(2,1)S(1)} %collective-permute-done.half0.cx0), channel_id=1, source_target_pairs={{0,4},{1,5},{2,6},{3,7},{4,0},{5,1},{6,2},{7,3},{8,12},{9,13},{10,... | collective-permute-start | bytes 737288 | tf_op jit(solution)/shard_map/ppermute | solution.py:605
  36.6 7.0 %collective-permute-start.6 = (bf16[8,120,128]{2,1,0:T(8,128)(2,1)S(1)}, bf16[8,120,128]{2,1,0:T(8,128)(2,1)S(1)}, u32[]{:S(2)}, u32[]{:S(2)}) collective-permute-start(bf16[8,120,128]{2,1,0:T(8,128)(2,1)S(1)} %collective-permute-done.5.cy1), channel_id=1, source_target_pairs={{0,2},{1,3},{2,0},{3,1},{4,6},{5,7},{6,4},{7,5},{8,10},{9,11},{10,... | collective-permute-start | bytes 737288 | tf_op jit(solution)/shard_map/ppermute | solution.py:608
  43.6 27.7 %copy-start = (s32[1,128]{1,0:T(1,128)S(1)}, s32[1,128]{1,0:T(1,128)}, u32[]{:S(2)}) copy-start(s32[1,128]{1,0:T(1,128)} %get-tuple-element.28.slots) | copy-start | bytes 1540

commit v8 on v7

--- a/solution.py
+++ b/solution.py
@@ -306,22 +306,13 @@
     return jnp.concatenate([found[c * many : (c + 1) * many, :] for c in range(COLS)], axis=1)
 
 
-def first_kernel(chunk, own, far_in, out, far, rows, sem, *work):
-    copy = pltpu.make_async_copy(far_in, far, sem)
-    copy.start()
+def first_kernel(chunk, own, far, out, rows, *work):
     rows[...] = main_rows(chunk)
-    waited = []
-
-    def partner():
-        if not waited:
-            copy.wait()
-            waited.append(True)
-        return far
 
     def emit(g, half, value):
         out[half * Q : (half + 1) * Q, :] = value
 
-    leaders([(2, lambda: rows[...])], lambda: own, partner, *work, emit=emit)
+    leaders([(2, lambda: rows[...])], lambda: own, lambda: far, *work, emit=emit)
 
 
 def early_kernel(half0, half1, own, far, out, rows, *work):
@@ -367,7 +358,7 @@
     return jnp.where(c < 0, -v, v)
 
 
-def late_kernel(at, cd0, cd1, own, far, r0, r1, r2, tails, out, rows, last, box, *work):
+def late_kernel(at, cd0, cd1, own, far, r0, r1, r2, tails, keep, give, rows, last, box, *work):
     rows[0:128, :] = main_rows(cd0)
     rows[128:256, :] = main_rows(cd1)
     rows[256:288, :] = tail_rows(cd0)
@@ -380,7 +371,7 @@
     leaders(
         [(2, lambda: rows[0:256, :]), (1, lambda: rows[256:384, :])], lambda: own, lambda: far, *work, emit=emit
     )
-    me = at[0]
+    me, side = at[0], at[1].astype(jnp.float32)
     owner = (me, me ^ 1, me ^ 2, me ^ 3)
     none = jnp.zeros((ROWS - CAP, TOPK), jnp.float32)
     for k in range(4):
@@ -393,14 +384,19 @@
                 main = (r1, r2)[half][start : start + MAIN, :]
             else:
                 main = last[lang * MAIN : (lang + 1) * MAIN, :]
-            box[k, 0:MAIN, :] = main
+            here = 2 * k + lang % 2
+            box[here, 0:MAIN, :] = main
             start = k * 64 + lang * TAIL
             if k < 3:
-                box[k, MAIN:CAP, :] = tails[start : start + TAIL, :]
+                box[here, MAIN:CAP, :] = tails[start : start + TAIL, :]
             else:
-                box[k, MAIN:CAP, :] = last[256 + lang * TAIL : 256 + (lang + 1) * TAIL, :]
-            box[k, CAP:ROWS, :] = none
-            out[lang, owner[k]] = coded(box[k]).astype(jnp.int32).astype(jnp.int16)
+                box[here, MAIN:CAP, :] = last[256 + lang * TAIL : 256 + (lang + 1) * TAIL, :]
+            box[here, CAP:ROWS, :] = none
+            if lang % 2 == 1:
+                even, odd = coded(box[2 * k]), coded(box[2 * k + 1])
+                shift = (odd - even) * side
+                keep[lang // 2, owner[k], 0] = (even + shift).astype(jnp.int32).astype(jnp.int16)
+                give[lang // 2, owner[k]] = (odd - shift).astype(jnp.int32).astype(jnp.int16)
 
 
 COST = 2 * 256 * 2048 * 768 * 8
@@ -416,13 +412,10 @@
 def first(chunk, own, far):
     return pl.pallas_call(
         first_kernel,
-        out_shape=(
-            jax.ShapeDtypeStruct((256, TOPK), jnp.float32),
-            jax.ShapeDtypeStruct((1024, WIDTH), jnp.bfloat16),
-        ),
-        in_specs=[VMEM, VMEM, pl.BlockSpec(memory_space=pl.ANY)],
-        out_specs=(VMEM, VMEM),
-        scratch_shapes=[pltpu.VMEM((256, WIDTH), jnp.bfloat16), pltpu.SemaphoreType.DMA] + WORK,
+        out_shape=jax.ShapeDtypeStruct((256, TOPK), jnp.float32),
+        in_specs=[VMEM] * 3,
+        out_specs=VMEM,
+        scratch_shapes=[pltpu.VMEM((256, WIDTH), jnp.bfloat16)] + WORK,
         compiler_params=LIMIT,
         cost_estimate=pl.CostEstimate(flops=COST, bytes_accessed=1 << 20, transcendentals=0),
         name="first",
@@ -458,13 +451,16 @@
 def late(at, halves, own, far, results):
     return pl.pallas_call(
         late_kernel,
-        out_shape=jax.ShapeDtypeStruct((LANGS, 4, ROWS, TOPK), jnp.int16),
+        out_shape=(
+            jax.ShapeDtypeStruct((LANGS // 2, 4, 2, ROWS, TOPK), jnp.int16),
+            jax.ShapeDtypeStruct((LANGS // 2, 4, ROWS, TOPK), jnp.int16),
+        ),
         in_specs=[pl.BlockSpec(memory_space=pltpu.SMEM)] + [VMEM] * 8,
-        out_specs=VMEM,
+        out_specs=(VMEM, VMEM),
         scratch_shapes=[
             pltpu.VMEM((384, WIDTH), jnp.bfloat16),
             pltpu.VMEM((384, TOPK), jnp.float32),
-            pltpu.VMEM((4, ROWS, TOPK), jnp.float32),
+            pltpu.VMEM((8, ROWS, TOPK), jnp.float32),
         ]
         + WORK,
         compiler_params=LIMIT,
@@ -473,7 +469,7 @@
     )(at, *halves, own, far, *results)
 
 
-def outbox_kernel(queries_in, routes_in, out, slots, queries, routes, sems):
+def outbox_kernel(at, queries_in, routes_in, out, slots, queries, routes, sems):
     copies = (
         pltpu.make_async_copy(routes_in, routes, sems.at[0]),
         pltpu.make_async_copy(queries_in, queries, sems.at[1]),
@@ -490,7 +486,7 @@
     earlier = jnp.where(before & (along == down), 1.0, 0.0)
     rank = jnp.sum(earlier, axis=0, keepdims=True).astype(jnp.int32)
     lang = routes[...]
-    slots[...] = lang * ROWS + rank
+    slots[...] = (lang ^ at[1]) * ROWS + rank
     main_at = jnp.where(rank < MAIN, lang * MAIN + rank, -1)
     hits = lax.broadcasted_iota(jnp.int32, (LANGS * MAIN, Q), 0) == jnp.broadcast_to(main_at, (LANGS * MAIN, Q))
     picks = jnp.where(hits, 1.0, 0.0).astype(jnp.bfloat16)
@@ -510,14 +506,14 @@
     out[:, MAIN * COLS : SENT, :] = tail.astype(jnp.bfloat16).reshape(LANGS, each, 128)
 
 
-def outbox_of(queries, routes):
+def outbox_of(at, queries, routes):
     return pl.pallas_call(
         outbox_kernel,
         out_shape=(
             jax.ShapeDtypeStruct((LANGS, SENT, 128), jnp.bfloat16),
             jax.ShapeDtypeStruct((1, Q), jnp.int32),
         ),
-        in_specs=[pl.BlockSpec(memory_space=pltpu.HBM)] * 2,
+        in_specs=[pl.BlockSpec(memory_space=pltpu.SMEM)] + [pl.BlockSpec(memory_space=pltpu.HBM)] * 2,
         out_specs=(VMEM, VMEM),
         scratch_shapes=[
             pltpu.VMEM((Q, WIDTH), jnp.bfloat16),
@@ -526,7 +522,7 @@
         ],
         compiler_params=pltpu.CompilerParams(vmem_limit_bytes=60 << 20),
         name="outbox",
-    )(queries, routes)
+    )(at, queries, routes)
 
 
 def join_kernel(back, slots, out, a, b):
@@ -588,32 +584,36 @@
 
 
 TEAMS = [
-    [lang * 8 + y * 4 + odd + 2 * half for lang in range(16) for y in range(2) for half in range(2)]
+    [lang * 8 + y * 4 + odd + 2 * half for lang in range(core, 16, 2) for y in range(2) for half in range(2)]
+    for core in range(2)
     for odd in range(2)
 ]
 
 
 def shards(queries, routes, corpus):
     far = lax.ppermute(corpus, AXES, moves(pair))
-    outbox, slots = outbox_of(queries, routes.reshape(1, Q))
+    shard, core = lax.axis_index("shard"), lax.axis_index("lang") & 1
+    seat = lax.shift_right_logical(shard, 2) * 2 + (lax.shift_right_logical(shard, 1) & 1)
+    at = jnp.stack([seat, core])
+    outbox, slots = outbox_of(at, queries, routes.reshape(1, Q))
     mine = lax.all_to_all(outbox, "lang", split_axis=0, concat_axis=0, tiled=True)
+    mine, far = lax.optimization_barrier((mine, far))
     cx0, cy0, cx1, cy1 = (
         lax.ppermute(part, AXES, moves(over)) for part in (mine[:8], mine[8:]) for over in (over_x, over_y)
     )
-    r0, far = first(mine, corpus, far)
+    r0 = first(mine, corpus, far)
     cx0, cy0, r0 = lax.optimization_barrier((cx0, cy0, r0))
     cd0 = lax.ppermute(cx0, AXES, moves(over_y))
     r1 = early(cx0, cy0, corpus, far)
     cx1, cy1, r1 = lax.optimization_barrier((cx1, cy1, r1))
     cd1 = lax.ppermute(cy1, AXES, moves(over_x))
     r2, tails = middle(mine, (cx0, cx1, cy0, cy1), corpus, far)
-    shard = lax.axis_index("shard")
-    at = (lax.shift_right_logical(shard, 2) * 2 + (lax.shift_right_logical(shard, 1) & 1)).reshape(1)
-    found = late(at, (cd0, cd1), corpus, far, (r0, r1, r2, tails))
-    back = lax.all_to_all(
-        found.reshape(LANGS * 4, ROWS, TOPK), AXES, 0, 0, axis_index_groups=TEAMS, tiled=True
-    )
-    return join(back.reshape(LANGS, 4, ROWS, TOPK), slots)
+    keep, give = late(at, (cd0, cd1), corpus, far, (r0, r1, r2, tails))
+    other = lax.ppermute(give, AXES, [(d, d ^ 8) for d in range(128)])
+    sent = lax.dynamic_update_slice(keep, other[:, :, None], (0, 0, 1, 0, 0))
+    sent = sent.reshape(LANGS * 2, 2 * ROWS, TOPK)
+    back = lax.all_to_all(sent, AXES, 0, 0, axis_index_groups=TEAMS, tiled=True)
+    return join(back.reshape(LANGS // 2, 4, 2 * ROWS, TOPK), slots)
 
 
 def solution(mesh):

time: 74.3 us -> 80.6 us (1.085)
  blocking collectives: 22.8 us -> 35.5 us
  starting transfers between devices: 20.5 us -> 15.4 us
  waiting for transfers between devices: 9.61 us -> 7.93 us
    all_to_all x1 -> x2, blocking collectives: 22.8 us -> 35.5 us  [the longest x1 19.7 us: shards(): back = lax.all_to_all(sent, AXES, 0, 0, axis_index_groups=TEAMS, tiled=True)]
    all_to_all x1 -> x0, waiting for transfers between devices: 9.31 us -> none  [shards(): lax.all_to_all(outbox, 'lang', split_axis=0, concat_axis=0, tiled=True)]
    ppermute x4, waiting for transfers between devices: 0.29 us -> 6.85 us  [shards(): lax.ppermute(part, AXES, moves(over))]
    all_to_all x1 -> x0, starting transfers between devices: 6.46 us -> none  [shards(): lax.all_to_all(outbox, 'lang', split_axis=0, concat_axis=0, tiled=True)]
    ppermute x0 -> x1, starting transfers between devices: none -> 3.09 us  [shards(): other = lax.ppermute(give, AXES, [(d, d ^ 8) for d in range(128)])]
    ppermute x1, starting transfers between devices: 2.7 us -> 0.41 us  [shards(): cd0 = lax.ppermute(cx0, AXES, moves(over_y))]
    ppermute x0 -> x1, waiting for transfers between devices: none -> 1.07 us  [shards(): other = lax.ppermute(give, AXES, [(d, d ^ 8) for d in range(128)])]
  transfers between devices with their start and end apart: 8 -> 8, of which waited for: 2 -> 3; matrix products, arithmetic and copies ran while one was open for 0% -> 1% of each run, Pallas kernels for 18% -> 16%
where the time goes in v8:
time: 80.6 us; the launch traced here: 79.7 us
  blocking collectives  35.5 us (44%)
  Pallas kernels  20.2 us (25%)
  starting transfers between devices  15.4 us (19%)
  waiting for transfers between devices  7.93 us (10%)
    all_to_all x1, blocking collectives, shards(): back = lax.all_to_all(sent, AXES, 0, 0, axis_index_groups=TEAMS, tiled=True)  19.7 us
    all_to_all x1, blocking collectives, shards(): lax.all_to_all(outbox, 'lang', split_axis=0, concat_axis=0, tiled=True)  15.8 us
    ppermute x4, waiting for transfers between devices, shards(): lax.ppermute(part, AXES, moves(over))  6.85 us
    ppermute x4, starting transfers between devices, shards(): lax.ppermute(part, AXES, moves(over))  6.02 us
    pallas_call x1, Pallas kernels, late(): pl.pallas_call(late_kernel, out_shape=(jax.ShapeDtypeStruct((LANGS // 2,...  5.46 us
    pallas_call x1, Pallas kernels, middle(): pl.pallas_call(middle_kernel, out_shape=[jax.ShapeDtypeStruct((256, TOPK)...  4.99 us
    ppermute x1, starting transfers between devices, shards(): far = lax.ppermute(corpus, AXES, moves(pair))  3.3 us
    ppermute x1, starting transfers between devices, shards(): other = lax.ppermute(give, AXES, [(d, d ^ 8) for d in range(128)])  3.09 us
  transfers between devices with their start and end apart: 8, of which 3 were waited for; matrix products, arithmetic and copies ran while one was open for 1% of the time, Pallas kernels for 16%

profile of v8, /device:TPU:1, one launch (start us, length us, event | category | flops | bytes accessed | tf_op | source)
XLA Modules:
  0.0 79.7 jit_solution(10645040913065872738)
XLA Ops:
  0.0 0.0 copy-start.2
  0.0 3.3 %collective-permute-start = (bf16[1024,768]{1,0:T(8,128)(2,1)}, bf16[1024,768]{1,0:T(8,128)(2,1)S(1)}, u32[]{:S(2)}, u32[]{:S(2)}) collective-permute-start(bf16[1024,768]{1,0:T(8,128)(2,1)} %own.7), channel_id=1, source_target_pairs={{0,1},{1,0},{2,3},{3,2},{4,5},{5,4},{6,7},{7,6},{8,11},{9,10},{10,... | collective-permute-start | bytes 4718600 | tf_op jit(solution)/shard_map/ppermute | solution.py:594
  3.3 0.6 pad_add_fusion.at
  3.9 3.0 %outbox.1 = (bf16[16,120,128]{2,1,0:T(8,128)(2,1)}, s32[1,128]{1,0:T(1,128)}) custom-call(s32[2]{0:T(128)} %pad_add_fusion.at, bf16[128,768]{1,0:T(8,128)(2,1)} %queries_in.1, s32[1,128]{1,0:T(1,128)} %bitcast.11), custom_call_target="tpu_custom_call" | custom-call | tf_op jit(solution)/shard_map/outbox/pallas_call | solution.py:510
  6.9 15.8 %all_to_all.10.chunk.mine = bf16[16,120,128]{2,1,0:T(8,128)(2,1)S(1)} all-to-all(bf16[16,120,128]{2,1,0:T(8,128)(2,1)} %get-tuple-element.19), channel_id=1, replica_groups=mesh['lang'=16,'shard'=8] {'lang'}, dimensions={0} | all-to-all | bytes 983040 | tf_op jit(solution)/shard_map/all_to_all | solution.py:599
  22.6 0.0 collective-permute-done.far
  22.7 2.7 %collective-permute-start.5 = (bf16[8,120,128]{2,1,0:T(8,128)(2,1)S(1)}, bf16[8,120,128]{2,1,0:T(8,128)(2,1)S(1)}, u32[]{:S(2)}, u32[]{:S(2)}) collective-permute-start(bf16[8,120,128]{2,1,0:T(8,128)(2,1)S(1)} %get-tuple-element.33), channel_id=1, source_target_pairs={{0,4},{1,5},{2,6},{3,7},{4,0},{5,1},{6,2},{7,3},{8,12},{9,13},{10,... | collective-permute-start | bytes 737288 | tf_op jit(solution)/shard_map/ppermute | solution.py:602
  25.4 2.0 %collective-permute-start.4 = (bf16[8,120,128]{2,1,0:T(8,128)(2,1)S(1)}, bf16[8,120,128]{2,1,0:T(8,128)(2,1)S(1)}, u32[]{:S(2)}, u32[]{:S(2)}) collective-permute-start(bf16[8,120,128]{2,1,0:T(8,128)(2,1)S(1)} %get-tuple-element.33), channel_id=1, source_target_pairs={{0,2},{1,3},{2,0},{3,1},{4,6},{5,7},{6,4},{7,5},{8,10},{9,11},{10,... | collective-permute-start | bytes 737288 | tf_op jit(solution)/shard_map/ppermute | solution.py:602
  27.4 0.3 collective-permute-start.2
  27.8 0.9 %collective-permute-start.1 = (bf16[8,120,128]{2,1,0:T(8,128)(2,1)S(1)}, bf16[8,120,128]{2,1,0:T(8,128)(2,1)S(1)}, u32[]{:S(2)}, u32[]{:S(2)}) collective-permute-start(bf16[8,120,128]{2,1,0:T(8,128)(2,1)S(1)} %get-tuple-element.34), channel_id=1, source_target_pairs={{0,2},{1,3},{2,0},{3,1},{4,6},{5,7},{6,4},{7,5},{8,10},{9,11},{10,... | collective-permute-start | bytes 737288 | tf_op jit(solution)/shard_map/ppermute | solution.py:602
  28.7 0.0 copy-done.2
  28.7 2.6 %first.1.r0 = f32[256,128]{1,0:T(8,128)S(1)} custom-call(bf16[16,120,128]{2,1,0:T(8,128)(2,1)S(1)} %all_to_all.10.chunk.mine, bf16[1024,768]{1,0:T(8,128)(2,1)S(1)} %copy-done.2, bf16[1024,768]{1,0:T(8,128)(2,1)S(1)} %collective-permute-done.far), custom_call_target="tpu_custom_call" | custom-call | flops 6442450944 | bytes 1048576 | tf_op jit(solution)/shard_map/first/pallas_call | solution.py:413
  31.3 4.6 %collective-permute-done.2.half1.cy0 = bf16[8,120,128]{2,1,0:T(8,128)(2,1)S(1)} collective-permute-done((bf16[8,120,128]{2,1,0:T(8,128)(2,1)S(1)}, bf16[8,120,128]{2,1,0:T(8,128)(2,1)S(1)}, u32[]{:S(2)}, u32[]{:S(2)}) %collective-permute-start.2) | collective-permute-done | bytes 245792 | tf_op jit(solution)/shard_map/ppermute | solution.py:602
  35.8 2.3 %collective-permute-done.1.half0.cx0 = bf16[8,120,128]{2,1,0:T(8,128)(2,1)S(1)} collective-permute-done((bf16[8,120,128]{2,1,0:T(8,128)(2,1)S(1)}, bf16[8,120,128]{2,1,0:T(8,128)(2,1)S(1)}, u32[]{:S(2)}, u32[]{:S(2)}) %collective-permute-start.1) | collective-permute-done | bytes 245792 | tf_op jit(solution)/shard_map/ppermute | solution.py:602
  38.1 0.4 collective-permute-start.3
  38.5 2.6 %early.1.r1 = f32[256,128]{1,0:T(8,128)S(1)} custom-call(bf16[8,120,128]{2,1,0:T(8,128)(2,1)S(1)} %collective-permute-done.1.half0.cx0, bf16[8,120,128]{2,1,0:T(8,128)(2,1)S(1)} %collective-permute-done.2.half1.cy0, bf16[1024,768]{1,0:T(8,128)(2,1)S(1)} %copy-done.2, bf16[1024,768]{1,0:T(8,128)(2,1)S(1)} %collective-permute-done.far), custom_call_target="tpu_custom_call" | custom-call | flops 6442450944 | bytes 1048576 | tf_op jit(solution)/shard_map/early/pallas_call | solution.py:426
  41.1 0.0 copy-start
  41.1 0.0 collective-permute-done.5.cy1
  41.1 0.0 collective-permute-done.4.cx1
  41.1 2.5 %collective-permute-start.6 = (bf16[8,120,128]{2,1,0:T(8,128)(2,1)S(1)}, bf16[8,120,128]{2,1,0:T(8,128)(2,1)S(1)}, u32[]{:S(2)}, u32[]{:S(2)}) collective-permute-start(bf16[8,120,128]{2,1,0:T(8,128)(2,1)S(1)} %collective-permute-done.5.cy1), channel_id=1, source_target_pairs={{0,2},{1,3},{2,0},{3,1},{4,6},{5,7},{6,4},{7,5},{8,10},{9,11},{10,... | collective-permute-start | bytes 737288 | tf_op jit(solution)/shard_map/ppermute | solution.py:609
  43.7 5.0 %middle.1 = (f32[256,128]{1,0:T(8,128)S(1)}, f32[256,128]{1,0:T(8,128)S(1)}) custom-call(bf16[16,120,128]{2,1,0:T(8,128)(2,1)S(1)} %all_to_all.10.chunk.mine, bf16[8,120,128]{2,1,0:T(8,128)(2,1)S(1)} %collective-permute-done.1.half0.cx0, bf16[8,120,128]{2,1,0:T(8,128)(2,1)S(1)} %collective-permute-done.4.cx1, ...), custom_call_target="tpu_custom_call" | custom-call | flops 12884901888 | bytes 1048576 | tf_op jit(solution)/shard_map/middle/pallas_call | solution.py:439
  48.7 0.0 collective-permute-done.6.cd1
  48.7 0.0 collective-permute-done.3.cd0
  48.7 0.0 copy-done
  48.7 0.0 copy-start.1
  48.7 5.5 %late.1 = (s16[8,4,2,24,128]{4,3,2,1,0:T(8,128)(2,1)S(1)}, s16[8,4,24,128]{3,2,1,0:T(8,128)(2,1)S(1)}) custom-call(s32[2]{0:T(128)S(1)} %copy-done, bf16[8,120,128]{2,1,0:T(8,128)(2,1)S(1)} %collective-permute-done.3.cd0, bf16[8,120,128]{2,1,0:T(8,128)(2,1)S(1)} %collective-permute-done.6.cd1, bf16[1024,768]{1,0:T(8,128)(2,1)S(1)} %copy-done.2, ...), custom_call_target="tpu_custom_call" | custom-call | flops 12884901888 | bytes 1048576 | tf_op jit(solution)/shard_map/late/pallas_call | solution.py:452
  54.2 3.1 %collective-permute-start.7 = (s16[8,4,24,128]{3,2,1,0:T(8,128)(2,1)S(1)}, s16[8,4,24,128]{3,2,1,0:T(8,128)(2,1)S(1)}, u32[]{:S(2)}, u32[]{:S(2)}) collective-permute-start(s16[8,4,24,128]{3,2,1,0:T(8,128)(2,1)S(1)} %get-tuple-element.31), channel_id=1, source_target_pairs={{0,8},{1,9},{2,10},{3,11},{4,12},{5,13},{6,14},{7,15},{8,0},{9,1},... | collective-permute-start | bytes 589832 | tf_op jit(solution)/shard_map/ppermute | solution.py:612
  57.3 1.1 %collective-permute-done.7 = s16[8,4,24,128]{3,2,1,0:T(8,128)(2,1)S(1)} collective-permute-done((s16[8,4,24,128]{3,2,1,0:T(8,128)(2,1)S(1)}, s16[8,4,24,128]{3,2,1,0:T(8,128)(2,1)S(1)}, u32[]{:S(2)}, u32[]{:S(2)}) %collective-permute-start.7) | collective-permute-done | bytes 196640 | tf_op jit(solution)/shard_map/ppermute | solution.py:612
  58.4 19.7 %all_to_all.11 = s16[32,48,128]{2,1,0:T(8,128)(2,1)S(1)} all-to-all(s16[32,48,128]{2,1,0:T(8,128)(2,1)S(1)} %bitcast.10), channel_id=1, replica_groups={{0,2,4,6,16,18,20,22,32,34,36,38,48,50,52,54,64,66,68,70,80,82,84,86,96..., dimensions={0} | all-to-all | bytes 786432 | tf_op jit(solution)/shard_map/all_to_all | solution.py:615
  78.1 0.0 copy-done.1
  78.1 1.6 %join.1 = f32[128,128]{1,0:T(8,128)} custom-call(s16[8,4,48,128]{3,2,1,0:T(8,128)(2,1)S(1)} %bitcast.9, s32[1,128]{1,0:T(1,128)S(1)} %copy-done.1), custom_call_target="tpu_custom_call" | custom-call | tf_op jit(solution)/shard_map/join/pallas_call | solution.py:550
  (2 shorter events, 0.1 us)
Async XLA Ops:
  0.0 28.7 %copy-start.2 = (bf16[1024,768]{1,0:T(8,128)(2,1)S(1)}, bf16[1024,768]{1,0:T(8,128)(2,1)}, u32[]{:S(2)}) copy-start(bf16[1024,768]{1,0:T(8,128)(2,1)} %own.7) | copy-start | bytes 4718596
  0.0 22.6 %collective-permute-start = (bf16[1024,768]{1,0:T(8,128)(2,1)}, bf16[1024,768]{1,0:T(8,128)(2,1)S(1)}, u32[]{:S(2)}, u32[]{:S(2)}) collective-permute-start(bf16[1024,768]{1,0:T(8,128)(2,1)} %own.7), channel_id=1, source_target_pairs={{0,1},{1,0},{2,3},{3,2},{4,5},{5,4},{6,7},{7,6},{8,11},{9,10},{10,... | collective-permute-start | bytes 4718600 | tf_op jit(solution)/shard_map/ppermute | solution.py:594
  22.7 18.4 %collective-permute-start.5 = (bf16[8,120,128]{2,1,0:T(8,128)(2,1)S(1)}, bf16[8,120,128]{2,1,0:T(8,128)(2,1)S(1)}, u32[]{:S(2)}, u32[]{:S(2)}) collective-permute-start(bf16[8,120,128]{2,1,0:T(8,128)(2,1)S(1)} %get-tuple-element.33), channel_id=1, source_target_pairs={{0,4},{1,5},{2,6},{3,7},{4,0},{5,1},{6,2},{7,3},{8,12},{9,13},{10,... | collective-permute-start | bytes 737288 | tf_op jit(solution)/shard_map/ppermute | solution.py:602
  25.4 15.7 %collective-permute-start.4 = (bf16[8,120,128]{2,1,0:T(8,128)(2,1)S(1)}, bf16[8,120,128]{2,1,0:T(8,128)(2,1)S(1)}, u32[]{:S(2)}, u32[]{:S(2)}) collective-permute-start(bf16[8,120,128]{2,1,0:T(8,128)(2,1)S(1)} %get-tuple-element.33), channel_id=1, source_target_pairs={{0,2},{1,3},{2,0},{3,1},{4,6},{5,7},{6,4},{7,5},{8,10},{9,11},{10,... | collective-permute-start | bytes 737288 | tf_op jit(solution)/shard_map/ppermute | solution.py:602
  27.4 8.4 %collective-permute-start.2 = (bf16[8,120,128]{2,1,0:T(8,128)(2,1)S(1)}, bf16[8,120,128]{2,1,0:T(8,128)(2,1)S(1)}, u32[]{:S(2)}, u32[]{:S(2)}) collective-permute-start(bf16[8,120,128]{2,1,0:T(8,128)(2,1)S(1)} %get-tuple-element.34), channel_id=1, source_target_pairs={{0,4},{1,5},{2,6},{3,7},{4,0},{5,1},{6,2},{7,3},{8,12},{9,13},{10,... | collective-permute-start | bytes 737288 | tf_op jit(solution)/shard_map/ppermute | solution.py:602
  27.8 10.4 %collective-permute-start.1 = (bf16[8,120,128]{2,1,0:T(8,128)(2,1)S(1)}, bf16[8,120,128]{2,1,0:T(8,128)(2,1)S(1)}, u32[]{:S(2)}, u32[]{:S(2)}) collective-permute-start(bf16[8,120,128]{2,1,0:T(8,128)(2,1)S(1)} %get-tuple-element.34), channel_id=1, source_target_pairs={{0,2},{1,3},{2,0},{3,1},{4,6},{5,7},{6,4},{7,5},{8,10},{9,11},{10,... | collective-permute-start | bytes 737288 | tf_op jit(solution)/shard_map/ppermute | solution.py:602
  38.1 10.6 %collective-permute-start.3 = (bf16[8,120,128]{2,1,0:T(8,128)(2,1)S(1)}, bf16[8,120,128]{2,1,0:T(8,128)(2,1)S(1)}, u32[]{:S(2)}, u32[]{:S(2)}) collective-permute-start(bf16[8,120,128]{2,1,0:T(8,128)(2,1)S(1)} %collective-permute-done.1.half0.cx0), channel_id=1, source_target_pairs={{0,4},{1,5},{2,6},{3,7},{4,0},{5,1},{6,2},{7,3},{8,12},{9,13},{10,... | collective-permute-start | bytes 737288 | tf_op jit(solution)/shard_map/ppermute | solution.py:606
  41.1 7.6 %copy-start = (s32[2]{0:T(128)S(1)}, s32[2]{0:T(128)}, u32[]{:S(2)}) copy-start(s32[2]{0:T(128)} %pad_add_fusion.at) | copy-start | bytes 28
  41.1 7.5 %collective-permute-start.6 = (bf16[8,120,128]{2,1,0:T(8,128)(2,1)S(1)}, bf16[8,120,128]{2,1,0:T(8,128)(2,1)S(1)}, u32[]{:S(2)}, u32[]{:S(2)}) collective-permute-start(bf16[8,120,128]{2,1,0:T(8,128)(2,1)S(1)} %collective-permute-done.5.cy1), channel_id=1, source_target_pairs={{0,2},{1,3},{2,0},{3,1},{4,6},{5,7},{6,4},{7,5},{8,10},{9,11},{10,... | collective-permute-start | bytes 737288 | tf_op jit(solution)/shard_map/ppermute | solution.py:609
  48.7 29.4 %copy-start.1 = (s32[1,128]{1,0:T(1,128)S(1)}, s32[1,128]{1,0:T(1,128)}, u32[]{:S(2)}) copy-start(s32[1,128]{1,0:T(1,128)} %get-tuple-element.32.slots) | copy-start | bytes 1540
  54.2 4.2 %collective-permute-start.7 = (s16[8,4,24,128]{3,2,1,0:T(8,128)(2,1)S(1)}, s16[8,4,24,128]{3,2,1,0:T(8,128)(2,1)S(1)}, u32[]{:S(2)}, u32[]{:S(2)}) collective-permute-start(s16[8,4,24,128]{3,2,1,0:T(8,128)(2,1)S(1)} %get-tuple-element.31), channel_id=1, source_target_pairs={{0,8},{1,9},{2,10},{3,11},{4,12},{5,13},{6,14},{7,15},{8,0},{9,1},... | collective-permute-start | bytes 589832 | tf_op jit(solution)/shard_map/ppermute | solution.py:612

commit v9 on v8

--- a/solution.py
+++ b/solution.py
@@ -306,13 +306,22 @@
     return jnp.concatenate([found[c * many : (c + 1) * many, :] for c in range(COLS)], axis=1)
 
 
-def first_kernel(chunk, own, far, out, rows, *work):
+def first_kernel(chunk, own, far_in, out, far, rows, sem, *work):
+    copy = pltpu.make_async_copy(far_in, far, sem)
+    copy.start()
     rows[...] = main_rows(chunk)
+    waited = []
+
+    def partner():
+        if not waited:
+            copy.wait()
+            waited.append(True)
+        return far
 
     def emit(g, half, value):
         out[half * Q : (half + 1) * Q, :] = value
 
-    leaders([(2, lambda: rows[...])], lambda: own, lambda: far, *work, emit=emit)
+    leaders([(2, lambda: rows[...])], lambda: own, partner, *work, emit=emit)
 
 
 def early_kernel(half0, half1, own, far, out, rows, *work):
@@ -412,10 +421,13 @@
 def first(chunk, own, far):
     return pl.pallas_call(
         first_kernel,
-        out_shape=jax.ShapeDtypeStruct((256, TOPK), jnp.float32),
-        in_specs=[VMEM] * 3,
-        out_specs=VMEM,
-        scratch_shapes=[pltpu.VMEM((256, WIDTH), jnp.bfloat16)] + WORK,
+        out_shape=(
+            jax.ShapeDtypeStruct((256, TOPK), jnp.float32),
+            jax.ShapeDtypeStruct((1024, WIDTH), jnp.bfloat16),
+        ),
+        in_specs=[VMEM, VMEM, pl.BlockSpec(memory_space=pl.ANY)],
+        out_specs=(VMEM, VMEM),
+        scratch_shapes=[pltpu.VMEM((256, WIDTH), jnp.bfloat16), pltpu.SemaphoreType.DMA] + WORK,
         compiler_params=LIMIT,
         cost_estimate=pl.CostEstimate(flops=COST, bytes_accessed=1 << 20, transcendentals=0),
         name="first",
@@ -469,7 +481,7 @@
     )(at, *halves, own, far, *results)
 
 
-def outbox_kernel(at, queries_in, routes_in, out, slots, queries, routes, sems):
+def outbox_kernel(queries_in, routes_in, out, slots, queries, routes, sems):
     copies = (
         pltpu.make_async_copy(routes_in, routes, sems.at[0]),
         pltpu.make_async_copy(queries_in, queries, sems.at[1]),
@@ -486,7 +498,8 @@
     earlier = jnp.where(before & (along == down), 1.0, 0.0)
     rank = jnp.sum(earlier, axis=0, keepdims=True).astype(jnp.int32)
     lang = routes[...]
-    slots[...] = (lang ^ at[1]) * ROWS + rank
+    for side in range(2):
+        slots[side] = (lang ^ side) * ROWS + rank
     main_at = jnp.where(rank < MAIN, lang * MAIN + rank, -1)
     hits = lax.broadcasted_iota(jnp.int32, (LANGS * MAIN, Q), 0) == jnp.broadcast_to(main_at, (LANGS * MAIN, Q))
     picks = jnp.where(hits, 1.0, 0.0).astype(jnp.bfloat16)
@@ -506,14 +519,14 @@
     out[:, MAIN * COLS : SENT, :] = tail.astype(jnp.bfloat16).reshape(LANGS, each, 128)
 
 
-def outbox_of(at, queries, routes):
+def outbox_of(queries, routes):
     return pl.pallas_call(
         outbox_kernel,
         out_shape=(
             jax.ShapeDtypeStruct((LANGS, SENT, 128), jnp.bfloat16),
-            jax.ShapeDtypeStruct((1, Q), jnp.int32),
+            jax.ShapeDtypeStruct((2, 1, Q), jnp.int32),
         ),
-        in_specs=[pl.BlockSpec(memory_space=pltpu.SMEM)] + [pl.BlockSpec(memory_space=pltpu.HBM)] * 2,
+        in_specs=[pl.BlockSpec(memory_space=pltpu.HBM)] * 2,
         out_specs=(VMEM, VMEM),
         scratch_shapes=[
             pltpu.VMEM((Q, WIDTH), jnp.bfloat16),
@@ -522,12 +535,12 @@
         ],
         compiler_params=pltpu.CompilerParams(vmem_limit_bytes=60 << 20),
         name="outbox",
-    )(at, queries, routes)
-
-
-def join_kernel(back, slots, out, a, b):
+    )(queries, routes)
+
+
+def join_kernel(at, back, slots, out, a, b):
     total = LANGS * ROWS
-    hits = lax.broadcasted_iota(jnp.int32, (total, Q), 0) == jnp.broadcast_to(slots[...], (total, Q))
+    hits = lax.broadcasted_iota(jnp.int32, (total, Q), 0) == jnp.broadcast_to(slots[at[1]], (total, Q))
     picks = jnp.where(hits, 1.0, 0.0)
     picks = jnp.concatenate([picks[i * Q : (i + 1) * Q, :].T for i in range(total // Q)], axis=1)
     picks = picks.astype(jnp.bfloat16)
@@ -546,16 +559,16 @@
     out[...] = a[pl.ds(0, TOPK, stride=8), :].T
 
 
-def join(back, slots):
+def join(at, back, slots):
     return pl.pallas_call(
         join_kernel,
         out_shape=jax.ShapeDtypeStruct((Q, TOPK), jnp.float32),
-        in_specs=[VMEM] * 2,
+        in_specs=[pl.BlockSpec(memory_space=pltpu.SMEM)] + [VMEM] * 2,
         out_specs=VMEM,
         scratch_shapes=[pltpu.VMEM((128 * 8, 128), jnp.float32)] * 2,
         compiler_params=LIMIT,
         name="join",
-    )(back, slots)
+    )(at, back, slots)
 
 
 AXES = ("lang", "shard")
@@ -592,28 +605,27 @@
 
 def shards(queries, routes, corpus):
     far = lax.ppermute(corpus, AXES, moves(pair))
-    shard, core = lax.axis_index("shard"), lax.axis_index("lang") & 1
-    seat = lax.shift_right_logical(shard, 2) * 2 + (lax.shift_right_logical(shard, 1) & 1)
-    at = jnp.stack([seat, core])
-    outbox, slots = outbox_of(at, queries, routes.reshape(1, Q))
+    outbox, slots = outbox_of(queries, routes.reshape(1, Q))
     mine = lax.all_to_all(outbox, "lang", split_axis=0, concat_axis=0, tiled=True)
-    mine, far = lax.optimization_barrier((mine, far))
     cx0, cy0, cx1, cy1 = (
         lax.ppermute(part, AXES, moves(over)) for part in (mine[:8], mine[8:]) for over in (over_x, over_y)
     )
-    r0 = first(mine, corpus, far)
+    r0, far = first(mine, corpus, far)
     cx0, cy0, r0 = lax.optimization_barrier((cx0, cy0, r0))
     cd0 = lax.ppermute(cx0, AXES, moves(over_y))
     r1 = early(cx0, cy0, corpus, far)
     cx1, cy1, r1 = lax.optimization_barrier((cx1, cy1, r1))
     cd1 = lax.ppermute(cy1, AXES, moves(over_x))
     r2, tails = middle(mine, (cx0, cx1, cy0, cy1), corpus, far)
+    shard, core = lax.axis_index("shard"), lax.axis_index("lang") & 1
+    seat = lax.shift_right_logical(shard, 2) * 2 + (lax.shift_right_logical(shard, 1) & 1)
+    at = jnp.stack([seat, core])
     keep, give = late(at, (cd0, cd1), corpus, far, (r0, r1, r2, tails))
     other = lax.ppermute(give, AXES, [(d, d ^ 8) for d in range(128)])
     sent = lax.dynamic_update_slice(keep, other[:, :, None], (0, 0, 1, 0, 0))
     sent = sent.reshape(LANGS * 2, 2 * ROWS, TOPK)
     back = lax.all_to_all(sent, AXES, 0, 0, axis_index_groups=TEAMS, tiled=True)
-    return join(back.reshape(LANGS // 2, 4, 2 * ROWS, TOPK), slots)
+    return join(at, back.reshape(LANGS // 2, 4, 2 * ROWS, TOPK), slots)
 
 
 def solution(mesh):

time: 80.6 us -> 76.8 us (0.953)
  the two profiles are of different devices: /device:TPU:1 before, /device:TPU:2 now
where the time goes in v9:
time: 76.8 us; the launch traced here: 76.5 us
  blocking collectives  21.2 us (28%)
  Pallas kernels  21.1 us (27%)
  starting transfers between devices  19 us (25%)
  waiting for transfers between devices  15 us (20%)
    all_to_all x1, blocking collectives, shards(): back = lax.all_to_all(sent, AXES, 0, 0, axis_index_groups=TEAMS, tiled=True)  21.2 us
    all_to_all x1, waiting for transfers between devices, shards(): lax.all_to_all(outbox, 'lang', split_axis=0, concat_axis=0, tiled=True)  10.4 us
    ppermute x4, starting transfers between devices, shards(): lax.ppermute(part, AXES, moves(over))  7.14 us
    all_to_all x1, starting transfers between devices, shards(): lax.all_to_all(outbox, 'lang', split_axis=0, concat_axis=0, tiled=True)  6.62 us
    pallas_call x1, Pallas kernels, late(): pl.pallas_call(late_kernel, out_shape=(jax.ShapeDtypeStruct((LANGS // 2,...  5.46 us
    pallas_call x1, Pallas kernels, middle(): pl.pallas_call(middle_kernel, out_shape=[jax.ShapeDtypeStruct((256, TOPK)...  4.99 us
    pallas_call x1, Pallas kernels, first(): pl.pallas_call(first_kernel, out_shape=(jax.ShapeDtypeStruct((256, TOPK),...  3.53 us
    ppermute x1, starting transfers between devices, shards(): cd0 = lax.ppermute(cx0, AXES, moves(over_y))  3.21 us
  transfers between devices with their start and end apart: 9, of which 4 were waited for; matrix products, arithmetic and copies ran while one was open for 0% of the time, Pallas kernels for 18%

profile of v9, /device:TPU:2, one launch (start us, length us, event | category | flops | bytes accessed | tf_op | source)
XLA Modules:
  0.0 76.5 jit_solution(6401284725016682140)
XLA Ops:
  0.0 0.0 copy-start.1
  0.0 0.4 collective-permute-start.2
  0.4 2.4 %outbox.1 = (bf16[16,120,128]{2,1,0:T(8,128)(2,1)}, s32[2,1,128]{2,1,0:T(1,128)}) custom-call(bf16[128,768]{1,0:T(8,128)(2,1)} %queries_in.1, s32[1,128]{1,0:T(1,128)} %bitcast.11), custom_call_target="tpu_custom_call" | custom-call | tf_op jit(solution)/shard_map/outbox/pallas_call | solution.py:523
  2.8 6.6 %all-to-all-start = ((bf16[16,120,128]{2,1,0:T(8,128)(2,1)}), bf16[16,120,128]{2,1,0:T(8,128)(2,1)S(1)}, u32[]{:S(2)}, u32[]{:S(2)}) async-start(bf16[16,120,128]{2,1,0:T(8,128)(2,1)} %get-tuple-element.19), calls=%async_computation | async-start | bytes 983040 | tf_op jit(solution)/shard_map/all_to_all | solution.py:609
  9.4 0.1 pad_add_fusion.at
  9.5 10.4 %all-to-all-done.chunk.mine = bf16[16,120,128]{2,1,0:T(8,128)(2,1)S(1)} async-done(((bf16[16,120,128]{2,1,0:T(8,128)(2,1)}), bf16[16,120,128]{2,1,0:T(8,128)(2,1)S(1)}, u32[]{:S(2)}, u32[]{:S(2)}) %all-to-all-start) | async-done | bytes 491552 | tf_op jit(solution)/shard_map/all_to_all | solution.py:609
  19.9 2.4 %collective-permute-start = (bf16[8,120,128]{2,1,0:T(8,128)(2,1)S(1)}, bf16[8,120,128]{2,1,0:T(8,128)(2,1)S(1)}, u32[]{:S(2)}, u32[]{:S(2)}) collective-permute-start(bf16[8,120,128]{2,1,0:T(8,128)(2,1)S(1)} %get-tuple-element.34), channel_id=1, source_target_pairs={{0,2},{1,3},{2,0},{3,1},{4,6},{5,7},{6,4},{7,5},{8,10},{9,11},{10,... | collective-permute-start | bytes 737288 | tf_op jit(solution)/shard_map/ppermute | solution.py:611
  22.3 2.9 %collective-permute-start.1 = (bf16[8,120,128]{2,1,0:T(8,128)(2,1)S(1)}, bf16[8,120,128]{2,1,0:T(8,128)(2,1)S(1)}, u32[]{:S(2)}, u32[]{:S(2)}) collective-permute-start(bf16[8,120,128]{2,1,0:T(8,128)(2,1)S(1)} %get-tuple-element.34), channel_id=1, source_target_pairs={{0,4},{1,5},{2,6},{3,7},{4,0},{5,1},{6,2},{7,3},{8,12},{9,13},{10,... | collective-permute-start | bytes 737288 | tf_op jit(solution)/shard_map/ppermute | solution.py:611
  25.2 1.2 %collective-permute-start.4 = (bf16[8,120,128]{2,1,0:T(8,128)(2,1)S(1)}, bf16[8,120,128]{2,1,0:T(8,128)(2,1)S(1)}, u32[]{:S(2)}, u32[]{:S(2)}) collective-permute-start(bf16[8,120,128]{2,1,0:T(8,128)(2,1)S(1)} %get-tuple-element.33), channel_id=1, source_target_pairs={{0,2},{1,3},{2,0},{3,1},{4,6},{5,7},{6,4},{7,5},{8,10},{9,11},{10,... | collective-permute-start | bytes 737288 | tf_op jit(solution)/shard_map/ppermute | solution.py:611
  26.5 0.6 collective-permute-start.5
  27.1 0.0 collective-permute-done.2.far_in
  27.1 0.0 copy-done.1
  27.1 3.5 %first.1 = (f32[256,128]{1,0:T(8,128)S(1)}, bf16[1024,768]{1,0:T(8,128)(2,1)S(1)}) custom-call(bf16[16,120,128]{2,1,0:T(8,128)(2,1)S(1)} %all-to-all-done.chunk.mine, bf16[1024,768]{1,0:T(8,128)(2,1)S(1)} %copy-done.1, bf16[1024,768]{1,0:T(8,128)(2,1)} %collective-permute-done.2.far_in), custom_call_target="tpu_custom_call" | custom-call | flops 6442450944 | bytes 1048576 | tf_op jit(solution)/shard_map/first/pallas_call | solution.py:422
  30.6 0.0 collective-permute-done.half0.cx0
  30.6 1.7 %collective-permute-done.1.half1.cy0 = bf16[8,120,128]{2,1,0:T(8,128)(2,1)S(1)} collective-permute-done((bf16[8,120,128]{2,1,0:T(8,128)(2,1)S(1)}, bf16[8,120,128]{2,1,0:T(8,128)(2,1)S(1)}, u32[]{:S(2)}, u32[]{:S(2)}) %collective-permute-start.1) | collective-permute-done | bytes 245792 | tf_op jit(solution)/shard_map/ppermute | solution.py:611
  32.4 3.2 %collective-permute-start.3 = (bf16[8,120,128]{2,1,0:T(8,128)(2,1)S(1)}, bf16[8,120,128]{2,1,0:T(8,128)(2,1)S(1)}, u32[]{:S(2)}, u32[]{:S(2)}) collective-permute-start(bf16[8,120,128]{2,1,0:T(8,128)(2,1)S(1)} %collective-permute-done.half0.cx0), channel_id=1, source_target_pairs={{0,4},{1,5},{2,6},{3,7},{4,0},{5,1},{6,2},{7,3},{8,12},{9,13},{10,... | collective-permute-start | bytes 737288 | tf_op jit(solution)/shard_map/ppermute | solution.py:615
  35.6 2.6 %early.1.r1 = f32[256,128]{1,0:T(8,128)S(1)} custom-call(bf16[8,120,128]{2,1,0:T(8,128)(2,1)S(1)} %collective-permute-done.half0.cx0, bf16[8,120,128]{2,1,0:T(8,128)(2,1)S(1)} %collective-permute-done.1.half1.cy0, bf16[1024,768]{1,0:T(8,128)(2,1)S(1)} %copy-done.1, bf16[1024,768]{1,0:T(8,128)(2,1)S(1)} %get-tuple-element.23.far), custom_call_target="tpu_custom_call" | custom-call | flops 6442450944 | bytes 1048576 | tf_op jit(solution)/shard_map/early/pallas_call | solution.py:438
  38.1 0.0 collective-permute-done.4.cx1
  38.1 0.0 collective-permute-done.5.cy1
  38.1 1.5 %collective-permute-start.6 = (bf16[8,120,128]{2,1,0:T(8,128)(2,1)S(1)}, bf16[8,120,128]{2,1,0:T(8,128)(2,1)S(1)}, u32[]{:S(2)}, u32[]{:S(2)}) collective-permute-start(bf16[8,120,128]{2,1,0:T(8,128)(2,1)S(1)} %collective-permute-done.5.cy1), channel_id=1, source_target_pairs={{0,2},{1,3},{2,0},{3,1},{4,6},{5,7},{6,4},{7,5},{8,10},{9,11},{10,... | collective-permute-start | bytes 737288 | tf_op jit(solution)/shard_map/ppermute | solution.py:618
  39.6 5.0 %middle.1 = (f32[256,128]{1,0:T(8,128)S(1)}, f32[256,128]{1,0:T(8,128)S(1)}) custom-call(bf16[16,120,128]{2,1,0:T(8,128)(2,1)S(1)} %all-to-all-done.chunk.mine, bf16[8,120,128]{2,1,0:T(8,128)(2,1)S(1)} %collective-permute-done.half0.cx0, bf16[8,120,128]{2,1,0:T(8,128)(2,1)S(1)} %collective-permute-done.4.cx1, ...), custom_call_target="tpu_custom_call" | custom-call | flops 12884901888 | bytes 1048576 | tf_op jit(solution)/shard_map/middle/pallas_call | solution.py:451
  44.6 1.5 %collective-permute-done.6.cd1 = bf16[8,120,128]{2,1,0:T(8,128)(2,1)S(1)} collective-permute-done((bf16[8,120,128]{2,1,0:T(8,128)(2,1)S(1)}, bf16[8,120,128]{2,1,0:T(8,128)(2,1)S(1)}, u32[]{:S(2)}, u32[]{:S(2)}) %collective-permute-start.6) | collective-permute-done | bytes 245792 | tf_op jit(solution)/shard_map/ppermute | solution.py:618
  46.1 0.0 collective-permute-done.3.cd0
  46.1 0.0 copy-start
  46.1 5.5 %late.1 = (s16[8,4,2,24,128]{4,3,2,1,0:T(8,128)(2,1)S(1)}, s16[8,4,24,128]{3,2,1,0:T(8,128)(2,1)S(1)}) custom-call(s32[2]{0:T(128)S(1)} %pad_add_fusion.at, bf16[8,120,128]{2,1,0:T(8,128)(2,1)S(1)} %collective-permute-done.3.cd0, bf16[8,120,128]{2,1,0:T(8,128)(2,1)S(1)} %collective-permute-done.6.cd1, bf16[1024,768]{1,0:T(8,128)(2,1)S(1)} %copy-done.1, ...), custom_call_target="tpu_custom_call" | custom-call | flops 12884901888 | bytes 1048576 | tf_op jit(solution)/shard_map/late/pallas_call | solution.py:464
  51.6 0.1 collective-permute-start.7
  51.7 1.4 %collective-permute-done.7 = s16[8,4,24,128]{3,2,1,0:T(8,128)(2,1)S(1)} collective-permute-done((s16[8,4,24,128]{3,2,1,0:T(8,128)(2,1)S(1)}, s16[8,4,24,128]{3,2,1,0:T(8,128)(2,1)S(1)}, u32[]{:S(2)}, u32[]{:S(2)}) %collective-permute-start.7) | collective-permute-done | bytes 196640 | tf_op jit(solution)/shard_map/ppermute | solution.py:624
  53.1 21.2 %all_to_all.10 = s16[32,48,128]{2,1,0:T(8,128)(2,1)S(1)} all-to-all(s16[32,48,128]{2,1,0:T(8,128)(2,1)S(1)} %bitcast.10), channel_id=1, replica_groups={{0,2,4,6,16,18,20,22,32,34,36,38,48,50,52,54,64,66,68,70,80,82,84,86,96..., dimensions={0} | all-to-all | bytes 786432 | tf_op jit(solution)/shard_map/all_to_all | solution.py:627
  74.3 0.0 copy-done
  74.3 2.2 %join.1 = f32[128,128]{1,0:T(8,128)} custom-call(s32[2]{0:T(128)S(1)} %pad_add_fusion.at, s16[8,4,48,128]{3,2,1,0:T(8,128)(2,1)S(1)} %bitcast.9, s32[2,1,128]{2,1,0:T(1,128)S(1)} %copy-done), custom_call_target="tpu_custom_call" | custom-call | tf_op jit(solution)/shard_map/join/pallas_call | solution.py:563
  (2 shorter events, 0.1 us)
Async XLA Ops:
  0.0 27.1 %copy-start.1 = (bf16[1024,768]{1,0:T(8,128)(2,1)S(1)}, bf16[1024,768]{1,0:T(8,128)(2,1)}, u32[]{:S(2)}) copy-start(bf16[1024,768]{1,0:T(8,128)(2,1)} %own.7) | copy-start | bytes 4718596
  0.0 27.1 %collective-permute-start.2 = (bf16[1024,768]{1,0:T(8,128)(2,1)}, bf16[1024,768]{1,0:T(8,128)(2,1)}, u32[]{:S(2)}, u32[]{:S(2)}) collective-permute-start(bf16[1024,768]{1,0:T(8,128)(2,1)} %own.7), channel_id=1, source_target_pairs={{0,1},{1,0},{2,3},{3,2},{4,5},{5,4},{6,7},{7,6},{8,11},{9,10},{10,... | collective-permute-start | bytes 4718600 | tf_op jit(solution)/shard_map/ppermute | solution.py:607
  2.8 17.1 %all-to-all-start = ((bf16[16,120,128]{2,1,0:T(8,128)(2,1)}), bf16[16,120,128]{2,1,0:T(8,128)(2,1)S(1)}, u32[]{:S(2)}, u32[]{:S(2)}) async-start(bf16[16,120,128]{2,1,0:T(8,128)(2,1)} %get-tuple-element.19), calls=%async_computation | async-start | bytes 983040 | tf_op jit(solution)/shard_map/all_to_all | solution.py:609
  19.9 10.7 %collective-permute-start = (bf16[8,120,128]{2,1,0:T(8,128)(2,1)S(1)}, bf16[8,120,128]{2,1,0:T(8,128)(2,1)S(1)}, u32[]{:S(2)}, u32[]{:S(2)}) collective-permute-start(bf16[8,120,128]{2,1,0:T(8,128)(2,1)S(1)} %get-tuple-element.34), channel_id=1, source_target_pairs={{0,2},{1,3},{2,0},{3,1},{4,6},{5,7},{6,4},{7,5},{8,10},{9,11},{10,... | collective-permute-start | bytes 737288 | tf_op jit(solution)/shard_map/ppermute | solution.py:611
  22.3 10.0 %collective-permute-start.1 = (bf16[8,120,128]{2,1,0:T(8,128)(2,1)S(1)}, bf16[8,120,128]{2,1,0:T(8,128)(2,1)S(1)}, u32[]{:S(2)}, u32[]{:S(2)}) collective-permute-start(bf16[8,120,128]{2,1,0:T(8,128)(2,1)S(1)} %get-tuple-element.34), channel_id=1, source_target_pairs={{0,4},{1,5},{2,6},{3,7},{4,0},{5,1},{6,2},{7,3},{8,12},{9,13},{10,... | collective-permute-start | bytes 737288 | tf_op jit(solution)/shard_map/ppermute | solution.py:611
  25.2 12.9 %collective-permute-start.4 = (bf16[8,120,128]{2,1,0:T(8,128)(2,1)S(1)}, bf16[8,120,128]{2,1,0:T(8,128)(2,1)S(1)}, u32[]{:S(2)}, u32[]{:S(2)}) collective-permute-start(bf16[8,120,128]{2,1,0:T(8,128)(2,1)S(1)} %get-tuple-element.33), channel_id=1, source_target_pairs={{0,2},{1,3},{2,0},{3,1},{4,6},{5,7},{6,4},{7,5},{8,10},{9,11},{10,... | collective-permute-start | bytes 737288 | tf_op jit(solution)/shard_map/ppermute | solution.py:611
  26.5 11.7 %collective-permute-start.5 = (bf16[8,120,128]{2,1,0:T(8,128)(2,1)S(1)}, bf16[8,120,128]{2,1,0:T(8,128)(2,1)S(1)}, u32[]{:S(2)}, u32[]{:S(2)}) collective-permute-start(bf16[8,120,128]{2,1,0:T(8,128)(2,1)S(1)} %get-tuple-element.33), channel_id=1, source_target_pairs={{0,4},{1,5},{2,6},{3,7},{4,0},{5,1},{6,2},{7,3},{8,12},{9,13},{10,... | collective-permute-start | bytes 737288 | tf_op jit(solution)/shard_map/ppermute | solution.py:611
  32.4 13.8 %collective-permute-start.3 = (bf16[8,120,128]{2,1,0:T(8,128)(2,1)S(1)}, bf16[8,120,128]{2,1,0:T(8,128)(2,1)S(1)}, u32[]{:S(2)}, u32[]{:S(2)}) collective-permute-start(bf16[8,120,128]{2,1,0:T(8,128)(2,1)S(1)} %collective-permute-done.half0.cx0), channel_id=1, source_target_pairs={{0,4},{1,5},{2,6},{3,7},{4,0},{5,1},{6,2},{7,3},{8,12},{9,13},{10,... | collective-permute-start | bytes 737288 | tf_op jit(solution)/shard_map/ppermute | solution.py:615
  38.1 8.0 %collective-permute-start.6 = (bf16[8,120,128]{2,1,0:T(8,128)(2,1)S(1)}, bf16[8,120,128]{2,1,0:T(8,128)(2,1)S(1)}, u32[]{:S(2)}, u32[]{:S(2)}) collective-permute-start(bf16[8,120,128]{2,1,0:T(8,128)(2,1)S(1)} %collective-permute-done.5.cy1), channel_id=1, source_target_pairs={{0,2},{1,3},{2,0},{3,1},{4,6},{5,7},{6,4},{7,5},{8,10},{9,11},{10,... | collective-permute-start | bytes 737288 | tf_op jit(solution)/shard_map/ppermute | solution.py:618
  46.1 28.2 %copy-start = (s32[2,1,128]{2,1,0:T(1,128)S(1)}, s32[2,1,128]{2,1,0:T(1,128)}, u32[]{:S(2)}) copy-start(s32[2,1,128]{2,1,0:T(1,128)} %get-tuple-element.32.slots) | copy-start | bytes 3076
  51.6 1.5 %collective-permute-start.7 = (s16[8,4,24,128]{3,2,1,0:T(8,128)(2,1)S(1)}, s16[8,4,24,128]{3,2,1,0:T(8,128)(2,1)S(1)}, u32[]{:S(2)}, u32[]{:S(2)}) collective-permute-start(s16[8,4,24,128]{3,2,1,0:T(8,128)(2,1)S(1)} %get-tuple-element.31), channel_id=1, source_target_pairs={{0,8},{1,9},{2,10},{3,11},{4,12},{5,13},{6,14},{7,15},{8,0},{9,1},... | collective-permute-start | bytes 589832 | tf_op jit(solution)/shard_map/ppermute | solution.py:624

commit v10 on v7

--- a/solution.py
+++ b/solution.py
@@ -381,7 +381,7 @@
         [(2, lambda: rows[0:256, :]), (1, lambda: rows[256:384, :])], lambda: own, lambda: far, *work, emit=emit
     )
     me = at[0]
-    owner = (me, me ^ 1, me ^ 2, me ^ 3)
+    owner = (me, me ^ 2, me ^ 1, me ^ 3)
     none = jnp.zeros((ROWS - CAP, TOPK), jnp.float32)
     for k in range(4):
         for lang in range(LANGS):
@@ -400,7 +400,7 @@
             else:
                 box[k, MAIN:CAP, :] = last[256 + lang * TAIL : 256 + (lang + 1) * TAIL, :]
             box[k, CAP:ROWS, :] = none
-            out[lang, owner[k]] = coded(box[k]).astype(jnp.int32).astype(jnp.int16)
+            out[lang % 2, owner[k], lang // 2] = coded(box[k]).astype(jnp.int32).astype(jnp.int16)
 
 
 COST = 2 * 256 * 2048 * 768 * 8
@@ -458,7 +458,7 @@
 def late(at, halves, own, far, results):
     return pl.pallas_call(
         late_kernel,
-        out_shape=jax.ShapeDtypeStruct((LANGS, 4, ROWS, TOPK), jnp.int16),
+        out_shape=jax.ShapeDtypeStruct((2, 4, LANGS // 2, ROWS, TOPK), jnp.int16),
         in_specs=[pl.BlockSpec(memory_space=pltpu.SMEM)] + [VMEM] * 8,
         out_specs=VMEM,
         scratch_shapes=[
@@ -490,7 +490,7 @@
     earlier = jnp.where(before & (along == down), 1.0, 0.0)
     rank = jnp.sum(earlier, axis=0, keepdims=True).astype(jnp.int32)
     lang = routes[...]
-    slots[...] = lang * ROWS + rank
+    slots[...] = ((lang & 1) * (LANGS // 2) + lax.shift_right_logical(lang, 1)) * ROWS + rank
     main_at = jnp.where(rank < MAIN, lang * MAIN + rank, -1)
     hits = lax.broadcasted_iota(jnp.int32, (LANGS * MAIN, Q), 0) == jnp.broadcast_to(main_at, (LANGS * MAIN, Q))
     picks = jnp.where(hits, 1.0, 0.0).astype(jnp.bfloat16)
@@ -588,7 +588,13 @@
 
 
 TEAMS = [
-    [lang * 8 + y * 4 + odd + 2 * half for lang in range(16) for y in range(2) for half in range(2)]
+    [
+        (pair * 2 + core) * 8 + y * 4 + odd + 2 * half
+        for core in range(2)
+        for half in range(2)
+        for y in range(2)
+        for pair in range(8)
+    ]
     for odd in range(2)
 ]
 
@@ -608,12 +614,12 @@
     cd1 = lax.ppermute(cy1, AXES, moves(over_x))
     r2, tails = middle(mine, (cx0, cx1, cy0, cy1), corpus, far)
     shard = lax.axis_index("shard")
-    at = (lax.shift_right_logical(shard, 2) * 2 + (lax.shift_right_logical(shard, 1) & 1)).reshape(1)
+    at = (lax.shift_right_logical(shard, 2) + (shard & 2)).reshape(1)
     found = late(at, (cd0, cd1), corpus, far, (r0, r1, r2, tails))
     back = lax.all_to_all(
         found.reshape(LANGS * 4, ROWS, TOPK), AXES, 0, 0, axis_index_groups=TEAMS, tiled=True
     )
-    return join(back.reshape(LANGS, 4, ROWS, TOPK), slots)
+    return join(back.reshape(2, 4, LANGS // 2, ROWS, TOPK), slots)
 
 
 def solution(mesh):

time: 74.3 us -> 74.8 us (level)
  no operation moved by 1% of the time
where the time goes in v10:
time: 74.8 us; the launch traced here: 73.5 us
  blocking collectives  23.4 us (31%)
  starting transfers between devices  20.5 us (27%)
  Pallas kernels  19.9 us (27%)
  waiting for transfers between devices  9.61 us (13%)
    all_to_all x1, blocking collectives, shards(): lax.all_to_all(found.reshape(LANGS * 4, ROWS, TOPK), AXES, 0, 0, axis_ind...  23.4 us
    all_to_all x1, waiting for transfers between devices, shards(): lax.all_to_all(outbox, 'lang', split_axis=0, concat_axis=0, tiled=True)  9.31 us
    all_to_all x1, starting transfers between devices, shards(): lax.all_to_all(outbox, 'lang', split_axis=0, concat_axis=0, tiled=True)  6.46 us
    ppermute x4, starting transfers between devices, shards(): lax.ppermute(part, AXES, moves(over))  6.02 us
    pallas_call x1, Pallas kernels, middle(): pl.pallas_call(middle_kernel, out_shape=[jax.ShapeDtypeStruct((256, TOPK)...  4.99 us
    pallas_call x1, Pallas kernels, late(): pl.pallas_call(late_kernel, out_shape=jax.ShapeDtypeStruct((2, 4, LANGS /...  4.88 us
    pallas_call x1, Pallas kernels, first(): pl.pallas_call(first_kernel, out_shape=(jax.ShapeDtypeStruct((256, TOPK),...  3.53 us
    ppermute x1, starting transfers between devices, shards(): far = lax.ppermute(corpus, AXES, moves(pair))  3.3 us
  transfers between devices with their start and end apart: 8, of which 2 were waited for; matrix products, arithmetic and copies ran while one was open for 0% of the time, Pallas kernels for 18%

profile of v10, /device:TPU:1, one launch (start us, length us, event | category | flops | bytes accessed | tf_op | source)
XLA Modules:
  0.0 73.5 jit_solution(12250006285104820554)
XLA Ops:
  0.0 0.0 copy-start.1
  0.0 3.3 %collective-permute-start.2 = (bf16[1024,768]{1,0:T(8,128)(2,1)}, bf16[1024,768]{1,0:T(8,128)(2,1)}, u32[]{:S(2)}, u32[]{:S(2)}) collective-permute-start(bf16[1024,768]{1,0:T(8,128)(2,1)} %own.7), channel_id=1, source_target_pairs={{0,1},{1,0},{2,3},{3,2},{4,5},{5,4},{6,7},{7,6},{8,11},{9,10},{10,... | collective-permute-start | bytes 4718600 | tf_op jit(solution)/shard_map/ppermute | solution.py:603
  3.3 2.3 %outbox.1 = (bf16[16,120,128]{2,1,0:T(8,128)(2,1)}, s32[1,128]{1,0:T(1,128)}) custom-call(bf16[128,768]{1,0:T(8,128)(2,1)} %queries_in.1, s32[1,128]{1,0:T(1,128)} %bitcast.6), custom_call_target="tpu_custom_call" | custom-call | tf_op jit(solution)/shard_map/outbox/pallas_call | solution.py:514
  5.6 6.5 %all-to-all-start = ((bf16[16,120,128]{2,1,0:T(8,128)(2,1)}), bf16[16,120,128]{2,1,0:T(8,128)(2,1)S(1)}, u32[]{:S(2)}, u32[]{:S(2)}) async-start(bf16[16,120,128]{2,1,0:T(8,128)(2,1)} %get-tuple-element.17), calls=%async_computation | async-start | bytes 983040 | tf_op jit(solution)/shard_map/all_to_all | solution.py:605
  12.1 9.3 %all-to-all-done.chunk.mine = bf16[16,120,128]{2,1,0:T(8,128)(2,1)S(1)} async-done(((bf16[16,120,128]{2,1,0:T(8,128)(2,1)}), bf16[16,120,128]{2,1,0:T(8,128)(2,1)S(1)}, u32[]{:S(2)}, u32[]{:S(2)}) %all-to-all-start) | async-done | bytes 491552 | tf_op jit(solution)/shard_map/all_to_all | solution.py:605
  21.4 2.1 %collective-permute-start = (bf16[8,120,128]{2,1,0:T(8,128)(2,1)S(1)}, bf16[8,120,128]{2,1,0:T(8,128)(2,1)S(1)}, u32[]{:S(2)}, u32[]{:S(2)}) collective-permute-start(bf16[8,120,128]{2,1,0:T(8,128)(2,1)S(1)} %get-tuple-element.30), channel_id=1, source_target_pairs={{0,2},{1,3},{2,0},{3,1},{4,6},{5,7},{6,4},{7,5},{8,10},{9,11},{10,... | collective-permute-start | bytes 737288 | tf_op jit(solution)/shard_map/ppermute | solution.py:607
  23.6 2.6 %collective-permute-start.1 = (bf16[8,120,128]{2,1,0:T(8,128)(2,1)S(1)}, bf16[8,120,128]{2,1,0:T(8,128)(2,1)S(1)}, u32[]{:S(2)}, u32[]{:S(2)}) collective-permute-start(bf16[8,120,128]{2,1,0:T(8,128)(2,1)S(1)} %get-tuple-element.30), channel_id=1, source_target_pairs={{0,4},{1,5},{2,6},{3,7},{4,0},{5,1},{6,2},{7,3},{8,12},{9,13},{10,... | collective-permute-start | bytes 737288 | tf_op jit(solution)/shard_map/ppermute | solution.py:607
  26.2 0.9 %collective-permute-start.4 = (bf16[8,120,128]{2,1,0:T(8,128)(2,1)S(1)}, bf16[8,120,128]{2,1,0:T(8,128)(2,1)S(1)}, u32[]{:S(2)}, u32[]{:S(2)}) collective-permute-start(bf16[8,120,128]{2,1,0:T(8,128)(2,1)S(1)} %get-tuple-element.29), channel_id=1, source_target_pairs={{0,2},{1,3},{2,0},{3,1},{4,6},{5,7},{6,4},{7,5},{8,10},{9,11},{10,... | collective-permute-start | bytes 737288 | tf_op jit(solution)/shard_map/ppermute | solution.py:607
  27.1 0.3 collective-permute-start.5
  27.5 0.0 collective-permute-done.2.far_in
  27.5 0.0 copy-done.1
  27.5 3.5 %first.1 = (f32[256,128]{1,0:T(8,128)S(1)}, bf16[1024,768]{1,0:T(8,128)(2,1)S(1)}) custom-call(bf16[16,120,128]{2,1,0:T(8,128)(2,1)S(1)} %all-to-all-done.chunk.mine, bf16[1024,768]{1,0:T(8,128)(2,1)S(1)} %copy-done.1, bf16[1024,768]{1,0:T(8,128)(2,1)} %collective-permute-done.2.far_in), custom_call_target="tpu_custom_call" | custom-call | flops 6442450944 | bytes 1048576 | tf_op jit(solution)/shard_map/first/pallas_call | solution.py:417
  31.0 0.0 collective-permute-done.half0.cx0
  31.0 0.0 collective-permute-done.1.half1.cy0
  31.0 2.7 %collective-permute-start.3 = (bf16[8,120,128]{2,1,0:T(8,128)(2,1)S(1)}, bf16[8,120,128]{2,1,0:T(8,128)(2,1)S(1)}, u32[]{:S(2)}, u32[]{:S(2)}) collective-permute-start(bf16[8,120,128]{2,1,0:T(8,128)(2,1)S(1)} %collective-permute-done.half0.cx0), channel_id=1, source_target_pairs={{0,4},{1,5},{2,6},{3,7},{4,0},{5,1},{6,2},{7,3},{8,12},{9,13},{10,... | collective-permute-start | bytes 737288 | tf_op jit(solution)/shard_map/ppermute | solution.py:611
  33.7 2.6 %early.1.r1 = f32[256,128]{1,0:T(8,128)S(1)} custom-call(bf16[8,120,128]{2,1,0:T(8,128)(2,1)S(1)} %collective-permute-done.half0.cx0, bf16[8,120,128]{2,1,0:T(8,128)(2,1)S(1)} %collective-permute-done.1.half1.cy0, bf16[1024,768]{1,0:T(8,128)(2,1)S(1)} %copy-done.1, bf16[1024,768]{1,0:T(8,128)(2,1)S(1)} %get-tuple-element.21.far), custom_call_target="tpu_custom_call" | custom-call | flops 6442450944 | bytes 1048576 | tf_op jit(solution)/shard_map/early/pallas_call | solution.py:433
  36.3 0.0 collective-permute-done.4.cx1
  36.3 0.3 collective-permute-done.5.cy1
  36.6 2.0 %collective-permute-start.6 = (bf16[8,120,128]{2,1,0:T(8,128)(2,1)S(1)}, bf16[8,120,128]{2,1,0:T(8,128)(2,1)S(1)}, u32[]{:S(2)}, u32[]{:S(2)}) collective-permute-start(bf16[8,120,128]{2,1,0:T(8,128)(2,1)S(1)} %collective-permute-done.5.cy1), channel_id=1, source_target_pairs={{0,2},{1,3},{2,0},{3,1},{4,6},{5,7},{6,4},{7,5},{8,10},{9,11},{10,... | collective-permute-start | bytes 737288 | tf_op jit(solution)/shard_map/ppermute | solution.py:614
  38.6 5.0 %middle.1 = (f32[256,128]{1,0:T(8,128)S(1)}, f32[256,128]{1,0:T(8,128)S(1)}) custom-call(bf16[16,120,128]{2,1,0:T(8,128)(2,1)S(1)} %all-to-all-done.chunk.mine, bf16[8,120,128]{2,1,0:T(8,128)(2,1)S(1)} %collective-permute-done.half0.cx0, bf16[8,120,128]{2,1,0:T(8,128)(2,1)S(1)} %collective-permute-done.4.cx1, ...), custom_call_target="tpu_custom_call" | custom-call | flops 12884901888 | bytes 1048576 | tf_op jit(solution)/shard_map/middle/pallas_call | solution.py:446
  43.6 0.0 collective-permute-done.6.cd1
  43.6 0.0 collective-permute-done.3.cd0
  43.6 0.0 copy-start
  43.6 4.9 %late.1 = s16[2,4,8,24,128]{4,3,2,1,0:T(8,128)(2,1)S(1)} custom-call(s32[1]{0:T(128)} %bitcast.at, bf16[8,120,128]{2,1,0:T(8,128)(2,1)S(1)} %collective-permute-done.3.cd0, bf16[8,120,128]{2,1,0:T(8,128)(2,1)S(1)} %collective-permute-done.6.cd1, bf16[1024,768]{1,0:T(8,128)(2,1)S(1)} %copy-done.1, bf16[1024,768]{1,0:T(8,128)(2,1)S(1)} %get-tuple-element.21.far, ...), custom_call_target="tpu_custom_call" | custom-call | flops 12884901888 | bytes 1048576 | tf_op jit(solution)/shard_map/late/pallas_call | solution.py:459
  48.5 23.4 %all_to_all.10 = s16[64,24,128]{2,1,0:T(8,128)(2,1)S(1)} all-to-all(s16[64,24,128]{2,1,0:T(8,128)(2,1)S(1)} %bitcast.5), channel_id=1, replica_groups={{0,16,32,48,64,80,96,112,4,20,36,52,68,84,100,116,2,18,34,50,66,82,98,1..., dimensions={0} | all-to-all | bytes 786432 | tf_op jit(solution)/shard_map/all_to_all | solution.py:619
  71.9 0.0 copy-done
  71.9 1.6 %join.1 = f32[128,128]{1,0:T(8,128)} custom-call(s16[2,4,8,24,128]{4,3,2,1,0:T(8,128)(2,1)S(1)} %bitcast.4, s32[1,128]{1,0:T(1,128)S(1)} %copy-done), custom_call_target="tpu_custom_call" | custom-call | tf_op jit(solution)/shard_map/join/pallas_call | solution.py:554
  (1 shorter events, 0.0 us)
Async XLA Ops:
  0.0 27.5 %copy-start.1 = (bf16[1024,768]{1,0:T(8,128)(2,1)S(1)}, bf16[1024,768]{1,0:T(8,128)(2,1)}, u32[]{:S(2)}) copy-start(bf16[1024,768]{1,0:T(8,128)(2,1)} %own.7) | copy-start | bytes 4718596
  0.0 27.5 %collective-permute-start.2 = (bf16[1024,768]{1,0:T(8,128)(2,1)}, bf16[1024,768]{1,0:T(8,128)(2,1)}, u32[]{:S(2)}, u32[]{:S(2)}) collective-permute-start(bf16[1024,768]{1,0:T(8,128)(2,1)} %own.7), channel_id=1, source_target_pairs={{0,1},{1,0},{2,3},{3,2},{4,5},{5,4},{6,7},{7,6},{8,11},{9,10},{10,... | collective-permute-start | bytes 4718600 | tf_op jit(solution)/shard_map/ppermute | solution.py:603
  5.6 15.8 %all-to-all-start = ((bf16[16,120,128]{2,1,0:T(8,128)(2,1)}), bf16[16,120,128]{2,1,0:T(8,128)(2,1)S(1)}, u32[]{:S(2)}, u32[]{:S(2)}) async-start(bf16[16,120,128]{2,1,0:T(8,128)(2,1)} %get-tuple-element.17), calls=%async_computation | async-start | bytes 983040 | tf_op jit(solution)/shard_map/all_to_all | solution.py:605
  21.4 9.6 %collective-permute-start = (bf16[8,120,128]{2,1,0:T(8,128)(2,1)S(1)}, bf16[8,120,128]{2,1,0:T(8,128)(2,1)S(1)}, u32[]{:S(2)}, u32[]{:S(2)}) collective-permute-start(bf16[8,120,128]{2,1,0:T(8,128)(2,1)S(1)} %get-tuple-element.30), channel_id=1, source_target_pairs={{0,2},{1,3},{2,0},{3,1},{4,6},{5,7},{6,4},{7,5},{8,10},{9,11},{10,... | collective-permute-start | bytes 737288 | tf_op jit(solution)/shard_map/ppermute | solution.py:607
  23.6 7.5 %collective-permute-start.1 = (bf16[8,120,128]{2,1,0:T(8,128)(2,1)S(1)}, bf16[8,120,128]{2,1,0:T(8,128)(2,1)S(1)}, u32[]{:S(2)}, u32[]{:S(2)}) collective-permute-start(bf16[8,120,128]{2,1,0:T(8,128)(2,1)S(1)} %get-tuple-element.30), channel_id=1, source_target_pairs={{0,4},{1,5},{2,6},{3,7},{4,0},{5,1},{6,2},{7,3},{8,12},{9,13},{10,... | collective-permute-start | bytes 737288 | tf_op jit(solution)/shard_map/ppermute | solution.py:607
  26.2 10.1 %collective-permute-start.4 = (bf16[8,120,128]{2,1,0:T(8,128)(2,1)S(1)}, bf16[8,120,128]{2,1,0:T(8,128)(2,1)S(1)}, u32[]{:S(2)}, u32[]{:S(2)}) collective-permute-start(bf16[8,120,128]{2,1,0:T(8,128)(2,1)S(1)} %get-tuple-element.29), channel_id=1, source_target_pairs={{0,2},{1,3},{2,0},{3,1},{4,6},{5,7},{6,4},{7,5},{8,10},{9,11},{10,... | collective-permute-start | bytes 737288 | tf_op jit(solution)/shard_map/ppermute | solution.py:607
  27.1 9.5 %collective-permute-start.5 = (bf16[8,120,128]{2,1,0:T(8,128)(2,1)S(1)}, bf16[8,120,128]{2,1,0:T(8,128)(2,1)S(1)}, u32[]{:S(2)}, u32[]{:S(2)}) collective-permute-start(bf16[8,120,128]{2,1,0:T(8,128)(2,1)S(1)} %get-tuple-element.29), channel_id=1, source_target_pairs={{0,4},{1,5},{2,6},{3,7},{4,0},{5,1},{6,2},{7,3},{8,12},{9,13},{10,... | collective-permute-start | bytes 737288 | tf_op jit(solution)/shard_map/ppermute | solution.py:607
  31.0 12.6 %collective-permute-start.3 = (bf16[8,120,128]{2,1,0:T(8,128)(2,1)S(1)}, bf16[8,120,128]{2,1,0:T(8,128)(2,1)S(1)}, u32[]{:S(2)}, u32[]{:S(2)}) collective-permute-start(bf16[8,120,128]{2,1,0:T(8,128)(2,1)S(1)} %collective-permute-done.half0.cx0), channel_id=1, source_target_pairs={{0,4},{1,5},{2,6},{3,7},{4,0},{5,1},{6,2},{7,3},{8,12},{9,13},{10,... | collective-permute-start | bytes 737288 | tf_op jit(solution)/shard_map/ppermute | solution.py:611
  36.6 7.0 %collective-permute-start.6 = (bf16[8,120,128]{2,1,0:T(8,128)(2,1)S(1)}, bf16[8,120,128]{2,1,0:T(8,128)(2,1)S(1)}, u32[]{:S(2)}, u32[]{:S(2)}) collective-permute-start(bf16[8,120,128]{2,1,0:T(8,128)(2,1)S(1)} %collective-permute-done.5.cy1), channel_id=1, source_target_pairs={{0,2},{1,3},{2,0},{3,1},{4,6},{5,7},{6,4},{7,5},{8,10},{9,11},{10,... | collective-permute-start | bytes 737288 | tf_op jit(solution)/shard_map/ppermute | solution.py:614
  43.6 28.3 %copy-start = (s32[1,128]{1,0:T(1,128)S(1)}, s32[1,128]{1,0:T(1,128)}, u32[]{:S(2)}) copy-start(s32[1,128]{1,0:T(1,128)} %get-tuple-element.28.slots) | copy-start | bytes 1540

commit v11 on v7

--- a/solution.py
+++ b/solution.py
@@ -38,7 +38,6 @@
 
 SORT32 = batcher(32)
 SORT16 = batcher(16)
-AHEAD = 2
 
 
 def wire(ref, base, i):
@@ -222,7 +221,7 @@
         clean_at(dst, at + 32)
 
 
-def leaders(groups, own, far, *work, emit):
+def leaders(groups, own, far, *work, emit, ahead=2):
     near_parts, far_parts, (s, u, w) = work[:4], work[4:8], work[8:]
     sides = (near_parts, far_parts)
     parts = [(g, side, i) for g in range(len(groups)) for side in range(2) for i in range(4)]
@@ -232,11 +231,11 @@
             g, side, i = parts[k]
             wires_of((own, far)[side](), groups[g][1](), sides[side], i)
 
-    for k in range(AHEAD):
+    for k in range(ahead):
         scored(k)
     peak = None
     for k, (g, side, i) in enumerate(parts):
-        scored(k + AHEAD)
+        scored(k + ahead)
         blocks = groups[g][0]
         if blocks == 2 or i % 2 == 1:
             nth = i if blocks == 2 else i // 2
@@ -261,12 +260,16 @@
         unsure = jnp.max(jnp.where(peak > wire(w, 127, 0), 1.0, 0.0)) > 0.0
         peak = None
 
+        def give(g=g, blocks=blocks):
+            for half in range(blocks):
+                emit(g, half, w[pl.ds(half, TOPK, stride=8), :].T)
+
+        give()
+
         @pl.when(unsure)
-        def _():
+        def _(g=g, blocks=blocks, give=give):
             long_way(blocks, groups[g][1](), own(), far(), s, u, w)
-
-        for half in range(blocks):
-            emit(g, half, w[pl.ds(half, TOPK, stride=8), :].T)
+            give()
 
 
 def long_way(blocks, rows, own, far, s, u, w):
@@ -321,7 +324,7 @@
     def emit(g, half, value):
         out[half * Q : (half + 1) * Q, :] = value
 
-    leaders([(2, lambda: rows[...])], lambda: own, partner, *work, emit=emit)
+    leaders([(2, lambda: rows[...])], lambda: own, partner, *work, emit=emit, ahead=0)
 
 
 def early_kernel(half0, half1, own, far, out, rows, *work):
@@ -480,10 +483,7 @@
     )
     for copy in copies:
         copy.start()
-    for copy in copies:
-        copy.wait()
-    x = queries[...].astype(jnp.float32)
-    unit = (x * lax.rsqrt(jnp.mean(x * x, axis=1, keepdims=True) + epsilon)).astype(jnp.bfloat16)
+    copies[0].wait()
     along = jnp.broadcast_to(routes[...].astype(jnp.float32), (Q, Q))
     down = along.T
     before = lax.broadcasted_iota(jnp.int32, (Q, Q), 0) < lax.broadcasted_iota(jnp.int32, (Q, Q), 1)
@@ -494,19 +494,24 @@
     main_at = jnp.where(rank < MAIN, lang * MAIN + rank, -1)
     hits = lax.broadcasted_iota(jnp.int32, (LANGS * MAIN, Q), 0) == jnp.broadcast_to(main_at, (LANGS * MAIN, Q))
     picks = jnp.where(hits, 1.0, 0.0).astype(jnp.bfloat16)
-    box = jnp.dot(picks, unit, preferred_element_type=jnp.float32).astype(jnp.bfloat16)
-    for c in range(COLS):
-        out[:, c * MAIN : (c + 1) * MAIN, :] = box[:, c * 128 : (c + 1) * 128].reshape(LANGS, MAIN, 128)
     each = TAIL * COLS
     tail_at = jnp.where(rank < MAIN, -1, lang * TAIL + rank - MAIN)
     shape = (LANGS, each, Q)
     of_lang, row = (lax.broadcasted_iota(jnp.int32, shape, d) for d in range(2))
     hits = of_lang * TAIL + (row & 3) == jnp.broadcast_to(tail_at.reshape(1, 1, Q), shape)
+    tail_picks = [
+        jnp.where(hits & (lax.shift_right_logical(row, 2) == c), 1.0, 0.0).astype(jnp.bfloat16).reshape(LANGS * each, Q)
+        for c in range(COLS)
+    ]
+    copies[1].wait()
+    x = queries[...].astype(jnp.float32)
+    unit = (x * lax.rsqrt(jnp.mean(x * x, axis=1, keepdims=True) + epsilon)).astype(jnp.bfloat16)
+    box = jnp.dot(picks, unit, preferred_element_type=jnp.float32).astype(jnp.bfloat16)
+    for c in range(COLS):
+        out[:, c * MAIN : (c + 1) * MAIN, :] = box[:, c * 128 : (c + 1) * 128].reshape(LANGS, MAIN, 128)
     tail = jnp.zeros((LANGS * each, 128), jnp.float32)
     for c in range(COLS):
-        picks = jnp.where(hits & (lax.shift_right_logical(row, 2) == c), 1.0, 0.0)
-        picks = picks.astype(jnp.bfloat16).reshape(LANGS * each, Q)
-        tail = tail + jnp.dot(picks, unit[:, c * 128 : (c + 1) * 128], preferred_element_type=jnp.float32)
+        tail = tail + jnp.dot(tail_picks[c], unit[:, c * 128 : (c + 1) * 128], preferred_element_type=jnp.float32)
     out[:, MAIN * COLS : SENT, :] = tail.astype(jnp.bfloat16).reshape(LANGS, each, 128)
 
 

time: 74.3 us -> 74.4 us (level); the launches traced: 73 us -> 74.7 us
  blocking collectives: 22.8 us -> 24.7 us
    all_to_all x1, blocking collectives: 22.8 us -> 24.7 us  [shards(): lax.all_to_all(found.reshape(LANGS * 4, ROWS, TOPK), AXES, 0, 0, axis_ind...]
  transfers between devices with their start and end apart: 8 -> 8, of which waited for: 2 -> 4; matrix products, arithmetic and copies ran while one was open for 0% -> 0% of each run, Pallas kernels for 18% -> 17%
where the time goes in v11:
time: 74.4 us; the launch traced here: 74.7 us
  blocking collectives  24.7 us (33%)
  starting transfers between devices  20 us (27%)
  Pallas kernels  19.5 us (26%)
  waiting for transfers between devices  10.3 us (14%)
    all_to_all x1, blocking collectives, shards(): lax.all_to_all(found.reshape(LANGS * 4, ROWS, TOPK), AXES, 0, 0, axis_ind...  24.7 us
    all_to_all x1, waiting for transfers between devices, shards(): lax.all_to_all(outbox, 'lang', split_axis=0, concat_axis=0, tiled=True)  9.31 us
    all_to_all x1, starting transfers between devices, shards(): lax.all_to_all(outbox, 'lang', split_axis=0, concat_axis=0, tiled=True)  6.46 us
    ppermute x4, starting transfers between devices, shards(): lax.ppermute(part, AXES, moves(over))  6.02 us
    pallas_call x1, Pallas kernels, middle(): pl.pallas_call(middle_kernel, out_shape=[jax.ShapeDtypeStruct((256, TOPK)...  4.95 us
    pallas_call x1, Pallas kernels, late(): pl.pallas_call(late_kernel, out_shape=jax.ShapeDtypeStruct((LANGS, 4, ROW...  4.91 us
    ppermute x1, starting transfers between devices, shards(): far = lax.ppermute(corpus, AXES, moves(pair))  3.3 us
    pallas_call x1, Pallas kernels, first(): pl.pallas_call(first_kernel, out_shape=(jax.ShapeDtypeStruct((256, TOPK),...  3.21 us
  transfers between devices with their start and end apart: 8, of which 4 were waited for; matrix products, arithmetic and copies ran while one was open for 0% of the time, Pallas kernels for 17%

profile of v11, /device:TPU:1, one launch (start us, length us, event | category | flops | bytes accessed | tf_op | source)
XLA Modules:
  0.0 74.7 jit_solution(3501643244019503)
XLA Ops:
  0.0 0.0 copy-start.1
  0.0 3.3 %collective-permute-start.2 = (bf16[1024,768]{1,0:T(8,128)(2,1)}, bf16[1024,768]{1,0:T(8,128)(2,1)}, u32[]{:S(2)}, u32[]{:S(2)}) collective-permute-start(bf16[1024,768]{1,0:T(8,128)(2,1)} %own.7), channel_id=1, source_target_pairs={{0,1},{1,0},{2,3},{3,2},{4,5},{5,4},{6,7},{7,6},{8,11},{9,10},{10,... | collective-permute-start | bytes 4718600 | tf_op jit(solution)/shard_map/ppermute | solution.py:602
  3.3 2.3 %outbox.1 = (bf16[16,120,128]{2,1,0:T(8,128)(2,1)}, s32[1,128]{1,0:T(1,128)}) custom-call(bf16[128,768]{1,0:T(8,128)(2,1)} %queries_in.1, s32[1,128]{1,0:T(1,128)} %bitcast.6), custom_call_target="tpu_custom_call" | custom-call | tf_op jit(solution)/shard_map/outbox/pallas_call | solution.py:519
  5.6 6.5 %all-to-all-start = ((bf16[16,120,128]{2,1,0:T(8,128)(2,1)}), bf16[16,120,128]{2,1,0:T(8,128)(2,1)S(1)}, u32[]{:S(2)}, u32[]{:S(2)}) async-start(bf16[16,120,128]{2,1,0:T(8,128)(2,1)} %get-tuple-element.17), calls=%async_computation | async-start | bytes 983040 | tf_op jit(solution)/shard_map/all_to_all | solution.py:604
  12.1 9.3 %all-to-all-done.chunk.mine = bf16[16,120,128]{2,1,0:T(8,128)(2,1)S(1)} async-done(((bf16[16,120,128]{2,1,0:T(8,128)(2,1)}), bf16[16,120,128]{2,1,0:T(8,128)(2,1)S(1)}, u32[]{:S(2)}, u32[]{:S(2)}) %all-to-all-start) | async-done | bytes 491552 | tf_op jit(solution)/shard_map/all_to_all | solution.py:604
  21.4 2.1 %collective-permute-start = (bf16[8,120,128]{2,1,0:T(8,128)(2,1)S(1)}, bf16[8,120,128]{2,1,0:T(8,128)(2,1)S(1)}, u32[]{:S(2)}, u32[]{:S(2)}) collective-permute-start(bf16[8,120,128]{2,1,0:T(8,128)(2,1)S(1)} %get-tuple-element.30), channel_id=1, source_target_pairs={{0,2},{1,3},{2,0},{3,1},{4,6},{5,7},{6,4},{7,5},{8,10},{9,11},{10,... | collective-permute-start | bytes 737288 | tf_op jit(solution)/shard_map/ppermute | solution.py:606
  23.5 2.6 %collective-permute-start.1 = (bf16[8,120,128]{2,1,0:T(8,128)(2,1)S(1)}, bf16[8,120,128]{2,1,0:T(8,128)(2,1)S(1)}, u32[]{:S(2)}, u32[]{:S(2)}) collective-permute-start(bf16[8,120,128]{2,1,0:T(8,128)(2,1)S(1)} %get-tuple-element.30), channel_id=1, source_target_pairs={{0,4},{1,5},{2,6},{3,7},{4,0},{5,1},{6,2},{7,3},{8,12},{9,13},{10,... | collective-permute-start | bytes 737288 | tf_op jit(solution)/shard_map/ppermute | solution.py:606
  26.1 0.9 %collective-permute-start.4 = (bf16[8,120,128]{2,1,0:T(8,128)(2,1)S(1)}, bf16[8,120,128]{2,1,0:T(8,128)(2,1)S(1)}, u32[]{:S(2)}, u32[]{:S(2)}) collective-permute-start(bf16[8,120,128]{2,1,0:T(8,128)(2,1)S(1)} %get-tuple-element.29), channel_id=1, source_target_pairs={{0,2},{1,3},{2,0},{3,1},{4,6},{5,7},{6,4},{7,5},{8,10},{9,11},{10,... | collective-permute-start | bytes 737288 | tf_op jit(solution)/shard_map/ppermute | solution.py:606
  27.1 0.3 collective-permute-start.5
  27.4 0.0 collective-permute-done.2.far_in
  27.4 0.0 copy-done.1
  27.4 3.2 %first.1 = (f32[256,128]{1,0:T(8,128)S(1)}, bf16[1024,768]{1,0:T(8,128)(2,1)S(1)}) custom-call(bf16[16,120,128]{2,1,0:T(8,128)(2,1)S(1)} %all-to-all-done.chunk.mine, bf16[1024,768]{1,0:T(8,128)(2,1)S(1)} %copy-done.1, bf16[1024,768]{1,0:T(8,128)(2,1)} %collective-permute-done.2.far_in), custom_call_target="tpu_custom_call" | custom-call | flops 6442450944 | bytes 1048576 | tf_op jit(solution)/shard_map/first/pallas_call | solution.py:420
  30.7 0.0 collective-permute-done.half0.cx0
  30.7 0.3 collective-permute-done.1.half1.cy0
  31.0 2.6 %collective-permute-start.3 = (bf16[8,120,128]{2,1,0:T(8,128)(2,1)S(1)}, bf16[8,120,128]{2,1,0:T(8,128)(2,1)S(1)}, u32[]{:S(2)}, u32[]{:S(2)}) collective-permute-start(bf16[8,120,128]{2,1,0:T(8,128)(2,1)S(1)} %collective-permute-done.half0.cx0), channel_id=1, source_target_pairs={{0,4},{1,5},{2,6},{3,7},{4,0},{5,1},{6,2},{7,3},{8,12},{9,13},{10,... | collective-permute-start | bytes 737288 | tf_op jit(solution)/shard_map/ppermute | solution.py:610
  33.6 2.5 %early.1.r1 = f32[256,128]{1,0:T(8,128)S(1)} custom-call(bf16[8,120,128]{2,1,0:T(8,128)(2,1)S(1)} %collective-permute-done.half0.cx0, bf16[8,120,128]{2,1,0:T(8,128)(2,1)S(1)} %collective-permute-done.1.half1.cy0, bf16[1024,768]{1,0:T(8,128)(2,1)S(1)} %copy-done.1, bf16[1024,768]{1,0:T(8,128)(2,1)S(1)} %get-tuple-element.21.far), custom_call_target="tpu_custom_call" | custom-call | flops 6442450944 | bytes 1048576 | tf_op jit(solution)/shard_map/early/pallas_call | solution.py:436
  36.1 0.0 collective-permute-done.4.cx1
  36.1 0.4 collective-permute-done.5.cy1
  36.6 1.6 %collective-permute-start.6 = (bf16[8,120,128]{2,1,0:T(8,128)(2,1)S(1)}, bf16[8,120,128]{2,1,0:T(8,128)(2,1)S(1)}, u32[]{:S(2)}, u32[]{:S(2)}) collective-permute-start(bf16[8,120,128]{2,1,0:T(8,128)(2,1)S(1)} %collective-permute-done.5.cy1), channel_id=1, source_target_pairs={{0,2},{1,3},{2,0},{3,1},{4,6},{5,7},{6,4},{7,5},{8,10},{9,11},{10,... | collective-permute-start | bytes 737288 | tf_op jit(solution)/shard_map/ppermute | solution.py:613
  38.2 5.0 %middle.1 = (f32[256,128]{1,0:T(8,128)S(1)}, f32[256,128]{1,0:T(8,128)S(1)}) custom-call(bf16[16,120,128]{2,1,0:T(8,128)(2,1)S(1)} %all-to-all-done.chunk.mine, bf16[8,120,128]{2,1,0:T(8,128)(2,1)S(1)} %collective-permute-done.half0.cx0, bf16[8,120,128]{2,1,0:T(8,128)(2,1)S(1)} %collective-permute-done.4.cx1, ...), custom_call_target="tpu_custom_call" | custom-call | flops 12884901888 | bytes 1048576 | tf_op jit(solution)/shard_map/middle/pallas_call | solution.py:449
  43.1 0.3 collective-permute-done.6.cd1
  43.4 0.0 collective-permute-done.3.cd0
  43.4 0.0 copy-start
  43.4 4.9 %late.1 = s16[16,4,24,128]{3,2,1,0:T(8,128)(2,1)S(1)} custom-call(s32[1]{0:T(128)} %bitcast.at, bf16[8,120,128]{2,1,0:T(8,128)(2,1)S(1)} %collective-permute-done.3.cd0, bf16[8,120,128]{2,1,0:T(8,128)(2,1)S(1)} %collective-permute-done.6.cd1, bf16[1024,768]{1,0:T(8,128)(2,1)S(1)} %copy-done.1, bf16[1024,768]{1,0:T(8,128)(2,1)S(1)} %get-tuple-element.21.far, ...), custom_call_target="tpu_custom_call" | custom-call | flops 12884901888 | bytes 1048576 | tf_op jit(solution)/shard_map/late/pallas_call | solution.py:462
  48.3 24.7 %all_to_all.10 = s16[64,24,128]{2,1,0:T(8,128)(2,1)S(1)} all-to-all(s16[64,24,128]{2,1,0:T(8,128)(2,1)S(1)} %bitcast.5), channel_id=1, replica_groups={{0,2,4,6,8,10,12,14,16,18,20,22,24,26,28,30,32,34,36,38,40,42,44,46,48,..., dimensions={0} | all-to-all | bytes 786432 | tf_op jit(solution)/shard_map/all_to_all | solution.py:618
  73.0 0.0 copy-done
  73.0 1.6 %join.1 = f32[128,128]{1,0:T(8,128)} custom-call(s16[16,4,24,128]{3,2,1,0:T(8,128)(2,1)S(1)} %bitcast.4, s32[1,128]{1,0:T(1,128)S(1)} %copy-done), custom_call_target="tpu_custom_call" | custom-call | tf_op jit(solution)/shard_map/join/pallas_call | solution.py:559
  (1 shorter events, 0.0 us)
Async XLA Ops:
  0.0 27.4 %copy-start.1 = (bf16[1024,768]{1,0:T(8,128)(2,1)S(1)}, bf16[1024,768]{1,0:T(8,128)(2,1)}, u32[]{:S(2)}) copy-start(bf16[1024,768]{1,0:T(8,128)(2,1)} %own.7) | copy-start | bytes 4718596
  0.0 27.4 %collective-permute-start.2 = (bf16[1024,768]{1,0:T(8,128)(2,1)}, bf16[1024,768]{1,0:T(8,128)(2,1)}, u32[]{:S(2)}, u32[]{:S(2)}) collective-permute-start(bf16[1024,768]{1,0:T(8,128)(2,1)} %own.7), channel_id=1, source_target_pairs={{0,1},{1,0},{2,3},{3,2},{4,5},{5,4},{6,7},{7,6},{8,11},{9,10},{10,... | collective-permute-start | bytes 4718600 | tf_op jit(solution)/shard_map/ppermute | solution.py:602
  5.6 15.8 %all-to-all-start = ((bf16[16,120,128]{2,1,0:T(8,128)(2,1)}), bf16[16,120,128]{2,1,0:T(8,128)(2,1)S(1)}, u32[]{:S(2)}, u32[]{:S(2)}) async-start(bf16[16,120,128]{2,1,0:T(8,128)(2,1)} %get-tuple-element.17), calls=%async_computation | async-start | bytes 983040 | tf_op jit(solution)/shard_map/all_to_all | solution.py:604
  21.4 9.2 %collective-permute-start = (bf16[8,120,128]{2,1,0:T(8,128)(2,1)S(1)}, bf16[8,120,128]{2,1,0:T(8,128)(2,1)S(1)}, u32[]{:S(2)}, u32[]{:S(2)}) collective-permute-start(bf16[8,120,128]{2,1,0:T(8,128)(2,1)S(1)} %get-tuple-element.30), channel_id=1, source_target_pairs={{0,2},{1,3},{2,0},{3,1},{4,6},{5,7},{6,4},{7,5},{8,10},{9,11},{10,... | collective-permute-start | bytes 737288 | tf_op jit(solution)/shard_map/ppermute | solution.py:606
  23.5 7.5 %collective-permute-start.1 = (bf16[8,120,128]{2,1,0:T(8,128)(2,1)S(1)}, bf16[8,120,128]{2,1,0:T(8,128)(2,1)S(1)}, u32[]{:S(2)}, u32[]{:S(2)}) collective-permute-start(bf16[8,120,128]{2,1,0:T(8,128)(2,1)S(1)} %get-tuple-element.30), channel_id=1, source_target_pairs={{0,4},{1,5},{2,6},{3,7},{4,0},{5,1},{6,2},{7,3},{8,12},{9,13},{10,... | collective-permute-start | bytes 737288 | tf_op jit(solution)/shard_map/ppermute | solution.py:606
  26.1 10.0 %collective-permute-start.4 = (bf16[8,120,128]{2,1,0:T(8,128)(2,1)S(1)}, bf16[8,120,128]{2,1,0:T(8,128)(2,1)S(1)}, u32[]{:S(2)}, u32[]{:S(2)}) collective-permute-start(bf16[8,120,128]{2,1,0:T(8,128)(2,1)S(1)} %get-tuple-element.29), channel_id=1, source_target_pairs={{0,2},{1,3},{2,0},{3,1},{4,6},{5,7},{6,4},{7,5},{8,10},{9,11},{10,... | collective-permute-start | bytes 737288 | tf_op jit(solution)/shard_map/ppermute | solution.py:606
  27.1 9.5 %collective-permute-start.5 = (bf16[8,120,128]{2,1,0:T(8,128)(2,1)S(1)}, bf16[8,120,128]{2,1,0:T(8,128)(2,1)S(1)}, u32[]{:S(2)}, u32[]{:S(2)}) collective-permute-start(bf16[8,120,128]{2,1,0:T(8,128)(2,1)S(1)} %get-tuple-element.29), channel_id=1, source_target_pairs={{0,4},{1,5},{2,6},{3,7},{4,0},{5,1},{6,2},{7,3},{8,12},{9,13},{10,... | collective-permute-start | bytes 737288 | tf_op jit(solution)/shard_map/ppermute | solution.py:606
  31.0 12.4 %collective-permute-start.3 = (bf16[8,120,128]{2,1,0:T(8,128)(2,1)S(1)}, bf16[8,120,128]{2,1,0:T(8,128)(2,1)S(1)}, u32[]{:S(2)}, u32[]{:S(2)}) collective-permute-start(bf16[8,120,128]{2,1,0:T(8,128)(2,1)S(1)} %collective-permute-done.half0.cx0), channel_id=1, source_target_pairs={{0,4},{1,5},{2,6},{3,7},{4,0},{5,1},{6,2},{7,3},{8,12},{9,13},{10,... | collective-permute-start | bytes 737288 | tf_op jit(solution)/shard_map/ppermute | solution.py:610
  36.6 6.8 %collective-permute-start.6 = (bf16[8,120,128]{2,1,0:T(8,128)(2,1)S(1)}, bf16[8,120,128]{2,1,0:T(8,128)(2,1)S(1)}, u32[]{:S(2)}, u32[]{:S(2)}) collective-permute-start(bf16[8,120,128]{2,1,0:T(8,128)(2,1)S(1)} %collective-permute-done.5.cy1), channel_id=1, source_target_pairs={{0,2},{1,3},{2,0},{3,1},{4,6},{5,7},{6,4},{7,5},{8,10},{9,11},{10,... | collective-permute-start | bytes 737288 | tf_op jit(solution)/shard_map/ppermute | solution.py:613
  43.4 29.6 %copy-start = (s32[1,128]{1,0:T(1,128)S(1)}, s32[1,128]{1,0:T(1,128)}, u32[]{:S(2)}) copy-start(s32[1,128]{1,0:T(1,128)} %get-tuple-element.28.slots) | copy-start | bytes 1540

commit v12 on v11

--- a/solution.py
+++ b/solution.py
@@ -337,7 +337,31 @@
     leaders([(2, lambda: rows[...])], lambda: own, lambda: far, *work, emit=emit)
 
 
-def middle_kernel(mine, cx0, cx1, cy0, cy1, own, far, out, tails, rows, *work):
+STEPS = 800.0
+FLOOR = 32.5
+LN2 = 0.6931471805599453
+
+
+def coded(v):
+    level = jnp.round(jnp.log(jnp.abs(v)) * (STEPS / LN2) + STEPS * FLOOR)
+    level = jnp.clip(level, 0.0, 32767.0)
+    return jnp.where(v < 0, -level, level)
+
+
+def decoded(c):
+    level = jnp.abs(c)
+    v = jnp.where(level > 0, jnp.exp(level * (LN2 / STEPS) - FLOOR * LN2), 0.0)
+    return jnp.where(c < 0, -v, v)
+
+
+def boxed(box, main, tail):
+    box[0:MAIN, :] = main
+    box[MAIN:CAP, :] = tail
+    box[CAP:ROWS, :] = jnp.zeros((ROWS - CAP, TOPK), jnp.float32)
+    return coded(box[...]).astype(jnp.int32).astype(jnp.int16)
+
+
+def middle_kernel(mine, cx0, cx1, cy0, cy1, own, far, r0, r1, out, rows, lists, box, *work):
     rows[0:128, :] = main_rows(cx1)
     rows[128:256, :] = main_rows(cy1)
     rows[256:320, :] = tail_rows(mine)
@@ -346,36 +370,33 @@
     rows[448:512, :] = jnp.zeros((64, WIDTH), jnp.bfloat16)
 
     def emit(g, half, value):
-        (out, tails)[g][half * Q : (half + 1) * Q, :] = value
+        lists[g * 256 + half * Q : g * 256 + (half + 1) * Q, :] = value
 
     leaders(
         [(2, lambda: rows[0:256, :]), (2, lambda: rows[256:512, :])], lambda: own, lambda: far, *work, emit=emit
     )
-
-
-STEPS = 800.0
-FLOOR = 32.5
-LN2 = 0.6931471805599453
-
-
-def coded(v):
-    level = jnp.round(jnp.log(jnp.abs(v)) * (STEPS / LN2) + STEPS * FLOOR)
-    level = jnp.clip(level, 0.0, 32767.0)
-    return jnp.where(v < 0, -level, level)
-
-
-def decoded(c):
-    level = jnp.abs(c)
-    v = jnp.where(level > 0, jnp.exp(level * (LN2 / STEPS) - FLOOR * LN2), 0.0)
-    return jnp.where(c < 0, -v, v)
-
-
-def late_kernel(at, cd0, cd1, own, far, r0, r1, r2, tails, out, rows, last, box, *work):
+    for k in range(3):
+        for lang in range(LANGS):
+            half, start = lang // 8, lang % 8 * MAIN
+            if k == 0:
+                main = r0[lang * MAIN : (lang + 1) * MAIN, :]
+            else:
+                start += (k - 1) * Q
+                main = (r1, lists)[half][start : start + MAIN, :]
+            start = 256 + k * 64 + lang * TAIL
+            out[k, lang] = boxed(box.at[k], main, lists[start : start + TAIL, :])
+
+
+def late_kernel(at, cd0, cd1, own, far, done, out, rows, last, box, *work):
     rows[0:128, :] = main_rows(cd0)
     rows[128:256, :] = main_rows(cd1)
     rows[256:288, :] = tail_rows(cd0)
     rows[288:320, :] = tail_rows(cd1)
     rows[320:384, :] = jnp.zeros((64, WIDTH), jnp.bfloat16)
+    me = at[0]
+    for k, owner in enumerate((me, me ^ 1, me ^ 2)):
+        for lang in range(LANGS):
+            out[lang, owner] = done[k, lang]
 
     def emit(g, half, value):
         last[g * 256 + half * Q : g * 256 + (half + 1) * Q, :] = value
@@ -383,27 +404,9 @@
     leaders(
         [(2, lambda: rows[0:256, :]), (1, lambda: rows[256:384, :])], lambda: own, lambda: far, *work, emit=emit
     )
-    me = at[0]
-    owner = (me, me ^ 1, me ^ 2, me ^ 3)
-    none = jnp.zeros((ROWS - CAP, TOPK), jnp.float32)
-    for k in range(4):
-        for lang in range(LANGS):
-            half, start = lang // 8, lang % 8 * MAIN
-            if k == 0:
-                main = r0[lang * MAIN : (lang + 1) * MAIN, :]
-            elif k < 3:
-                start += (k - 1) * Q
-                main = (r1, r2)[half][start : start + MAIN, :]
-            else:
-                main = last[lang * MAIN : (lang + 1) * MAIN, :]
-            box[k, 0:MAIN, :] = main
-            start = k * 64 + lang * TAIL
-            if k < 3:
-                box[k, MAIN:CAP, :] = tails[start : start + TAIL, :]
-            else:
-                box[k, MAIN:CAP, :] = last[256 + lang * TAIL : 256 + (lang + 1) * TAIL, :]
-            box[k, CAP:ROWS, :] = none
-            out[lang, owner[k]] = coded(box[k]).astype(jnp.int32).astype(jnp.int16)
+    for lang in range(LANGS):
+        tail = last[256 + lang * TAIL : 256 + (lang + 1) * TAIL, :]
+        out[lang, me ^ 3] = boxed(box.at[lang % 4], last[lang * MAIN : (lang + 1) * MAIN, :], tail)
 
 
 COST = 2 * 256 * 2048 * 768 * 8
@@ -445,24 +448,29 @@
     )(half0, half1, own, far)
 
 
-def middle(mine, halves, own, far):
+def middle(mine, halves, own, far, results):
     return pl.pallas_call(
         middle_kernel,
-        out_shape=[jax.ShapeDtypeStruct((256, TOPK), jnp.float32)] * 2,
-        in_specs=[VMEM] * 7,
-        out_specs=[VMEM] * 2,
-        scratch_shapes=[pltpu.VMEM((512, WIDTH), jnp.bfloat16)] + WORK,
+        out_shape=jax.ShapeDtypeStruct((3, LANGS, ROWS, TOPK), jnp.int16),
+        in_specs=[VMEM] * 9,
+        out_specs=VMEM,
+        scratch_shapes=[
+            pltpu.VMEM((512, WIDTH), jnp.bfloat16),
+            pltpu.VMEM((512, TOPK), jnp.float32),
+            pltpu.VMEM((3, ROWS, TOPK), jnp.float32),
+        ]
+        + WORK,
         compiler_params=LIMIT,
         cost_estimate=pl.CostEstimate(flops=COST * 2, bytes_accessed=1 << 20, transcendentals=0),
         name="middle",
-    )(mine, *halves, own, far)
-
-
-def late(at, halves, own, far, results):
+    )(mine, *halves, own, far, *results)
+
+
+def late(at, halves, own, far, done):
     return pl.pallas_call(
         late_kernel,
         out_shape=jax.ShapeDtypeStruct((LANGS, 4, ROWS, TOPK), jnp.int16),
-        in_specs=[pl.BlockSpec(memory_space=pltpu.SMEM)] + [VMEM] * 8,
+        in_specs=[pl.BlockSpec(memory_space=pltpu.SMEM)] + [VMEM] * 5,
         out_specs=VMEM,
         scratch_shapes=[
             pltpu.VMEM((384, WIDTH), jnp.bfloat16),
@@ -473,7 +481,7 @@
         compiler_params=LIMIT,
         cost_estimate=pl.CostEstimate(flops=COST * 2, bytes_accessed=1 << 20, transcendentals=0),
         name="late",
-    )(at, *halves, own, far, *results)
+    )(at, *halves, own, far, done)
 
 
 def outbox_kernel(queries_in, routes_in, out, slots, queries, routes, sems):
@@ -611,10 +619,10 @@
     r1 = early(cx0, cy0, corpus, far)
     cx1, cy1, r1 = lax.optimization_barrier((cx1, cy1, r1))
     cd1 = lax.ppermute(cy1, AXES, moves(over_x))
-    r2, tails = middle(mine, (cx0, cx1, cy0, cy1), corpus, far)
+    done = middle(mine, (cx0, cx1, cy0, cy1), corpus, far, (r0, r1))
     shard = lax.axis_index("shard")
     at = (lax.shift_right_logical(shard, 2) * 2 + (lax.shift_right_logical(shard, 1) & 1)).reshape(1)
-    found = late(at, (cd0, cd1), corpus, far, (r0, r1, r2, tails))
+    found = late(at, (cd0, cd1), corpus, far, done)
     back = lax.all_to_all(
         found.reshape(LANGS * 4, ROWS, TOPK), AXES, 0, 0, axis_index_groups=TEAMS, tiled=True
     )

time: 74.4 us -> 73.6 us (0.989); the launches traced: 74.7 us -> 72.6 us
  blocking collectives: 24.7 us -> 22.9 us
    all_to_all x1, blocking collectives: 24.7 us -> 22.9 us  [shards(): lax.all_to_all(found.reshape(LANGS * 4, ROWS, TOPK), AXES, 0, 0, axis_ind...]
  transfers between devices with their start and end apart: 8 -> 8, of which waited for: 4 -> 3; matrix products, arithmetic and copies ran while one was open for 0% -> 0% of each run, Pallas kernels for 17% -> 18%
where the time goes in v12:
time: 73.6 us; the launch traced here: 72.6 us
  blocking collectives  22.9 us (31%)
  starting transfers between devices  20 us (27%)
  Pallas kernels  19.5 us (26%)
  waiting for transfers between devices  10.1 us (14%)
    all_to_all x1, blocking collectives, shards(): lax.all_to_all(found.reshape(LANGS * 4, ROWS, TOPK), AXES, 0, 0, axis_ind...  22.9 us
    all_to_all x1, waiting for transfers between devices, shards(): lax.all_to_all(outbox, 'lang', split_axis=0, concat_axis=0, tiled=True)  9.31 us
    all_to_all x1, starting transfers between devices, shards(): lax.all_to_all(outbox, 'lang', split_axis=0, concat_axis=0, tiled=True)  6.46 us
    ppermute x4, starting transfers between devices, shards(): lax.ppermute(part, AXES, moves(over))  6.02 us
    pallas_call x1, Pallas kernels, middle(): pl.pallas_call(middle_kernel, out_shape=jax.ShapeDtypeStruct((3, LANGS, R...  5.27 us
    pallas_call x1, Pallas kernels, late(): pl.pallas_call(late_kernel, out_shape=jax.ShapeDtypeStruct((LANGS, 4, ROW...  4.61 us
    ppermute x1, starting transfers between devices, shards(): far = lax.ppermute(corpus, AXES, moves(pair))  3.3 us
    pallas_call x1, Pallas kernels, first(): pl.pallas_call(first_kernel, out_shape=(jax.ShapeDtypeStruct((256, TOPK),...  3.21 us
  transfers between devices with their start and end apart: 8, of which 3 were waited for; matrix products, arithmetic and copies ran while one was open for 0% of the time, Pallas kernels for 18%

profile of v12, /device:TPU:1, one launch (start us, length us, event | category | flops | bytes accessed | tf_op | source)
XLA Modules:
  0.0 72.6 jit_solution(5729526772156909696)
XLA Ops:
  0.0 0.0 copy-start.1
  0.0 3.3 %collective-permute-start.2 = (bf16[1024,768]{1,0:T(8,128)(2,1)}, bf16[1024,768]{1,0:T(8,128)(2,1)}, u32[]{:S(2)}, u32[]{:S(2)}) collective-permute-start(bf16[1024,768]{1,0:T(8,128)(2,1)} %own.7), channel_id=1, source_target_pairs={{0,1},{1,0},{2,3},{3,2},{4,5},{5,4},{6,7},{7,6},{8,11},{9,10},{10,... | collective-permute-start | bytes 4718600 | tf_op jit(solution)/shard_map/ppermute | solution.py:610
  3.3 2.3 %outbox.1 = (bf16[16,120,128]{2,1,0:T(8,128)(2,1)}, s32[1,128]{1,0:T(1,128)}) custom-call(bf16[128,768]{1,0:T(8,128)(2,1)} %queries_in.1, s32[1,128]{1,0:T(1,128)} %bitcast.6), custom_call_target="tpu_custom_call" | custom-call | tf_op jit(solution)/shard_map/outbox/pallas_call | solution.py:527
  5.6 6.5 %all-to-all-start = ((bf16[16,120,128]{2,1,0:T(8,128)(2,1)}), bf16[16,120,128]{2,1,0:T(8,128)(2,1)S(1)}, u32[]{:S(2)}, u32[]{:S(2)}) async-start(bf16[16,120,128]{2,1,0:T(8,128)(2,1)} %get-tuple-element.15), calls=%async_computation | async-start | bytes 983040 | tf_op jit(solution)/shard_map/all_to_all | solution.py:612
  12.0 9.3 %all-to-all-done.chunk.mine = bf16[16,120,128]{2,1,0:T(8,128)(2,1)S(1)} async-done(((bf16[16,120,128]{2,1,0:T(8,128)(2,1)}), bf16[16,120,128]{2,1,0:T(8,128)(2,1)S(1)}, u32[]{:S(2)}, u32[]{:S(2)}) %all-to-all-start) | async-done | bytes 491552 | tf_op jit(solution)/shard_map/all_to_all | solution.py:612
  21.4 2.1 %collective-permute-start = (bf16[8,120,128]{2,1,0:T(8,128)(2,1)S(1)}, bf16[8,120,128]{2,1,0:T(8,128)(2,1)S(1)}, u32[]{:S(2)}, u32[]{:S(2)}) collective-permute-start(bf16[8,120,128]{2,1,0:T(8,128)(2,1)S(1)} %get-tuple-element.26), channel_id=1, source_target_pairs={{0,2},{1,3},{2,0},{3,1},{4,6},{5,7},{6,4},{7,5},{8,10},{9,11},{10,... | collective-permute-start | bytes 737288 | tf_op jit(solution)/shard_map/ppermute | solution.py:614
  23.5 2.6 %collective-permute-start.1 = (bf16[8,120,128]{2,1,0:T(8,128)(2,1)S(1)}, bf16[8,120,128]{2,1,0:T(8,128)(2,1)S(1)}, u32[]{:S(2)}, u32[]{:S(2)}) collective-permute-start(bf16[8,120,128]{2,1,0:T(8,128)(2,1)S(1)} %get-tuple-element.26), channel_id=1, source_target_pairs={{0,4},{1,5},{2,6},{3,7},{4,0},{5,1},{6,2},{7,3},{8,12},{9,13},{10,... | collective-permute-start | bytes 737288 | tf_op jit(solution)/shard_map/ppermute | solution.py:614
  26.1 0.9 %collective-permute-start.4 = (bf16[8,120,128]{2,1,0:T(8,128)(2,1)S(1)}, bf16[8,120,128]{2,1,0:T(8,128)(2,1)S(1)}, u32[]{:S(2)}, u32[]{:S(2)}) collective-permute-start(bf16[8,120,128]{2,1,0:T(8,128)(2,1)S(1)} %get-tuple-element.25), channel_id=1, source_target_pairs={{0,2},{1,3},{2,0},{3,1},{4,6},{5,7},{6,4},{7,5},{8,10},{9,11},{10,... | collective-permute-start | bytes 737288 | tf_op jit(solution)/shard_map/ppermute | solution.py:614
  27.1 0.3 collective-permute-start.5
  27.4 0.0 collective-permute-done.2.far_in
  27.4 0.0 copy-done.1
  27.4 3.2 %first.1 = (f32[256,128]{1,0:T(8,128)S(1)}, bf16[1024,768]{1,0:T(8,128)(2,1)S(1)}) custom-call(bf16[16,120,128]{2,1,0:T(8,128)(2,1)S(1)} %all-to-all-done.chunk.mine, bf16[1024,768]{1,0:T(8,128)(2,1)S(1)} %copy-done.1, bf16[1024,768]{1,0:T(8,128)(2,1)} %collective-permute-done.2.far_in), custom_call_target="tpu_custom_call" | custom-call | flops 6442450944 | bytes 1048576 | tf_op jit(solution)/shard_map/first/pallas_call | solution.py:423
  30.6 0.0 collective-permute-done.half0.cx0
  30.7 0.3 collective-permute-done.1.half1.cy0
  31.0 2.6 %collective-permute-start.3 = (bf16[8,120,128]{2,1,0:T(8,128)(2,1)S(1)}, bf16[8,120,128]{2,1,0:T(8,128)(2,1)S(1)}, u32[]{:S(2)}, u32[]{:S(2)}) collective-permute-start(bf16[8,120,128]{2,1,0:T(8,128)(2,1)S(1)} %collective-permute-done.half0.cx0), channel_id=1, source_target_pairs={{0,4},{1,5},{2,6},{3,7},{4,0},{5,1},{6,2},{7,3},{8,12},{9,13},{10,... | collective-permute-start | bytes 737288 | tf_op jit(solution)/shard_map/ppermute | solution.py:618
  33.6 2.5 %early.1.r1 = f32[256,128]{1,0:T(8,128)S(1)} custom-call(bf16[8,120,128]{2,1,0:T(8,128)(2,1)S(1)} %collective-permute-done.half0.cx0, bf16[8,120,128]{2,1,0:T(8,128)(2,1)S(1)} %collective-permute-done.1.half1.cy0, bf16[1024,768]{1,0:T(8,128)(2,1)S(1)} %copy-done.1, bf16[1024,768]{1,0:T(8,128)(2,1)S(1)} %get-tuple-element.19.far), custom_call_target="tpu_custom_call" | custom-call | flops 6442450944 | bytes 1048576 | tf_op jit(solution)/shard_map/early/pallas_call | solution.py:439
  36.1 0.0 collective-permute-done.4.cx1
  36.1 0.4 collective-permute-done.5.cy1
  36.5 1.6 %collective-permute-start.6 = (bf16[8,120,128]{2,1,0:T(8,128)(2,1)S(1)}, bf16[8,120,128]{2,1,0:T(8,128)(2,1)S(1)}, u32[]{:S(2)}, u32[]{:S(2)}) collective-permute-start(bf16[8,120,128]{2,1,0:T(8,128)(2,1)S(1)} %collective-permute-done.5.cy1), channel_id=1, source_target_pairs={{0,2},{1,3},{2,0},{3,1},{4,6},{5,7},{6,4},{7,5},{8,10},{9,11},{10,... | collective-permute-start | bytes 737288 | tf_op jit(solution)/shard_map/ppermute | solution.py:621
  38.2 5.3 %middle.1.done = s16[3,16,24,128]{3,2,1,0:T(8,128)(2,1)S(1)} custom-call(bf16[16,120,128]{2,1,0:T(8,128)(2,1)S(1)} %all-to-all-done.chunk.mine, bf16[8,120,128]{2,1,0:T(8,128)(2,1)S(1)} %collective-permute-done.half0.cx0, bf16[8,120,128]{2,1,0:T(8,128)(2,1)S(1)} %collective-permute-done.4.cx1, bf16[8,120,128]{2,1,0:T(8,128)(2,1)S(1)} %collective-permute-done.1.half1.cy0, ...), custom_call_target="tpu_custom_call" | custom-call | flops 12884901888 | bytes 1048576 | tf_op jit(solution)/shard_map/middle/pallas_call | solution.py:452
  43.4 0.0 collective-permute-done.6.cd1
  43.5 0.0 collective-permute-done.3.cd0
  43.5 0.0 copy-start
  43.5 4.6 %late.1 = s16[16,4,24,128]{3,2,1,0:T(8,128)(2,1)S(1)} custom-call(s32[1]{0:T(128)} %bitcast.at, bf16[8,120,128]{2,1,0:T(8,128)(2,1)S(1)} %collective-permute-done.3.cd0, bf16[8,120,128]{2,1,0:T(8,128)(2,1)S(1)} %collective-permute-done.6.cd1, bf16[1024,768]{1,0:T(8,128)(2,1)S(1)} %copy-done.1, bf16[1024,768]{1,0:T(8,128)(2,1)S(1)} %get-tuple-element.19.far, ...), custom_call_target="tpu_custom_call" | custom-call | flops 12884901888 | bytes 1048576 | tf_op jit(solution)/shard_map/late/pallas_call | solution.py:470
  48.1 22.9 %all_to_all.10 = s16[64,24,128]{2,1,0:T(8,128)(2,1)S(1)} all-to-all(s16[64,24,128]{2,1,0:T(8,128)(2,1)S(1)} %bitcast.5), channel_id=1, replica_groups={{0,2,4,6,8,10,12,14,16,18,20,22,24,26,28,30,32,34,36,38,40,42,44,46,48,..., dimensions={0} | all-to-all | bytes 786432 | tf_op jit(solution)/shard_map/all_to_all | solution.py:626
  71.0 0.0 copy-done
  71.0 1.6 %join.1 = f32[128,128]{1,0:T(8,128)} custom-call(s16[16,4,24,128]{3,2,1,0:T(8,128)(2,1)S(1)} %bitcast.4, s32[1,128]{1,0:T(1,128)S(1)} %copy-done), custom_call_target="tpu_custom_call" | custom-call | tf_op jit(solution)/shard_map/join/pallas_call | solution.py:567
  (1 shorter events, 0.0 us)
Async XLA Ops:
  0.0 27.4 %copy-start.1 = (bf16[1024,768]{1,0:T(8,128)(2,1)S(1)}, bf16[1024,768]{1,0:T(8,128)(2,1)}, u32[]{:S(2)}) copy-start(bf16[1024,768]{1,0:T(8,128)(2,1)} %own.7) | copy-start | bytes 4718596
  0.0 27.4 %collective-permute-start.2 = (bf16[1024,768]{1,0:T(8,128)(2,1)}, bf16[1024,768]{1,0:T(8,128)(2,1)}, u32[]{:S(2)}, u32[]{:S(2)}) collective-permute-start(bf16[1024,768]{1,0:T(8,128)(2,1)} %own.7), channel_id=1, source_target_pairs={{0,1},{1,0},{2,3},{3,2},{4,5},{5,4},{6,7},{7,6},{8,11},{9,10},{10,... | collective-permute-start | bytes 4718600 | tf_op jit(solution)/shard_map/ppermute | solution.py:610
  5.6 15.8 %all-to-all-start = ((bf16[16,120,128]{2,1,0:T(8,128)(2,1)}), bf16[16,120,128]{2,1,0:T(8,128)(2,1)S(1)}, u32[]{:S(2)}, u32[]{:S(2)}) async-start(bf16[16,120,128]{2,1,0:T(8,128)(2,1)} %get-tuple-element.15), calls=%async_computation | async-start | bytes 983040 | tf_op jit(solution)/shard_map/all_to_all | solution.py:612
  21.4 9.3 %collective-permute-start = (bf16[8,120,128]{2,1,0:T(8,128)(2,1)S(1)}, bf16[8,120,128]{2,1,0:T(8,128)(2,1)S(1)}, u32[]{:S(2)}, u32[]{:S(2)}) collective-permute-start(bf16[8,120,128]{2,1,0:T(8,128)(2,1)S(1)} %get-tuple-element.26), channel_id=1, source_target_pairs={{0,2},{1,3},{2,0},{3,1},{4,6},{5,7},{6,4},{7,5},{8,10},{9,11},{10,... | collective-permute-start | bytes 737288 | tf_op jit(solution)/shard_map/ppermute | solution.py:614
  23.5 7.5 %collective-permute-start.1 = (bf16[8,120,128]{2,1,0:T(8,128)(2,1)S(1)}, bf16[8,120,128]{2,1,0:T(8,128)(2,1)S(1)}, u32[]{:S(2)}, u32[]{:S(2)}) collective-permute-start(bf16[8,120,128]{2,1,0:T(8,128)(2,1)S(1)} %get-tuple-element.26), channel_id=1, source_target_pairs={{0,4},{1,5},{2,6},{3,7},{4,0},{5,1},{6,2},{7,3},{8,12},{9,13},{10,... | collective-permute-start | bytes 737288 | tf_op jit(solution)/shard_map/ppermute | solution.py:614
  26.1 10.0 %collective-permute-start.4 = (bf16[8,120,128]{2,1,0:T(8,128)(2,1)S(1)}, bf16[8,120,128]{2,1,0:T(8,128)(2,1)S(1)}, u32[]{:S(2)}, u32[]{:S(2)}) collective-permute-start(bf16[8,120,128]{2,1,0:T(8,128)(2,1)S(1)} %get-tuple-element.25), channel_id=1, source_target_pairs={{0,2},{1,3},{2,0},{3,1},{4,6},{5,7},{6,4},{7,5},{8,10},{9,11},{10,... | collective-permute-start | bytes 737288 | tf_op jit(solution)/shard_map/ppermute | solution.py:614
  27.1 9.5 %collective-permute-start.5 = (bf16[8,120,128]{2,1,0:T(8,128)(2,1)S(1)}, bf16[8,120,128]{2,1,0:T(8,128)(2,1)S(1)}, u32[]{:S(2)}, u32[]{:S(2)}) collective-permute-start(bf16[8,120,128]{2,1,0:T(8,128)(2,1)S(1)} %get-tuple-element.25), channel_id=1, source_target_pairs={{0,4},{1,5},{2,6},{3,7},{4,0},{5,1},{6,2},{7,3},{8,12},{9,13},{10,... | collective-permute-start | bytes 737288 | tf_op jit(solution)/shard_map/ppermute | solution.py:614
  31.0 12.5 %collective-permute-start.3 = (bf16[8,120,128]{2,1,0:T(8,128)(2,1)S(1)}, bf16[8,120,128]{2,1,0:T(8,128)(2,1)S(1)}, u32[]{:S(2)}, u32[]{:S(2)}) collective-permute-start(bf16[8,120,128]{2,1,0:T(8,128)(2,1)S(1)} %collective-permute-done.half0.cx0), channel_id=1, source_target_pairs={{0,4},{1,5},{2,6},{3,7},{4,0},{5,1},{6,2},{7,3},{8,12},{9,13},{10,... | collective-permute-start | bytes 737288 | tf_op jit(solution)/shard_map/ppermute | solution.py:618
  36.5 6.9 %collective-permute-start.6 = (bf16[8,120,128]{2,1,0:T(8,128)(2,1)S(1)}, bf16[8,120,128]{2,1,0:T(8,128)(2,1)S(1)}, u32[]{:S(2)}, u32[]{:S(2)}) collective-permute-start(bf16[8,120,128]{2,1,0:T(8,128)(2,1)S(1)} %collective-permute-done.5.cy1), channel_id=1, source_target_pairs={{0,2},{1,3},{2,0},{3,1},{4,6},{5,7},{6,4},{7,5},{8,10},{9,11},{10,... | collective-permute-start | bytes 737288 | tf_op jit(solution)/shard_map/ppermute | solution.py:621
  43.5 27.5 %copy-start = (s32[1,128]{1,0:T(1,128)S(1)}, s32[1,128]{1,0:T(1,128)}, u32[]{:S(2)}) copy-start(s32[1,128]{1,0:T(1,128)} %get-tuple-element.24.slots) | copy-start | bytes 1540

commit v13 on v12

--- a/solution.py
+++ b/solution.py
@@ -394,9 +394,9 @@
     rows[288:320, :] = tail_rows(cd1)
     rows[320:384, :] = jnp.zeros((64, WIDTH), jnp.bfloat16)
     me = at[0]
-    for k, owner in enumerate((me, me ^ 1, me ^ 2)):
+    for k, owner in enumerate((me, me ^ 2, me ^ 1)):
         for lang in range(LANGS):
-            out[lang, owner] = done[k, lang]
+            out[lang % 2, owner, lang // 2] = done[k, lang]
 
     def emit(g, half, value):
         last[g * 256 + half * Q : g * 256 + (half + 1) * Q, :] = value
@@ -406,7 +406,7 @@
     )
     for lang in range(LANGS):
         tail = last[256 + lang * TAIL : 256 + (lang + 1) * TAIL, :]
-        out[lang, me ^ 3] = boxed(box.at[lang % 4], last[lang * MAIN : (lang + 1) * MAIN, :], tail)
+        out[lang % 2, me ^ 3, lang // 2] = boxed(box.at[lang % 4], last[lang * MAIN : (lang + 1) * MAIN, :], tail)
 
 
 COST = 2 * 256 * 2048 * 768 * 8
@@ -469,7 +469,7 @@
 def late(at, halves, own, far, done):
     return pl.pallas_call(
         late_kernel,
-        out_shape=jax.ShapeDtypeStruct((LANGS, 4, ROWS, TOPK), jnp.int16),
+        out_shape=jax.ShapeDtypeStruct((2, 4, LANGS // 2, ROWS, TOPK), jnp.int16),
         in_specs=[pl.BlockSpec(memory_space=pltpu.SMEM)] + [VMEM] * 5,
         out_specs=VMEM,
         scratch_shapes=[
@@ -498,7 +498,7 @@
     earlier = jnp.where(before & (along == down), 1.0, 0.0)
     rank = jnp.sum(earlier, axis=0, keepdims=True).astype(jnp.int32)
     lang = routes[...]
-    slots[...] = lang * ROWS + rank
+    slots[...] = ((lang & 1) * (LANGS // 2) + lax.shift_right_logical(lang, 1)) * ROWS + rank
     main_at = jnp.where(rank < MAIN, lang * MAIN + rank, -1)
     hits = lax.broadcasted_iota(jnp.int32, (LANGS * MAIN, Q), 0) == jnp.broadcast_to(main_at, (LANGS * MAIN, Q))
     picks = jnp.where(hits, 1.0, 0.0).astype(jnp.bfloat16)
@@ -601,7 +601,13 @@
 
 
 TEAMS = [
-    [lang * 8 + y * 4 + odd + 2 * half for lang in range(16) for y in range(2) for half in range(2)]
+    [
+        (pair * 2 + core) * 8 + y * 4 + odd + 2 * half
+        for core in range(2)
+        for half in range(2)
+        for y in range(2)
+        for pair in range(8)
+    ]
     for odd in range(2)
 ]
 
@@ -621,12 +627,12 @@
     cd1 = lax.ppermute(cy1, AXES, moves(over_x))
     done = middle(mine, (cx0, cx1, cy0, cy1), corpus, far, (r0, r1))
     shard = lax.axis_index("shard")
-    at = (lax.shift_right_logical(shard, 2) * 2 + (lax.shift_right_logical(shard, 1) & 1)).reshape(1)
+    at = (lax.shift_right_logical(shard, 2) + (shard & 2)).reshape(1)
     found = late(at, (cd0, cd1), corpus, far, done)
     back = lax.all_to_all(
         found.reshape(LANGS * 4, ROWS, TOPK), AXES, 0, 0, axis_index_groups=TEAMS, tiled=True
     )
-    return join(back.reshape(LANGS, 4, ROWS, TOPK), slots)
+    return join(back.reshape(2, 4, LANGS // 2, ROWS, TOPK), slots)
 
 
 def solution(mesh):

time: 73.6 us -> 74.2 us (level)
  no operation moved by 1% of the time
where the time goes in v13:
time: 74.2 us; the launch traced here: 73.2 us
  blocking collectives  23.5 us (32%)
  starting transfers between devices  20 us (27%)
  Pallas kernels  19.5 us (26%)
  waiting for transfers between devices  10.1 us (14%)
    all_to_all x1, blocking collectives, shards(): lax.all_to_all(found.reshape(LANGS * 4, ROWS, TOPK), AXES, 0, 0, axis_ind...  23.5 us
    all_to_all x1, waiting for transfers between devices, shards(): lax.all_to_all(outbox, 'lang', split_axis=0, concat_axis=0, tiled=True)  9.31 us
    all_to_all x1, starting transfers between devices, shards(): lax.all_to_all(outbox, 'lang', split_axis=0, concat_axis=0, tiled=True)  6.46 us
    ppermute x4, starting transfers between devices, shards(): lax.ppermute(part, AXES, moves(over))  6.02 us
    pallas_call x1, Pallas kernels, middle(): pl.pallas_call(middle_kernel, out_shape=jax.ShapeDtypeStruct((3, LANGS, R...  5.27 us
    pallas_call x1, Pallas kernels, late(): pl.pallas_call(late_kernel, out_shape=jax.ShapeDtypeStruct((2, 4, LANGS /...  4.61 us
    ppermute x1, starting transfers between devices, shards(): far = lax.ppermute(corpus, AXES, moves(pair))  3.3 us
    pallas_call x1, Pallas kernels, first(): pl.pallas_call(first_kernel, out_shape=(jax.ShapeDtypeStruct((256, TOPK),...  3.22 us
  transfers between devices with their start and end apart: 8, of which 3 were waited for; matrix products, arithmetic and copies ran while one was open for 0% of the time, Pallas kernels for 18%

profile of v13, /device:TPU:1, one launch (start us, length us, event | category | flops | bytes accessed | tf_op | source)
XLA Modules:
  0.0 73.2 jit_solution(14304341594398819424)
XLA Ops:
  0.0 0.0 copy-start.1
  0.0 3.3 %collective-permute-start.2 = (bf16[1024,768]{1,0:T(8,128)(2,1)}, bf16[1024,768]{1,0:T(8,128)(2,1)}, u32[]{:S(2)}, u32[]{:S(2)}) collective-permute-start(bf16[1024,768]{1,0:T(8,128)(2,1)} %own.7), channel_id=1, source_target_pairs={{0,1},{1,0},{2,3},{3,2},{4,5},{5,4},{6,7},{7,6},{8,11},{9,10},{10,... | collective-permute-start | bytes 4718600 | tf_op jit(solution)/shard_map/ppermute | solution.py:616
  3.3 2.3 %outbox.1 = (bf16[16,120,128]{2,1,0:T(8,128)(2,1)}, s32[1,128]{1,0:T(1,128)}) custom-call(bf16[128,768]{1,0:T(8,128)(2,1)} %queries_in.1, s32[1,128]{1,0:T(1,128)} %bitcast.6), custom_call_target="tpu_custom_call" | custom-call | tf_op jit(solution)/shard_map/outbox/pallas_call | solution.py:527
  5.6 6.5 %all-to-all-start = ((bf16[16,120,128]{2,1,0:T(8,128)(2,1)}), bf16[16,120,128]{2,1,0:T(8,128)(2,1)S(1)}, u32[]{:S(2)}, u32[]{:S(2)}) async-start(bf16[16,120,128]{2,1,0:T(8,128)(2,1)} %get-tuple-element.15), calls=%async_computation | async-start | bytes 983040 | tf_op jit(solution)/shard_map/all_to_all | solution.py:618
  12.0 9.3 %all-to-all-done.chunk.mine = bf16[16,120,128]{2,1,0:T(8,128)(2,1)S(1)} async-done(((bf16[16,120,128]{2,1,0:T(8,128)(2,1)}), bf16[16,120,128]{2,1,0:T(8,128)(2,1)S(1)}, u32[]{:S(2)}, u32[]{:S(2)}) %all-to-all-start) | async-done | bytes 491552 | tf_op jit(solution)/shard_map/all_to_all | solution.py:618
  21.4 2.1 %collective-permute-start = (bf16[8,120,128]{2,1,0:T(8,128)(2,1)S(1)}, bf16[8,120,128]{2,1,0:T(8,128)(2,1)S(1)}, u32[]{:S(2)}, u32[]{:S(2)}) collective-permute-start(bf16[8,120,128]{2,1,0:T(8,128)(2,1)S(1)} %get-tuple-element.26), channel_id=1, source_target_pairs={{0,2},{1,3},{2,0},{3,1},{4,6},{5,7},{6,4},{7,5},{8,10},{9,11},{10,... | collective-permute-start | bytes 737288 | tf_op jit(solution)/shard_map/ppermute | solution.py:620
  23.5 2.6 %collective-permute-start.1 = (bf16[8,120,128]{2,1,0:T(8,128)(2,1)S(1)}, bf16[8,120,128]{2,1,0:T(8,128)(2,1)S(1)}, u32[]{:S(2)}, u32[]{:S(2)}) collective-permute-start(bf16[8,120,128]{2,1,0:T(8,128)(2,1)S(1)} %get-tuple-element.26), channel_id=1, source_target_pairs={{0,4},{1,5},{2,6},{3,7},{4,0},{5,1},{6,2},{7,3},{8,12},{9,13},{10,... | collective-permute-start | bytes 737288 | tf_op jit(solution)/shard_map/ppermute | solution.py:620
  26.1 0.9 %collective-permute-start.4 = (bf16[8,120,128]{2,1,0:T(8,128)(2,1)S(1)}, bf16[8,120,128]{2,1,0:T(8,128)(2,1)S(1)}, u32[]{:S(2)}, u32[]{:S(2)}) collective-permute-start(bf16[8,120,128]{2,1,0:T(8,128)(2,1)S(1)} %get-tuple-element.25), channel_id=1, source_target_pairs={{0,2},{1,3},{2,0},{3,1},{4,6},{5,7},{6,4},{7,5},{8,10},{9,11},{10,... | collective-permute-start | bytes 737288 | tf_op jit(solution)/shard_map/ppermute | solution.py:620
  27.1 0.3 collective-permute-start.5
  27.4 0.0 collective-permute-done.2.far_in
  27.4 0.0 copy-done.1
  27.4 3.2 %first.1 = (f32[256,128]{1,0:T(8,128)S(1)}, bf16[1024,768]{1,0:T(8,128)(2,1)S(1)}) custom-call(bf16[16,120,128]{2,1,0:T(8,128)(2,1)S(1)} %all-to-all-done.chunk.mine, bf16[1024,768]{1,0:T(8,128)(2,1)S(1)} %copy-done.1, bf16[1024,768]{1,0:T(8,128)(2,1)} %collective-permute-done.2.far_in), custom_call_target="tpu_custom_call" | custom-call | flops 6442450944 | bytes 1048576 | tf_op jit(solution)/shard_map/first/pallas_call | solution.py:423
  30.6 0.0 collective-permute-done.half0.cx0
  30.7 0.3 collective-permute-done.1.half1.cy0
  31.0 2.6 %collective-permute-start.3 = (bf16[8,120,128]{2,1,0:T(8,128)(2,1)S(1)}, bf16[8,120,128]{2,1,0:T(8,128)(2,1)S(1)}, u32[]{:S(2)}, u32[]{:S(2)}) collective-permute-start(bf16[8,120,128]{2,1,0:T(8,128)(2,1)S(1)} %collective-permute-done.half0.cx0), channel_id=1, source_target_pairs={{0,4},{1,5},{2,6},{3,7},{4,0},{5,1},{6,2},{7,3},{8,12},{9,13},{10,... | collective-permute-start | bytes 737288 | tf_op jit(solution)/shard_map/ppermute | solution.py:624
  33.6 2.5 %early.1.r1 = f32[256,128]{1,0:T(8,128)S(1)} custom-call(bf16[8,120,128]{2,1,0:T(8,128)(2,1)S(1)} %collective-permute-done.half0.cx0, bf16[8,120,128]{2,1,0:T(8,128)(2,1)S(1)} %collective-permute-done.1.half1.cy0, bf16[1024,768]{1,0:T(8,128)(2,1)S(1)} %copy-done.1, bf16[1024,768]{1,0:T(8,128)(2,1)S(1)} %get-tuple-element.19.far), custom_call_target="tpu_custom_call" | custom-call | flops 6442450944 | bytes 1048576 | tf_op jit(solution)/shard_map/early/pallas_call | solution.py:439
  36.1 0.0 collective-permute-done.4.cx1
  36.1 0.4 collective-permute-done.5.cy1
  36.5 1.6 %collective-permute-start.6 = (bf16[8,120,128]{2,1,0:T(8,128)(2,1)S(1)}, bf16[8,120,128]{2,1,0:T(8,128)(2,1)S(1)}, u32[]{:S(2)}, u32[]{:S(2)}) collective-permute-start(bf16[8,120,128]{2,1,0:T(8,128)(2,1)S(1)} %collective-permute-done.5.cy1), channel_id=1, source_target_pairs={{0,2},{1,3},{2,0},{3,1},{4,6},{5,7},{6,4},{7,5},{8,10},{9,11},{10,... | collective-permute-start | bytes 737288 | tf_op jit(solution)/shard_map/ppermute | solution.py:627
  38.2 5.3 %middle.1.done = s16[3,16,24,128]{3,2,1,0:T(8,128)(2,1)S(1)} custom-call(bf16[16,120,128]{2,1,0:T(8,128)(2,1)S(1)} %all-to-all-done.chunk.mine, bf16[8,120,128]{2,1,0:T(8,128)(2,1)S(1)} %collective-permute-done.half0.cx0, bf16[8,120,128]{2,1,0:T(8,128)(2,1)S(1)} %collective-permute-done.4.cx1, bf16[8,120,128]{2,1,0:T(8,128)(2,1)S(1)} %collective-permute-done.1.half1.cy0, ...), custom_call_target="tpu_custom_call" | custom-call | flops 12884901888 | bytes 1048576 | tf_op jit(solution)/shard_map/middle/pallas_call | solution.py:452
  43.4 0.0 collective-permute-done.6.cd1
  43.5 0.0 collective-permute-done.3.cd0
  43.5 0.0 copy-start
  43.5 4.6 %late.1 = s16[2,4,8,24,128]{4,3,2,1,0:T(8,128)(2,1)S(1)} custom-call(s32[1]{0:T(128)} %bitcast.at, bf16[8,120,128]{2,1,0:T(8,128)(2,1)S(1)} %collective-permute-done.3.cd0, bf16[8,120,128]{2,1,0:T(8,128)(2,1)S(1)} %collective-permute-done.6.cd1, bf16[1024,768]{1,0:T(8,128)(2,1)S(1)} %copy-done.1, bf16[1024,768]{1,0:T(8,128)(2,1)S(1)} %get-tuple-element.19.far, ...), custom_call_target="tpu_custom_call" | custom-call | flops 12884901888 | bytes 1048576 | tf_op jit(solution)/shard_map/late/pallas_call | solution.py:470
  48.1 23.5 %all_to_all.10 = s16[64,24,128]{2,1,0:T(8,128)(2,1)S(1)} all-to-all(s16[64,24,128]{2,1,0:T(8,128)(2,1)S(1)} %bitcast.5), channel_id=1, replica_groups={{0,16,32,48,64,80,96,112,4,20,36,52,68,84,100,116,2,18,34,50,66,82,98,1..., dimensions={0} | all-to-all | bytes 786432 | tf_op jit(solution)/shard_map/all_to_all | solution.py:632
  71.5 0.0 copy-done
  71.5 1.6 %join.1 = f32[128,128]{1,0:T(8,128)} custom-call(s16[2,4,8,24,128]{4,3,2,1,0:T(8,128)(2,1)S(1)} %bitcast.4, s32[1,128]{1,0:T(1,128)S(1)} %copy-done), custom_call_target="tpu_custom_call" | custom-call | tf_op jit(solution)/shard_map/join/pallas_call | solution.py:567
  (1 shorter events, 0.0 us)
Async XLA Ops:
  0.0 27.4 %copy-start.1 = (bf16[1024,768]{1,0:T(8,128)(2,1)S(1)}, bf16[1024,768]{1,0:T(8,128)(2,1)}, u32[]{:S(2)}) copy-start(bf16[1024,768]{1,0:T(8,128)(2,1)} %own.7) | copy-start | bytes 4718596
  0.0 27.4 %collective-permute-start.2 = (bf16[1024,768]{1,0:T(8,128)(2,1)}, bf16[1024,768]{1,0:T(8,128)(2,1)}, u32[]{:S(2)}, u32[]{:S(2)}) collective-permute-start(bf16[1024,768]{1,0:T(8,128)(2,1)} %own.7), channel_id=1, source_target_pairs={{0,1},{1,0},{2,3},{3,2},{4,5},{5,4},{6,7},{7,6},{8,11},{9,10},{10,... | collective-permute-start | bytes 4718600 | tf_op jit(solution)/shard_map/ppermute | solution.py:616
  5.6 15.8 %all-to-all-start = ((bf16[16,120,128]{2,1,0:T(8,128)(2,1)}), bf16[16,120,128]{2,1,0:T(8,128)(2,1)S(1)}, u32[]{:S(2)}, u32[]{:S(2)}) async-start(bf16[16,120,128]{2,1,0:T(8,128)(2,1)} %get-tuple-element.15), calls=%async_computation | async-start | bytes 983040 | tf_op jit(solution)/shard_map/all_to_all | solution.py:618
  21.4 9.3 %collective-permute-start = (bf16[8,120,128]{2,1,0:T(8,128)(2,1)S(1)}, bf16[8,120,128]{2,1,0:T(8,128)(2,1)S(1)}, u32[]{:S(2)}, u32[]{:S(2)}) collective-permute-start(bf16[8,120,128]{2,1,0:T(8,128)(2,1)S(1)} %get-tuple-element.26), channel_id=1, source_target_pairs={{0,2},{1,3},{2,0},{3,1},{4,6},{5,7},{6,4},{7,5},{8,10},{9,11},{10,... | collective-permute-start | bytes 737288 | tf_op jit(solution)/shard_map/ppermute | solution.py:620
  23.5 7.5 %collective-permute-start.1 = (bf16[8,120,128]{2,1,0:T(8,128)(2,1)S(1)}, bf16[8,120,128]{2,1,0:T(8,128)(2,1)S(1)}, u32[]{:S(2)}, u32[]{:S(2)}) collective-permute-start(bf16[8,120,128]{2,1,0:T(8,128)(2,1)S(1)} %get-tuple-element.26), channel_id=1, source_target_pairs={{0,4},{1,5},{2,6},{3,7},{4,0},{5,1},{6,2},{7,3},{8,12},{9,13},{10,... | collective-permute-start | bytes 737288 | tf_op jit(solution)/shard_map/ppermute | solution.py:620
  26.1 10.0 %collective-permute-start.4 = (bf16[8,120,128]{2,1,0:T(8,128)(2,1)S(1)}, bf16[8,120,128]{2,1,0:T(8,128)(2,1)S(1)}, u32[]{:S(2)}, u32[]{:S(2)}) collective-permute-start(bf16[8,120,128]{2,1,0:T(8,128)(2,1)S(1)} %get-tuple-element.25), channel_id=1, source_target_pairs={{0,2},{1,3},{2,0},{3,1},{4,6},{5,7},{6,4},{7,5},{8,10},{9,11},{10,... | collective-permute-start | bytes 737288 | tf_op jit(solution)/shard_map/ppermute | solution.py:620
  27.1 9.5 %collective-permute-start.5 = (bf16[8,120,128]{2,1,0:T(8,128)(2,1)S(1)}, bf16[8,120,128]{2,1,0:T(8,128)(2,1)S(1)}, u32[]{:S(2)}, u32[]{:S(2)}) collective-permute-start(bf16[8,120,128]{2,1,0:T(8,128)(2,1)S(1)} %get-tuple-element.25), channel_id=1, source_target_pairs={{0,4},{1,5},{2,6},{3,7},{4,0},{5,1},{6,2},{7,3},{8,12},{9,13},{10,... | collective-permute-start | bytes 737288 | tf_op jit(solution)/shard_map/ppermute | solution.py:620
  31.0 12.5 %collective-permute-start.3 = (bf16[8,120,128]{2,1,0:T(8,128)(2,1)S(1)}, bf16[8,120,128]{2,1,0:T(8,128)(2,1)S(1)}, u32[]{:S(2)}, u32[]{:S(2)}) collective-permute-start(bf16[8,120,128]{2,1,0:T(8,128)(2,1)S(1)} %collective-permute-done.half0.cx0), channel_id=1, source_target_pairs={{0,4},{1,5},{2,6},{3,7},{4,0},{5,1},{6,2},{7,3},{8,12},{9,13},{10,... | collective-permute-start | bytes 737288 | tf_op jit(solution)/shard_map/ppermute | solution.py:624
  36.5 6.9 %collective-permute-start.6 = (bf16[8,120,128]{2,1,0:T(8,128)(2,1)S(1)}, bf16[8,120,128]{2,1,0:T(8,128)(2,1)S(1)}, u32[]{:S(2)}, u32[]{:S(2)}) collective-permute-start(bf16[8,120,128]{2,1,0:T(8,128)(2,1)S(1)} %collective-permute-done.5.cy1), channel_id=1, source_target_pairs={{0,2},{1,3},{2,0},{3,1},{4,6},{5,7},{6,4},{7,5},{8,10},{9,11},{10,... | collective-permute-start | bytes 737288 | tf_op jit(solution)/shard_map/ppermute | solution.py:627
  43.5 28.1 %copy-start = (s32[1,128]{1,0:T(1,128)S(1)}, s32[1,128]{1,0:T(1,128)}, u32[]{:S(2)}) copy-start(s32[1,128]{1,0:T(1,128)} %get-tuple-element.24.slots) | copy-start | bytes 1540
